TPU v7x, 128 devices: a whole 4x4x4 slice. The times are simulated.
128 devices in a mesh: cp: 2 (over core), fsdp: 64 (over z, y, x).
Axes of the slice: x: 4, y: 4, z: 4, core: 2. Of those that a mesh axis runs over, the one named last changes fastest.
Arguments:
- tokens: int32 [1024, 256], P('fsdp', 'cp')
- lengths: int32 [1024], P('fsdp')
- embed_table: bfloat16 [33, 640], replicated
- layer_vecs: float32 [9, 640], P(None, 'fsdp')
- w_qkv: bfloat16 [640, 3, 20, 32], P('fsdp')
- w_out: bfloat16 [640, 640], P('fsdp')
- w_up: bfloat16 [640, 2560], P('fsdp')
- b_up: float32 [2560], P('fsdp')
- w_down: bfloat16 [2560, 640], P('fsdp')
- grad_out: bfloat16 [1024, 256, 640], P('fsdp', 'cp')
Outputs:
- output 1: bfloat16 [1024, 256, 640], P('fsdp', 'cp')
- output 2: float32 [33, 640], replicated
- output 3: float32 [9, 640], P(None, 'fsdp')
- output 4: float32 [640, 3, 20, 32], P('fsdp')
- output 5: float32 [640, 640], P('fsdp')
- output 6: float32 [640, 2560], P('fsdp')
- output 7: float32 [2560], P('fsdp')
- output 8: float32 [2560, 640], P('fsdp')
All inputs are finite; a program needn't handle non-finite values.
Results may differ from a plain program's by a relative error of at most 0.00989253.
Values are sent between devices in bfloat16 or wider.
A program may use at most 1 GiB of HBM per device.

v0:
```python
import jax
import jax.numpy as jnp
from jax import lax
from jax.sharding import PartitionSpec as P

MASK_ID = 32
LN_EPS = 1e-5
ROPE_BASE = 10000.0
TRAIN_RATIO = 0.15 * 0.8
NEG_BIG = -1e30


def layer_norm(z_in, ln_gain, ln_bias):
    row_mean = jnp.mean(z_in, axis=-1, keepdims=True)
    centered = z_in - row_mean
    row_var = jnp.mean(centered * centered, axis=-1, keepdims=True)
    return centered * lax.rsqrt(row_var + LN_EPS) * ln_gain + ln_bias


def gelu_exact(z_in):
    return jax.nn.gelu(z_in, approximate=False)


def rope_tables(positions, head_dim):
    inv_freq = 1.0 / (ROPE_BASE ** (jnp.arange(0, head_dim, 2, dtype=jnp.float32) / head_dim))
    angles = positions.astype(jnp.float32)[:, None] * inv_freq[None, :]
    return jnp.cos(angles)[:, None, :], jnp.sin(angles)[:, None, :]


def rotate(z_in, cos_t, sin_t):
    lower_half, upper_half = jnp.split(z_in, 2, axis=-1)
    return jnp.concatenate([lower_half * cos_t - upper_half * sin_t, upper_half * cos_t + lower_half * sin_t], axis=-1)


def reduce_grad(full_grad, axis_dim):
    return lax.psum(lax.psum_scatter(full_grad, 'fsdp', scatter_dimension=axis_dim, tiled=True), 'cp')


def solution(mesh):
    cp_size = mesh.shape['cp']
    send_pairs = [(dev_index, (dev_index + 1) % cp_size) for dev_index in range(cp_size)]

    def local_step(tokens, lengths, embed_table, layer_vecs, w_qkv, w_out, w_up, b_up, w_down, grad_out):
        vecs_all = lax.all_gather(layer_vecs, 'fsdp', axis=1, tiled=True)
        qkv_w = lax.all_gather(w_qkv, 'fsdp', axis=0, tiled=True)
        out_w = lax.all_gather(w_out, 'fsdp', axis=0, tiled=True)
        up_w = lax.all_gather(w_up, 'fsdp', axis=0, tiled=True)
        up_b = lax.all_gather(b_up, 'fsdp', axis=0, tiled=True)
        down_w = lax.all_gather(w_down, 'fsdp', axis=0, tiled=True)
        n_seq, seq_loc = tokens.shape
        vocab_size, model_dim = embed_table.shape
        n_heads, head_dim = qkv_w.shape[2], qkv_w.shape[3]
        cp_index = lax.axis_index('cp')
        positions = cp_index * seq_loc + jnp.arange(seq_loc)
        len_col = lengths[:, None]
        is_mask = tokens == MASK_ID
        tok_valid = positions[None, :] < len_col
        mask_count = lax.psum(jnp.sum(is_mask.astype(jnp.int32), axis=1), 'cp')
        drop_scale = (1.0 - TRAIN_RATIO) / (1.0 - mask_count.astype(jnp.float32) / lengths.astype(jnp.float32))
        keep_scale = jnp.where(is_mask | jnp.logical_not(tok_valid), 0.0, drop_scale[:, None])[:, :, None]
        one_hot = (tokens[:, :, None] == jnp.arange(vocab_size)).astype(jnp.bfloat16)
        embedded = jnp.einsum('bsv,vd->bsd', one_hot, embed_table, preferred_element_type=jnp.float32) * keep_scale
        norm_in32, ln1_pull = jax.vjp(layer_norm, embedded, vecs_all[0], vecs_all[1])
        norm_in = norm_in32.astype(jnp.bfloat16)
        qkv_lin = jnp.einsum('bsd,dthe->bsthe', norm_in, qkv_w, preferred_element_type=jnp.float32) + vecs_all[2:5].reshape(3, n_heads, head_dim)
        cos_t, sin_t = rope_tables(positions, head_dim)
        q_rot = rotate(qkv_lin[:, :, 0] * head_dim ** -0.5, cos_t, sin_t).astype(jnp.bfloat16)
        k_rot = rotate(qkv_lin[:, :, 1], cos_t, sin_t).astype(jnp.bfloat16)
        v_val = qkv_lin[:, :, 2].astype(jnp.bfloat16)

        def block_scores(k_blk, step):
            src_index = (cp_index - step) % cp_size
            key_pos = src_index * seq_loc + jnp.arange(seq_loc)
            key_ok = key_pos[None, :] < len_col
            raw_scores = jnp.einsum('bqhd,bkhd->bhqk', q_rot, k_blk, preferred_element_type=jnp.float32)
            return jnp.where(key_ok[:, None, None, :], raw_scores, NEG_BIG)

        def fwd_block(step, k_blk, v_blk, run_max, run_sum, acc_out):
            scores = block_scores(k_blk, step)
            new_max = jnp.maximum(run_max, jnp.max(scores, axis=-1))
            weights = jnp.exp(scores - new_max[..., None])
            rescale = jnp.exp(run_max - new_max)
            run_sum = run_sum * rescale + jnp.sum(weights, axis=-1)
            acc_out = acc_out * jnp.swapaxes(rescale, 1, 2)[..., None] + jnp.einsum('bhqk,bkhd->bqhd', weights.astype(jnp.bfloat16), v_blk, preferred_element_type=jnp.float32)
            return new_max, run_sum, acc_out

        def fwd_body(step, carry):
            k_blk, v_blk, run_max, run_sum, acc_out = carry
            run_max, run_sum, acc_out = fwd_block(step, k_blk, v_blk, run_max, run_sum, acc_out)
            return (lax.ppermute(k_blk, 'cp', send_pairs), lax.ppermute(v_blk, 'cp', send_pairs), run_max, run_sum, acc_out)

        stat_shape = (n_seq, n_heads, seq_loc)
        carry = (k_rot, v_val, jnp.full(stat_shape, NEG_BIG, jnp.float32), jnp.zeros(stat_shape, jnp.float32), jnp.zeros(q_rot.shape, jnp.float32))
        carry = lax.fori_loop(0, cp_size - 1, fwd_body, carry)
        run_max, run_sum, acc_out = fwd_block(cp_size - 1, carry[0], carry[1], carry[2], carry[3], carry[4])
        log_sum = run_max + jnp.log(run_sum)
        attn32 = acc_out / jnp.swapaxes(run_sum, 1, 2)[..., None]
        attn_out = attn32.astype(jnp.bfloat16).reshape(n_seq, seq_loc, model_dim)
        resid_mid = embedded + jnp.einsum('bsd,de->bse', attn_out, out_w, preferred_element_type=jnp.float32) + vecs_all[5]
        norm_mid32, ln2_pull = jax.vjp(layer_norm, resid_mid, vecs_all[6], vecs_all[7])
        norm_mid = norm_mid32.astype(jnp.bfloat16)
        up_lin = jnp.einsum('bsd,df->bsf', norm_mid, up_w, preferred_element_type=jnp.float32) + up_b
        gelu32, gelu_pull = jax.vjp(gelu_exact, up_lin)
        gelu_out = gelu32.astype(jnp.bfloat16)
        layer_out = (resid_mid + jnp.einsum('bsf,fd->bsd', gelu_out, down_w, preferred_element_type=jnp.float32) + vecs_all[8]).astype(jnp.bfloat16)

        grad32 = grad_out.astype(jnp.float32)
        d_down = jnp.einsum('bsf,bsd->fd', gelu_out, grad_out, preferred_element_type=jnp.float32)
        d_gelu = jnp.einsum('bsd,fd->bsf', grad_out, down_w, preferred_element_type=jnp.float32)
        d_up_lin = gelu_pull(d_gelu)[0]
        d_up_b = d_up_lin.astype(jnp.bfloat16)
        d_up = jnp.einsum('bsd,bsf->df', norm_mid, d_up_b, preferred_element_type=jnp.float32)
        d_norm_mid = jnp.einsum('bsf,df->bsd', d_up_b, up_w, preferred_element_type=jnp.float32)
        d_resid_ln, d_gain2, d_bias2 = ln2_pull(d_norm_mid)
        d_resid = grad32 + d_resid_ln
        d_resid_b = d_resid.astype(jnp.bfloat16)
        d_outw = jnp.einsum('bsd,bse->de', attn_out, d_resid_b, preferred_element_type=jnp.float32)
        d_attn = jnp.einsum('bse,de->bsd', d_resid_b, out_w, preferred_element_type=jnp.float32).reshape(n_seq, seq_loc, n_heads, head_dim)
        d_attn_b = d_attn.astype(jnp.bfloat16)
        delta = jnp.swapaxes(jnp.sum(d_attn * attn32, axis=-1), 1, 2)

        def bwd_block(step, k_blk, v_blk, d_query):
            scores = block_scores(k_blk, step)
            weights = jnp.exp(scores - log_sum[..., None])
            d_weights = jnp.einsum('bqhd,bkhd->bhqk', d_attn_b, v_blk, preferred_element_type=jnp.float32)
            d_scores = (weights * (d_weights - delta[..., None])).astype(jnp.bfloat16)
            d_query = d_query + jnp.einsum('bhqk,bkhd->bqhd', d_scores, k_blk, preferred_element_type=jnp.float32)
            d_key = jnp.einsum('bhqk,bqhd->bkhd', d_scores, q_rot, preferred_element_type=jnp.float32)
            d_value = jnp.einsum('bhqk,bqhd->bkhd', weights.astype(jnp.bfloat16), d_attn_b, preferred_element_type=jnp.float32)
            return d_query, d_key, d_value

        def bwd_body(step, carry):
            k_blk, v_blk, dk_blk, dv_blk, d_query = carry
            d_query, d_key, d_value = bwd_block(step, k_blk, v_blk, d_query)
            return (lax.ppermute(k_blk, 'cp', send_pairs), lax.ppermute(v_blk, 'cp', send_pairs), lax.ppermute(dk_blk + d_key, 'cp', send_pairs), lax.ppermute(dv_blk + d_value, 'cp', send_pairs), d_query)

        kv_zero = jnp.zeros(q_rot.shape, jnp.float32)
        carry = (k_rot, v_val, kv_zero, kv_zero, kv_zero)
        carry = lax.fori_loop(0, cp_size - 1, bwd_body, carry)
        d_query, d_key, d_value = bwd_block(cp_size - 1, carry[0], carry[1], carry[4])
        d_key = lax.ppermute(carry[2] + d_key, 'cp', send_pairs)
        d_value = lax.ppermute(carry[3] + d_value, 'cp', send_pairs)

        d_q_lin = rotate(d_query, cos_t, -sin_t) * head_dim ** -0.5
        d_k_lin = rotate(d_key, cos_t, -sin_t)
        d_qkv_lin = jnp.stack([d_q_lin, d_k_lin, d_value], axis=2)
        d_qkv_b = d_qkv_lin.astype(jnp.bfloat16)
        d_qkvw = jnp.einsum('bsd,bsthe->dthe', norm_in, d_qkv_b, preferred_element_type=jnp.float32)
        d_norm_in = jnp.einsum('bsthe,dthe->bsd', d_qkv_b, qkv_w, preferred_element_type=jnp.float32)
        d_embedded, d_gain1, d_bias1 = ln1_pull(d_norm_in)
        d_embedded = d_embedded + d_resid
        d_table = jnp.einsum('bsv,bsd->vd', one_hot, (d_embedded * keep_scale).astype(jnp.bfloat16), preferred_element_type=jnp.float32)
        d_bqkv = jnp.sum(d_qkv_lin, axis=(0, 1)).reshape(3, model_dim)
        d_tail = jnp.stack([jnp.sum(d_resid, axis=(0, 1)), d_gain2, d_bias2, jnp.sum(grad32, axis=(0, 1))])
        d_vecs_full = jnp.concatenate([jnp.stack([d_gain1, d_bias1]), d_bqkv, d_tail], axis=0)
        return (layer_out, lax.psum(d_table, ('cp', 'fsdp')), reduce_grad(d_vecs_full, 1), reduce_grad(d_qkvw, 0), reduce_grad(d_outw, 0), reduce_grad(d_up, 0), reduce_grad(jnp.sum(d_up_lin, axis=(0, 1)), 0), reduce_grad(d_down, 0))

    in_specs = (P('fsdp', 'cp'), P('fsdp'), P(), P(None, 'fsdp'), P('fsdp', None, None, None), P('fsdp', None), P('fsdp', None), P('fsdp'), P('fsdp', None), P('fsdp', 'cp', None))
    out_specs = (P('fsdp', 'cp', None), P(), P(None, 'fsdp'), P('fsdp', None, None, None), P('fsdp', None), P('fsdp', None), P('fsdp'), P('fsdp', None))
    return jax.shard_map(local_step, mesh=mesh, in_specs=in_specs, out_specs=out_specs, check_vma=False)
```

profile of v0, /device:TPU:1, one launch (start us, length us, event | category | flops | bytes accessed | tf_op | source)
XLA Modules:
  0.0 2115.5 jit_solution(5098566839846624733)
XLA Ops:
  9.5 155.4 %all-gather = f32[64,10,9]{2,1,0:T(8,128)S(1)} all-gather(f32[1,10,9]{2,1,0:T(8,128)S(1)} %bitcast.181), channel_id=1, replica_groups=mesh['cp'=2,'fsdp'=64] {'fsdp'}, dimensions={0}, use_global_device_ids=true | all-gather | bytes 23400 | tf_op jit(solution)/shard_map/all_gather | solution.py:44
  166.6 29.7 %psum.56 = s32[16]{0:T(128)S(1)} all-reduce(s32[16]{0:T(128)S(1)} %get-tuple-element.124), channel_id=1, replica_groups=mesh['cp'=2,'fsdp'=64] {'cp'}, use_global_device_ids=true, to_apply=%region_1.0 | all-reduce | flops 16 | bytes 128 | tf_op jit(solution)/shard_map/psum | solution.py:58
  199.5 2.2 copy-done.2
  204.2 16.9 fusion.41
  221.1 3.1 slice_bitcast_fusion
  224.2 3.1 fusion.45
  232.6 150.5 %all-gather.1 = bf16[64,10,640]{2,1,0:T(8,128)(2,1)} all-gather(bf16[1,10,640]{2,1,0:T(8,128)(2,1)S(1)} %bitcast.182), channel_id=1, replica_groups=mesh['cp'=2,'fsdp'=64] {'fsdp'}, dimensions={0}, use_global_device_ids=true | all-gather | bytes 832000 | tf_op jit(solution)/shard_map/all_gather | solution.py:46
  386.2 288.9 %all-reduce = f32[2560]{0:T(1024)S(1)} all-reduce(f32[2560]{0:T(1024)S(1)} %dynamic-update-slice), channel_id=1, replica_groups=mesh['cp'=2,'fsdp'=64] {'fsdp'}, use_global_device_ids=true, to_apply=%add | all-reduce | flops 2560 | bytes 20480
  675.2 4.8 fusion.55
  680.0 82.3 %collective-permute-start.1 = (bf16[16,128,20,32]{1,3,2,0:T(8,128)(2,1)}, bf16[16,128,20,32]{1,3,2,0:T(8,128)(2,1)}, u32[]{:S(2)}, u32[]{:S(2)}) collective-permute-start(bf16[16,128,20,32]{1,3,2,0:T(8,128)(2,1)} %fusion.55), channel_id=1, source_target_pairs={{0,64},{64,0},{1,65},{65,1},{2,66},{66,2},{3,67},{67,3},{4,68},{68... | collective-permute-start | bytes 7864328 | tf_op jit(solution)/shard_map/while/body/eval_jaxpr/ppermute | solution.py:90
  762.2 10.3 select_reduce_fusion.1
  772.5 7.0 reshape.327
  779.5 10.9 select_reduce_fusion
  790.5 17.9 fusion.6
  809.2 14.4 fusion.20
  823.7 14.6 fusion.102
  838.4 3.5 fusion.103
  842.7 3.0 copy-done.15
  845.7 16.2 fusion.31
  861.9 50.3 %multiply_convert_fusion.2 = (bf16[16,128,2560]{2,1,0:T(8,128)(2,1)}, f32[16,128,2560]{2,1,0:T(8,128)}) fusion(f32[16,128,2560]{2,1,0:T(8,128)} %get-tuple-element.161, f32[2560]{0:T(1024)S(1)} %all-reduce, u16[128,2560]{1,0:T(8,128)(2,1)S(1)} %get-tuple-element.94, u16[128,2560]{1,0:T(8,128)(2,1)S(1)} %get-tuple-element.93), kind=kLoop, calls=%fused_computation.12 | loop fusion | flops 372244480 | bytes 53749760 | tf_op jit(solution)/shard_map/convert_element_type | solution.py:104
  912.2 26.7 %fusion.104 = (f32[2560]{0:T(1024)}, bf16[16,128,2560]{2,1,0:T(8,128)(2,1)}) fusion(f32[16,128,2560]{2,1,0:T(8,128)} %get-tuple-element.123, bf16[16,128,640]{2,1,0:T(8,128)(2,1)} %param.19, bf16[2560,640]{1,0:T(8,128)(2,1)} %all-gather.9.cloned.1.call-done, f32[16,128,2560]{2,1,0:T(8,128)} %get-tuple-element.161, f32[2560]{0:T(1024)S(1)} %all-reduce), kind=kOutput, calls=%fused_computation.190 | convolution fusion | flops 6794769920 | bytes 58347520 | tf_op jit(solution)/shard_map/bsd,fd->bsf/dot_general | solution.py:109
  938.9 12.3 multiply_reduce_fusion
  951.1 12.2 convolution_bitcast_fusion.1
  969.0 3.4 convolution_bitcast_fusion.3
  976.1 3.7 multiply_reduce_fusion.2
  979.8 15.7 multiply_convert_fusion.1
  995.5 12.6 convolution_bitcast_fusion.2
  1008.2 11.4 fusion.62
  1020.1 13.8 convolution_bitcast_fusion
  1034.6 15.4 multiply_convert_fusion
  1050.0 14.1 bitcast_add_fusion.1
  1064.2 12.9 bitcast_add_fusion
  1077.5 6.7 fusion.98
  1084.2 6.3 add_bitcast_fusion
  1090.6 6.6 subtract_bitcast_fusion
  1097.1 5.8 maximum_multiply_fusion
  1103.0 3.0 maximum_bitcast_fusion
  1106.0 14.7 fusion.67
  1120.7 16.1 copy.83
  1138.3 13.9 add_convert_fusion
  1153.8 34.1 %bitcast_reduce_fusion = (f32[640]{0:T(1024)S(1)}, f32[16,128]{1,0:T(8,128)S(1)}, f32[16,128,640,1,1]{2,1,3,0,4:T(8,128)}) fusion(f32[640]{0:T(1024)S(1)} %copy-done.45, f32[16,128]{1,0:T(8,128)S(1)} %copy-done.32, f32[16,128,640]{2,1,0:T(8,128)} %copy-done.2, f32[16,128]{1,0:T(8,128)S(1)} %copy-done.28, bf16[640,3,20,32,1]{3,2,1,0,4:T(8,128)(2,1)} %bitcast.183, ...), kind=kOutput, calls=%fused_computation.75 | convolution fusion | flops 5048890880 | bytes 28701696 | tf_op jit(solution)/shard_map/bsthe,dthe->bsd/dot_general | solution.py:149
  1188.0 4.9 fusion.46
  1193.0 6.0 fusion.74
  1199.9 251.1 %reduce-scatter.9.cloned.1.call-done = f32[40,640]{1,0:T(8,128)} async-done(((f32[2560,640]{1,0:T(8,128)}), f32[40,640]{1,0:T(8,128)}) %reduce-scatter.9.cloned.1.call-update) | async-done | bytes 102416
  1451.0 293.4 %reduce-scatter.7.cloned.1.call-done = f32[10,3,20,32]{3,2,1,0:T(8,128)} async-done(((f32[640,3,20,32]{3,2,1,0:T(8,128)}), f32[10,3,20,32]{3,2,1,0:T(8,128)}) %reduce-scatter.7.cloned.1.call-update) | async-done | bytes 76816 | tf_op jit(solution)/shard_map/reduce_scatter | solution.py:36
  1744.4 6.1 fusion.12
  1750.7 289.4 %all-reduce.6 = (f32[9,640]{1,0:T(8,128)S(1)}, f32[2560]{0:T(1024)S(1)}) all-reduce(f32[9,640]{1,0:T(8,128)S(1)} %concatenate.34, f32[2560]{0:T(1024)S(1)} %copy-done.48), channel_id=2, replica_groups=mesh['cp'=2,'fsdp'=64] {'fsdp'}, use_global_device_ids=true, to_apply=%region_23.24.clone | all-reduce | flops 8320 | bytes 66560
  2040.3 61.8 %all-reduce.8 = (f32[9,10]{1,0:T(8,128)}, f32[10,640]{1,0:T(8,128)}, f32[40]{0:T(128)}) all-reduce(f32[9,10]{1,0:T(8,128)S(1)} %constant_dynamic-slice_fusion.2, f32[10,640]{1,0:T(8,128)S(1)} %constant_dynamic-slice_fusion.1, f32[40]{0:T(128)S(1)} %dynamic-slice.8), channel_id=1, replica_groups=mesh['cp'=2,'fsdp'=64] {'cp'}, use_global_device_ids=true, to_apply=%region_24.25 | all-reduce | flops 6530 | bytes 52240 | tf_op jit(solution)/shard_map/psum | solution.py:36
  (221 shorter events, 39.2 us)
Async XLA Ops:
  7.2 190.6 %copy-start = (bf16[33,640]{1,0:T(8,128)(2,1)S(1)}, bf16[33,640]{1,0:T(8,128)(2,1)}, u32[]{:S(2)}) copy-start(bf16[33,640]{1,0:T(8,128)(2,1)} %param.12) | copy-start | bytes 126724
  7.2 197.0 %all-gather.7.cloned.1.call-start = ((), (), s32[]{:S(2)}) async-start(), calls=%async_computation.2 | async-start | bytes 11980800 | tf_op jit(solution)/shard_map/all_gather | solution.py:45
  7.9 764.6 %all-gather.11.cloned.1.call-start = ((), (), s32[]{:S(2)}) async-start(), calls=%async_computation.6 | async-start | bytes 5324800 | tf_op jit(solution)/shard_map/all_gather | solution.py:47
  8.7 903.5 %all-gather.9.cloned.1.call-start = ((), (), s32[]{:S(2)}) async-start(), calls=%async_computation.3 | async-start | bytes 3328000 | tf_op jit(solution)/shard_map/all_gather | solution.py:49
  165.8 38.4 %copy-start.44 = (f32[640]{0:T(1024)}, f32[640]{0:T(1024)S(1)}, u32[]{:S(2)}) copy-start(f32[640]{0:T(1024)S(1)} %get-tuple-element.109) | copy-start | bytes 7684
  165.8 38.4 %copy-start.50 = (f32[640]{0:T(1024)}, f32[640]{0:T(1024)S(1)}, u32[]{:S(2)}) copy-start(f32[640]{0:T(1024)S(1)} %get-tuple-element.108) | copy-start | bytes 7684
  197.8 640.6 %copy-start.27 = (f32[16,128]{1,0:T(8,128)}, f32[16,128]{1,0:T(8,128)S(1)}, u32[]{:S(2)}) copy-start(f32[16,128]{1,0:T(8,128)S(1)} %or_select_fusion) | copy-start | bytes 24580
  199.5 21.6 %copy-start.31 = (f32[16,128]{1,0:T(8,128)}, f32[16,128]{1,0:T(8,128)S(1)}, u32[]{:S(2)}) copy-start(f32[16,128]{1,0:T(8,128)S(1)} %broadcast_multiply_fusion.1) | copy-start | bytes 24580
  203.4 17.6 copy-start.36
  204.2 23.2 %copy-start.33 = (f32[128,16]{0,1:T(8,128)}, f32[128,16]{0,1:T(8,128)S(1)}, u32[]{:S(2)}) copy-start(f32[128,16]{0,1:T(8,128)S(1)} %get-tuple-element.146) | copy-start | bytes 24580
  228.9 550.6 %copy-start.5 = (bf16[16,128,20,16]{1,3,2,0:T(8,128)(2,1)}, bf16[16,128,20,16]{1,3,2,0:T(8,128)(2,1)S(1)}, u32[]{:S(2)}) copy-start(bf16[16,128,20,16]{1,3,2,0:T(8,128)(2,1)S(1)} %get-tuple-element.142) | copy-start | bytes 3932164
  228.9 550.5 %copy-start.6 = (bf16[16,128,20,16]{1,3,2,0:T(8,128)(2,1)}, bf16[16,128,20,16]{1,3,2,0:T(8,128)(2,1)S(1)}, u32[]{:S(2)}) copy-start(bf16[16,128,20,16]{1,3,2,0:T(8,128)(2,1)S(1)} %get-tuple-element.143) | copy-start | bytes 3932164
  229.0 155.6 %copy-start.54 = (u32[128]{0:T(128)S(1)}, u32[128]{0:T(128)}, u32[]{:S(2)}) copy-start(u32[128]{0:T(128)} %constant.166) | copy-start | bytes 1540
  229.0 156.9 %copy-start.56 = (f32[40]{0:T(128)S(1)}, f32[40]{0:T(128)}, u32[]{:S(2)}) copy-start(f32[40]{0:T(128)} %param.17) | copy-start | bytes 484
  229.0 446.1 %copy-start.55 = (s32[16]{0:T(128)S(1)}, s32[16]{0:T(128)}, u32[]{:S(2)}) copy-start(s32[16]{0:T(128)} %param.11) | copy-start | bytes 196
  232.1 547.4 %collective-permute-start = (bf16[16,128,20,32]{1,3,2,0:T(8,128)(2,1)}, bf16[16,128,20,32]{1,3,2,0:T(8,128)(2,1)}, u32[]{:S(2)}, u32[]{:S(2)}) collective-permute-start(bf16[16,128,20,32]{1,3,2,0:T(8,128)(2,1)} %pad_maximum_fusion.2), channel_id=1, source_target_pairs={{0,64},{64,0},{1,65},{65,1},{2,66},{66,2},{3,67},{67,3},{4,68},{68... | collective-permute-start | bytes 7864328 | tf_op jit(solution)/shard_map/while/body/eval_jaxpr/ppermute | solution.py:90
  232.5 919.7 %all-reduce.16.cloned.1.call-start = ((), (), s32[]{:S(2)}) async-start(), calls=%async_computation.8 | async-start | bytes 16384000
  675.1 87.2 %copy-start.8 = (bf16[16,128,20,16]{1,3,2,0:T(8,128)(2,1)S(1)}, bf16[16,128,20,16]{1,3,2,0:T(8,128)(2,1)}, u32[]{:S(2)}) copy-start(bf16[16,128,20,16]{1,3,2,0:T(8,128)(2,1)} %copy-done.7) | copy-start | bytes 3932164
  675.1 87.2 %copy-start.10 = (bf16[16,128,20,16]{1,3,2,0:T(8,128)(2,1)S(1)}, bf16[16,128,20,16]{1,3,2,0:T(8,128)(2,1)}, u32[]{:S(2)}) copy-start(bf16[16,128,20,16]{1,3,2,0:T(8,128)(2,1)} %copy-done.9) | copy-start | bytes 3932164
  675.2 134.1 %copy-start.29 = (pred[16,128]{1,0:T(8,128)(4,1)}, pred[16,128]{1,0:T(8,128)(4,1)S(1)}, u32[]{:S(2)}) copy-start(pred[16,128]{1,0:T(8,128)(4,1)S(1)} %get-tuple-element.150) | copy-start | bytes 6148
  675.2 148.5 %copy-start.42 = (pred[16,128]{1,0:T(8,128)(4,1)}, pred[16,128]{1,0:T(8,128)(4,1)S(1)}, u32[]{:S(2)}) copy-start(pred[16,128]{1,0:T(8,128)(4,1)S(1)} %get-tuple-element.149) | copy-start | bytes 6148
  680.0 143.7 %collective-permute-start.1 = (bf16[16,128,20,32]{1,3,2,0:T(8,128)(2,1)}, bf16[16,128,20,32]{1,3,2,0:T(8,128)(2,1)}, u32[]{:S(2)}, u32[]{:S(2)}) collective-permute-start(bf16[16,128,20,32]{1,3,2,0:T(8,128)(2,1)} %fusion.55), channel_id=1, source_target_pairs={{0,64},{64,0},{1,65},{65,1},{2,66},{66,2},{3,67},{67,3},{4,68},{68... | collective-permute-start | bytes 7864328 | tf_op jit(solution)/shard_map/while/body/eval_jaxpr/ppermute | solution.py:90
  779.5 11.0 copy-start.17
  790.5 17.9 copy-start.19
  808.3 15.3 copy-start.23
  808.4 15.3 copy-start.25
  809.2 29.1 %slice-start = ((s8[5242880]{0:T(1024)(128)(4,1)}), s8[1048576]{0:T(1024)(128)(4,1)S(1)}, s32[]{:S(2)}) async-start(s8[5242880]{0:T(1024)(128)(4,1)} %bitcast.164), calls=%async_computation.10 | async-start | bytes 2097152
  823.7 14.7 slice-start.1
  841.8 20.0 copy-start.3
  861.8 77.0 %slice-start.6 = ((s8[5242880]{0:T(1024)(128)(4,1)}), s8[1048576]{0:T(1024)(128)(4,1)S(1)}, s32[]{:S(2)}) async-start(s8[5242880]{0:T(1024)(128)(4,1)} %bitcast.170), calls=%async_computation.16 | async-start | bytes 2097152
  912.2 26.7 %slice-start.7 = ((s8[5242880]{0:T(1024)(128)(4,1)}), s8[4194304]{0:T(1024)(128)(4,1)S(1)}, s32[]{:S(2)}) async-start(s8[5242880]{0:T(1024)(128)(4,1)} %bitcast.170), calls=%async_computation.17 | async-start | bytes 8388608
  912.2 26.7 %copy-start.16 = (bf16[640,2560,1]{1,0,2:T(8,128)(2,1)S(1)}, bf16[640,2560,1]{1,0,2:T(8,128)(2,1)}, u32[]{:S(2)}) copy-start(bf16[640,2560,1]{1,0,2:T(8,128)(2,1)} %reshape.327) | copy-start | bytes 9830404
  972.5 478.5 %reduce-scatter.9.cloned.1.call-start = ((), (), s32[]{:S(2)}) async-start(), calls=%async_computation.7 | async-start | bytes 6656000
  1008.2 41.8 %collective-permute-start.2 = (f32[16,128,20,32]{1,3,2,0:T(8,128)}, f32[16,128,20,32]{1,3,2,0:T(8,128)}, u32[]{:S(2)}, u32[]{:S(2)}) collective-permute-start(f32[16,128,20,32]{1,3,2,0:T(8,128)} %convolution_bitcast_fusion.2), channel_id=1, source_target_pairs={{0,64},{64,0},{1,65},{65,1},{2,66},{66,2},{3,67},{67,3},{4,68},{68... | collective-permute-start | bytes 15728648 | tf_op jit(solution)/shard_map/while/body/eval_jaxpr/ppermute | solution.py:135
  1019.6 44.6 %collective-permute-start.4 = (f32[16,128,20,32]{1,3,2,0:T(8,128)}, f32[16,128,20,32]{1,3,2,0:T(8,128)}, u32[]{:S(2)}, u32[]{:S(2)}) collective-permute-start(f32[16,128,20,32]{1,3,2,0:T(8,128)} %fusion.62), channel_id=1, source_target_pairs={{0,64},{64,0},{1,65},{65,1},{2,66},{66,2},{3,67},{67,3},{4,68},{68... | collective-permute-start | bytes 15728648 | tf_op jit(solution)/shard_map/while/body/eval_jaxpr/ppermute | solution.py:135
  1033.9 710.4 %reduce-scatter.7.cloned.1.call-start = ((), (), s32[]{:S(2)}) async-start(), calls=%async_computation.5 | async-start | bytes 23961600 | tf_op jit(solution)/shard_map/reduce_scatter | solution.py:36
  1064.2 26.4 %collective-permute-start.3 = (f32[16,128,20,32]{1,3,2,0:T(8,128)}, f32[16,128,20,32]{1,3,2,0:T(8,128)}, u32[]{:S(2)}, u32[]{:S(2)}) collective-permute-start(f32[16,128,20,32]{1,3,2,0:T(8,128)} %bitcast_add_fusion.1), channel_id=1, source_target_pairs={{0,64},{64,0},{1,65},{65,1},{2,66},{66,2},{3,67},{67,3},{4,68},{68... | collective-permute-start | bytes 15728648 | tf_op jit(solution)/shard_map/ppermute | solution.py:141
  1077.1 28.8 %collective-permute-start.5 = (f32[16,128,20,32]{1,3,2,0:T(8,128)}, f32[16,128,20,32]{1,3,2,0:T(8,128)}, u32[]{:S(2)}, u32[]{:S(2)}) collective-permute-start(f32[16,128,20,32]{1,3,2,0:T(8,128)} %bitcast_add_fusion), channel_id=1, source_target_pairs={{0,64},{64,0},{1,65},{65,1},{2,66},{66,2},{3,67},{67,3},{4,68},{68... | collective-permute-start | bytes 15728648 | tf_op jit(solution)/shard_map/ppermute | solution.py:142
  1084.2 6.3 copy-start.34
  1084.2 6.3 copy-start.46
  1097.1 8.8 slice-start.2
  1136.8 965.2 %all-reduce.14.cloned.1.call-start = ((), (), s32[]{:S(2)}) async-start(), calls=%async_computation.4 | async-start | bytes 204800 | tf_op jit(solution)/shard_map/psum | solution.py:156
  1138.3 49.7 %slice-start.4 = ((s8[5242880]{0:T(1024)(128)(4,1)}), s8[1048576]{0:T(1024)(128)(4,1)S(1)}, s32[]{:S(2)}) async-start(s8[5242880]{0:T(1024)(128)(4,1)} %bitcast.168), calls=%async_computation.14 | async-start | bytes 2097152
  1153.8 34.1 %copy-start.41 = (f32[16,128]{1,0:T(8,128)S(1)}, f32[16,128]{1,0:T(8,128)}, u32[]{:S(2)}) copy-start(f32[16,128]{1,0:T(8,128)} %copy-done.40) | copy-start | bytes 24580
  1153.8 34.2 %slice-start.5 = ((s8[5242880]{0:T(1024)(128)(4,1)}), s8[4194304]{0:T(1024)(128)(4,1)S(1)}, s32[]{:S(2)}) async-start(s8[5242880]{0:T(1024)(128)(4,1)} %bitcast.168), calls=%async_computation.15 | async-start | bytes 8388608
  1199.0 903.0 %all-reduce.18.cloned.1.call-start = ((), (), s32[]{:S(2)}) async-start(), calls=%async_computation.9 | async-start | bytes 1269760 | tf_op jit(solution)/shard_map/psum | solution.py:36
  1744.4 6.3 copy-start.48
  1744.4 364.1 %copy-start.1 = (bf16[33,640]{1,0:T(8,128)(2,1)S(1)}, bf16[33,640]{1,0:T(8,128)(2,1)}, u32[]{:S(2)}) copy-start(bf16[33,640]{1,0:T(8,128)(2,1)} %param.12) | copy-start | bytes 126724
  (31 other events, 85.6 us)
Sparse Core Ops, SparseCore 0:
  10.7 92.5 all-gather.6
  106.2 68.2 all-gather.10
  232.6 58.8 all-gather.8
  972.6 159.4 all-reduce.15
  1134.4 316.5 reduce-scatter.8
  1455.7 288.5 reduce-scatter.6
  1749.7 145.7 all-reduce.13
  1898.7 22.8 all-reduce.17
where the time goes:
time: 2130 us; the launch traced here: 2120 us
  blocking collectives  976 us (46%)
  waiting for transfers between devices  546 us (26%)
  matrix products  323 us (15%)
  other arithmetic  115 us (5%)
  starting transfers between devices  83.9 us (4%)
  local copies, waits for them, and re-layouts  54.4 us (3%)
    unnamed x2, blocking collectives  578 us
    reduce_scatter x1, waiting for transfers between devices, reduce_grad(): lax.psum_scatter(full_grad, 'fsdp', scatter_dimension=axis_dim, tiled=True)  293 us
    unnamed x10, waiting for transfers between devices  253 us
    all_gather x1, blocking collectives, local_step(): vecs_all = lax.all_gather(layer_vecs, 'fsdp', axis=1, tiled=True)  155 us
    all_gather x1, blocking collectives, local_step(): out_w = lax.all_gather(w_out, 'fsdp', axis=0, tiled=True)  151 us
    ppermute x1, starting transfers between devices, fwd_body(): lax.ppermute(v_blk, 'cp', send_pairs)  82.3 us
    psum x1, blocking collectives, reduce_grad(): lax.psum(lax.psum_scatter(full_grad, 'fsdp', scatter_dimension=axis_dim,...  61.8 us
    convert_element_type x1, other arithmetic, local_step(): gelu_out = gelu32.astype(jnp.bfloat16)  50.3 us
  transfers between devices with their start and end apart: 14, of which 2 were waited for; matrix products, arithmetic and copies ran while one was open for 20% of the time, Pallas kernels for 0%

commit v1 on v0

v1 whole, which is shorter than its diff:
```python
import functools

import jax
import jax.numpy as jnp
from jax import lax
from jax.experimental import pallas as pl
from jax.experimental.pallas import tpu as pltpu
from jax.sharding import PartitionSpec as P

MASK_ID = 32
LN_EPS = 1e-5
ROPE_BASE = 10000.0
TRAIN_RATIO = 0.15 * 0.8
NEG_BIG = -1e30
SIDE = 4
COLORS = 3
NB = 10
HALF = 5
SMALL_ROWS = 120
MESH_ID = pl.DeviceIdType.MESH
ANY = pl.BlockSpec(memory_space=pl.ANY)

GATHER_ORDER = ((2, 1, 0), (1, 0, 2), (0, 2, 1))
REDUCE_ORDER = ((0, 1, 2), (1, 2, 0), (2, 0, 1))


def my_coords():
    chip = lax.axis_index('fsdp')
    return [chip // 16, lax.rem(chip // 4, 4), lax.rem(chip, 4)]


def moved(coords, dim, by):
    out = list(coords)
    out[dim] = lax.rem(coords[dim] + by + SIDE, SIDE)
    return out


def chip_id(coords):
    return {'fsdp': coords[0] * 16 + coords[1] * 4 + coords[2]}


def entry_barrier(coords, cp):
    barrier = pltpu.get_barrier_semaphore()
    for dim in range(3):
        for by in (1, 2, 3):
            pl.semaphore_signal(barrier, inc=1, device_id=chip_id(moved(coords, dim, by)), device_id_type=MESH_ID)
    pl.semaphore_signal(barrier, inc=1, device_id={'cp': 1 - cp}, device_id_type=MESH_ID)
    pl.semaphore_wait(barrier, 10)


def push(src, dst, send_sem, recv_sem, target):
    return pltpu.make_async_remote_copy(src_ref=src, dst_ref=dst, send_sem=send_sem, recv_sem=recv_sem, device_id=target, device_id_type=MESH_ID)


def gather_kernel(w_loc, s_loc, g_own, t_own, w_all, s_all, g_oth, t_oth, ssem, rsem, fsend, frecv, s_ssem, s_rsem, psend, precv, lsem):
    cp = lax.axis_index('cp')
    me = my_coords()
    mate = {'cp': 1 - cp}
    own_w = pltpu.make_async_copy(w_loc, w_all.at[:, me[0], me[1], me[2]], lsem.at[0])
    own_s = pltpu.make_async_copy(s_loc, s_all.at[me[0], me[1], me[2]], lsem.at[1])
    own_w.start()
    own_s.start()
    entry_barrier(me, cp)
    swap_g = push(g_own.at[pl.ds(8 * (1 - cp), 8)], g_oth, psend.at[0], precv.at[0], mate)
    swap_t = push(t_own.at[pl.ds(8 * (1 - cp), 8)], t_oth, psend.at[1], precv.at[1], mate)
    swap_t.start()

    def region(ref, first, count, dims, at):
        index = [slice(None) if d in dims else at[d] for d in range(3)]
        return ref.at[(pl.ds(first, count), *index)]

    def small_region(dims, at):
        index = [slice(None) if d in dims else at[d] for d in range(3)]
        return s_all.at[tuple(index)]

    forwards = []
    pending = []
    own_s.wait()
    own_w.wait()
    for phase in range(3):
        firsts = {}
        for color in range(COLORS):
            dim = GATHER_ORDER[color][phase]
            done = GATHER_ORDER[color][:phase]
            base = cp * (COLORS * NB) + color * NB
            mine = region(w_all, base, NB, done, me)
            right, left = chip_id(moved(me, dim, 1)), chip_id(moved(me, dim, 3))
            to_right = push(mine, mine, ssem.at[color, phase, 0], rsem.at[color, phase, 0], right)
            to_left = push(mine, mine, ssem.at[color, phase, 1], rsem.at[color, phase, 1], left)
            to_right.start()
            to_left.start()
            firsts[color] = (to_right, to_left)
            pending += [to_right, to_left]
            if color == 0:
                s_mine = small_region(done, me)
                s_right = push(s_mine, s_mine, s_ssem.at[phase, 0], s_rsem.at[phase, 0], right)
                s_left = push(s_mine, s_mine, s_ssem.at[phase, 1], s_rsem.at[phase, 1], left)
                s_right.start()
                s_left.start()
                pending += [s_right, s_left]
        seconds = {}
        for color in range(COLORS):
            dim = GATHER_ORDER[color][phase]
            done = GATHER_ORDER[color][:phase]
            base = cp * (COLORS * NB) + color * NB
            right, left = chip_id(moved(me, dim, 1)), chip_id(moved(me, dim, 3))
            from_left, from_right = moved(me, dim, 3), moved(me, dim, 1)
            to_right, to_left = firsts[color]
            to_right.wait_recv()
            part = region(w_all, base, HALF, done, from_left)
            on_right = push(part, part, ssem.at[color, phase, 2], rsem.at[color, phase, 2], right)
            on_right.start()
            whole_l = region(w_all, base, NB, done, from_left)
            fwd_l = push(whole_l, whole_l, fsend.at[color, phase, 0], frecv.at[color, phase, 0], mate)
            fwd_l.start()
            to_left.wait_recv()
            part = region(w_all, base + HALF, HALF, done, from_right)
            on_left = push(part, part, ssem.at[color, phase, 3], rsem.at[color, phase, 3], left)
            on_left.start()
            whole_r = region(w_all, base, NB, done, from_right)
            fwd_r = push(whole_r, whole_r, fsend.at[color, phase, 1], frecv.at[color, phase, 1], mate)
            fwd_r.start()
            seconds[color] = (on_right, on_left)
            pending += [on_right, on_left]
            forwards += [fwd_l, fwd_r]
            if color == 0:
                s_right.wait_recv()
                s_left.wait_recv()
                s_part = small_region(done, from_left)
                s_on = push(s_part, s_part, s_ssem.at[phase, 2], s_rsem.at[phase, 2], right)
                s_on.start()
                pending.append(s_on)
        for color in range(COLORS):
            dim = GATHER_ORDER[color][phase]
            done = GATHER_ORDER[color][:phase]
            base = cp * (COLORS * NB) + color * NB
            on_right, on_left = seconds[color]
            on_right.wait_recv()
            on_left.wait_recv()
            far = region(w_all, base, NB, done, moved(me, dim, 2))
            fwd_f = push(far, far, fsend.at[color, phase, 2], frecv.at[color, phase, 2], mate)
            fwd_f.start()
            forwards.append(fwd_f)
            if color == 0:
                s_on.wait_recv()
        if phase == 0:
            swap_g.start()
    for copy in forwards:
        copy.wait_recv()
    swap_g.wait()
    swap_t.wait()
    for copy in pending + forwards:
        copy.wait_send()


def gather_all(w_loc, s_loc, grad_out, tokens):
    bf16, f32 = jnp.bfloat16, jnp.float32
    blocks = w_loc.shape[0]
    seqs, pos, width = grad_out.shape
    dma = pltpu.SemaphoreType.DMA
    return pl.pallas_call(
        gather_kernel,
        out_shape=(
            jax.ShapeDtypeStruct((blocks, SIDE, SIDE, SIDE, NB, 128), bf16),
            jax.ShapeDtypeStruct((SIDE, SIDE, SIDE, 8, 128), f32),
            jax.ShapeDtypeStruct((seqs // 2, pos, width), bf16),
            jax.ShapeDtypeStruct((seqs // 2, pos), jnp.int32),
        ),
        in_specs=[ANY] * 4,
        out_specs=(ANY,) * 4,
        scratch_shapes=[dma((3, 3, 4)), dma((3, 3, 4)), dma((3, 3, 3)), dma((3, 3, 3)), dma((3, 3)), dma((3, 3)), dma((2,)), dma((2,)), dma((2,))],
        compiler_params=pltpu.CompilerParams(collective_id=0, has_side_effects=True),
        name='gather_weights',
    )(w_loc, s_loc, grad_out, tokens)


def reduce_kernel(g_all, small, y_oth, g_out, s_out, y_recv, held, pair, ra0, rb0, ra1, rb1, ra2, rb2, s_pair, s_slots, s_acc,
                  lsem, psend, precv, ssem, rsem, s_ssem, s_rsem, osend, orecv, msem):
    cp = lax.axis_index('cp')
    me = my_coords()
    mate = {'cp': 1 - cp}
    per = COLORS * NB
    loads = []
    for color in range(COLORS):
        load = pltpu.make_async_copy(g_all.at[pl.ds(cp * per + color * NB, NB)], held.at[pl.ds(color * NB, NB)], lsem.at[color])
        load.start()
        loads.append(load)
    s_load = pltpu.make_async_copy(small, s_acc, lsem.at[3])
    s_load.start()
    entry_barrier(me, cp)
    sends = []
    s_swap = push(small, s_pair, psend.at[3], precv.at[3], mate)
    s_swap.start()
    swaps = []
    for color in range(COLORS):
        swap = push(g_all.at[pl.ds((1 - cp) * per + color * NB, NB)], pair.at[pl.ds(color * NB, NB)], psend.at[color], precv.at[color], mate)
        swap.start()
        swaps.append(swap)
    y_swap = push(y_oth, y_recv, psend.at[4], precv.at[4], mate)
    y_swap.start()

    bufs = ((ra0, rb0), (ra1, rb1), (ra2, rb2))

    def index_of(dims, at):
        return [slice(None) if d in dims else at[d] for d in range(3)]

    def region(first, count, dims, at):
        return held.at[(pl.ds(first, count), *index_of(dims, at))]

    def start_phase(color, phase):
        dim = REDUCE_ORDER[color][phase]
        rest = REDUCE_ORDER[color][phase + 1:]
        base = color * NB
        ra, rb = bufs[phase]
        right, left = moved(me, dim, 1), moved(me, dim, 3)
        far = moved(me, dim, 2)
        out = [
            push(region(base, HALF, rest, far), ra.at[color, 0], ssem.at[color, phase, 0], rsem.at[color, phase, 0], chip_id(right)),
            push(region(base + HALF, HALF, rest, far), ra.at[color, 1], ssem.at[color, phase, 1], rsem.at[color, phase, 1], chip_id(left)),
            push(region(base + HALF, HALF, rest, right), rb.at[color, 0, pl.ds(HALF, HALF)], ssem.at[color, phase, 2], rsem.at[color, phase, 2], chip_id(right)),
            push(region(base, HALF, rest, left), rb.at[color, 1, pl.ds(0, HALF)], ssem.at[color, phase, 3], rsem.at[color, phase, 3], chip_id(left)),
        ]
        for copy in out:
            copy.start()
        sends.extend(out)
        return out

    def middle(color, phase, copies):
        dim = REDUCE_ORDER[color][phase]
        rest = REDUCE_ORDER[color][phase + 1:]
        base = color * NB
        ra, rb = bufs[phase]
        right, left = moved(me, dim, 1), moved(me, dim, 3)
        copies[0].wait_recv()
        to_r = index_of(rest, right)

        @pl.loop(0, HALF)
        def _(b):
            held[(base + b, *to_r)] += ra[color, 0, b]

        fwd_r = push(region(base, HALF, rest, right), rb.at[color, 0, pl.ds(0, HALF)], ssem.at[color, phase, 4], rsem.at[color, phase, 4], chip_id(right))
        fwd_r.start()
        copies[1].wait_recv()
        to_l = index_of(rest, left)

        @pl.loop(0, HALF)
        def _(b):
            held[(base + HALF + b, *to_l)] += ra[color, 1, b]

        fwd_l = push(region(base + HALF, HALF, rest, left), rb.at[color, 1, pl.ds(HALF, HALF)], ssem.at[color, phase, 5], rsem.at[color, phase, 5], chip_id(left))
        fwd_l.start()
        sends.extend([fwd_r, fwd_l])
        return [fwd_r, fwd_l]

    def finish(color, phase, copies, late):
        rest = REDUCE_ORDER[color][phase + 1:]
        base = color * NB
        ra, rb = bufs[phase]
        copies[2].wait_recv()
        copies[3].wait_recv()
        late[0].wait_recv()
        late[1].wait_recv()
        here = index_of(rest, me)

        @pl.loop(0, NB)
        def _(b):
            held[(base + b, *here)] += rb[color, 0, b] + rb[color, 1, b]

    s_copies = []

    def small_start(phase):
        dim = REDUCE_ORDER[0][phase]
        out = []
        for by in (1, 2, 3):
            out.append(push(s_acc.at[cp], s_slots.at[phase, by - 1], s_ssem.at[phase, by - 1], s_rsem.at[phase, by - 1], chip_id(moved(me, dim, by))))
        for copy in out:
            copy.start()
        return out

    def small_finish(phase, copies):
        dim = REDUCE_ORDER[0][phase]
        for copy in copies:
            copy.wait()
        mine = me[dim]
        total = None
        own = s_acc[cp]
        got = [own] + [s_slots[phase, by] for by in range(3)]
        for coord in range(SIDE):
            gap = lax.rem(mine - coord + SIDE, SIDE)
            value = jnp.where(gap == 0, got[0], jnp.where(gap == 1, got[1], jnp.where(gap == 2, got[2], got[3])))
            total = value if total is None else total + value
        s_acc[cp] = total

    s_load.wait()
    s_swap.wait()
    s_acc[...] = s_acc[...] + s_pair[...]
    s_out_copies = small_start(0)
    started = []
    for color in range(COLORS):
        loads[color].wait()
        swaps[color].wait_recv()

        @pl.loop(0, NB)
        def _(b):
            for z in range(SIDE):
                held[color * NB + b, z] += pair[color * NB + b, z]

        started.append(start_phase(color, 0))
    for phase in range(3):
        late = [middle(color, phase, started[color]) for color in range(COLORS)]
        nxt = []
        for color in range(COLORS):
            finish(color, phase, started[color], late[color])
            if phase < 2:
                nxt.append(start_phase(color, phase + 1))
        small_finish(phase, s_out_copies)
        if phase < 2:
            s_out_copies = small_start(phase + 1)
        started = nxt
    mine = held.at[:, me[0], me[1], me[2]]
    out_far = push(mine, g_out.at[pl.ds(cp * per, per)], osend.at[0], orecv.at[0], mate)
    out_far.start()
    s_far = push(s_acc.at[cp], s_out.at[cp], osend.at[1], orecv.at[1], mate)
    s_far.start()
    out_own = pltpu.make_async_copy(mine, g_out.at[pl.ds(cp * per, per)], msem.at[0])
    out_own.start()
    s_own = pltpu.make_async_copy(s_acc.at[cp], s_out.at[cp], msem.at[1])
    s_own.start()
    for copy in sends:
        copy.wait_send()
    for copy in swaps:
        copy.wait_send()
    y_swap.wait()
    out_own.wait()
    s_own.wait()
    out_far.wait()
    s_far.wait()


def reduce_all(g_all, small, y_oth):
    f32 = jnp.float32
    blocks = g_all.shape[0]
    dma = pltpu.SemaphoreType.DMA
    vm = pltpu.VMEM
    return pl.pallas_call(
        reduce_kernel,
        out_shape=(
            jax.ShapeDtypeStruct((blocks, NB, 128), f32),
            jax.ShapeDtypeStruct(small.shape, f32),
            jax.ShapeDtypeStruct(y_oth.shape, y_oth.dtype),
        ),
        in_specs=[ANY] * 3,
        out_specs=(ANY,) * 3,
        scratch_shapes=[
            vm((blocks // 2, SIDE, SIDE, SIDE, NB, 128), f32),
            vm((blocks // 2, SIDE, SIDE, SIDE, NB, 128), f32),
            vm((COLORS, 2, HALF, SIDE, SIDE, NB, 128), f32),
            vm((COLORS, 2, NB, SIDE, SIDE, NB, 128), f32),
            vm((COLORS, 2, HALF, SIDE, NB, 128), f32),
            vm((COLORS, 2, NB, SIDE, NB, 128), f32),
            vm((COLORS, 2, HALF, NB, 128), f32),
            vm((COLORS, 2, NB, NB, 128), f32),
            vm(small.shape, f32),
            vm((3, 3) + small.shape[1:], f32),
            vm(small.shape, f32),
            dma((4,)), dma((5,)), dma((5,)), dma((3, 3, 6)), dma((3, 3, 6)), dma((3, 3)), dma((3, 3)), dma((2,)), dma((2,)), dma((2,)),
        ],
        compiler_params=pltpu.CompilerParams(collective_id=1, has_side_effects=True, vmem_limit_bytes=62 * 1024 * 1024),
        name='reduce_grads',
    )(g_all, small, y_oth)


def layer_norm(z_in, ln_gain, ln_bias):
    row_mean = jnp.mean(z_in, axis=-1, keepdims=True)
    centered = z_in - row_mean
    row_var = jnp.mean(centered * centered, axis=-1, keepdims=True)
    return centered * lax.rsqrt(row_var + LN_EPS) * ln_gain + ln_bias


def gelu_exact(z_in):
    return jax.nn.gelu(z_in, approximate=False)


def rope_tables(positions, head_dim):
    inv_freq = 1.0 / (ROPE_BASE ** (jnp.arange(0, head_dim, 2, dtype=jnp.float32) / head_dim))
    angles = positions.astype(jnp.float32)[:, None] * inv_freq[None, :]
    return jnp.cos(angles)[:, None, :], jnp.sin(angles)[:, None, :]


def rotate(z_in, cos_t, sin_t):
    lower_half, upper_half = jnp.split(z_in, 2, axis=-1)
    return jnp.concatenate([lower_half * cos_t - upper_half * sin_t, upper_half * cos_t + lower_half * sin_t], axis=-1)


def layer_compute(tokens, lengths, positions, embed_table, vecs_all, w_all, up_b, grad_out):
    f32, bf16 = jnp.float32, jnp.bfloat16
    n_seq, seq_len = tokens.shape
    vocab_size, model_dim = embed_table.shape
    n_heads, head_dim = 20, 32
    mats = w_all.reshape(60, model_dim, 128)
    qkv_w = mats[:15].transpose(1, 0, 2).reshape(model_dim, 3, n_heads, head_dim)
    out_w = mats[15:20].transpose(1, 0, 2).reshape(model_dim, model_dim)
    up_w = mats[20:40].transpose(1, 0, 2).reshape(model_dim, 2560)
    down_w = mats[40:60].reshape(4, 5, model_dim, 128).transpose(0, 2, 1, 3).reshape(2560, model_dim)
    len_col = lengths[:, None]
    is_mask = tokens == MASK_ID
    tok_valid = positions[None, :] < len_col
    mask_count = jnp.sum(is_mask.astype(jnp.int32), axis=1)
    drop_scale = (1.0 - TRAIN_RATIO) / (1.0 - mask_count.astype(f32) / lengths.astype(f32))
    keep_scale = jnp.where(is_mask | jnp.logical_not(tok_valid), 0.0, drop_scale[:, None])[:, :, None]
    one_hot = (tokens[:, :, None] == jnp.arange(vocab_size)).astype(bf16)
    embedded = jnp.einsum('bsv,vd->bsd', one_hot, embed_table, preferred_element_type=f32) * keep_scale
    norm_in32, ln1_pull = jax.vjp(layer_norm, embedded, vecs_all[0], vecs_all[1])
    norm_in = norm_in32.astype(bf16)
    qkv_lin = jnp.einsum('bsd,dthe->bsthe', norm_in, qkv_w, preferred_element_type=f32) + vecs_all[2:5].reshape(3, n_heads, head_dim)
    cos_t, sin_t = rope_tables(positions, head_dim)
    q_rot = rotate(qkv_lin[:, :, 0] * head_dim ** -0.5, cos_t, sin_t).astype(bf16)
    k_rot = rotate(qkv_lin[:, :, 1], cos_t, sin_t).astype(bf16)
    v_val = qkv_lin[:, :, 2].astype(bf16)
    scores = jnp.einsum('bqhd,bkhd->bhqk', q_rot, k_rot, preferred_element_type=f32)
    scores = jnp.where(tok_valid[:, None, None, :], scores, NEG_BIG)
    weights = jax.nn.softmax(scores, axis=-1)
    weights_b = weights.astype(bf16)
    attn32 = jnp.einsum('bhqk,bkhd->bqhd', weights_b, v_val, preferred_element_type=f32)
    attn_out = attn32.astype(bf16).reshape(n_seq, seq_len, model_dim)
    resid_mid = embedded + jnp.einsum('bsd,de->bse', attn_out, out_w, preferred_element_type=f32) + vecs_all[5]
    norm_mid32, ln2_pull = jax.vjp(layer_norm, resid_mid, vecs_all[6], vecs_all[7])
    norm_mid = norm_mid32.astype(bf16)
    up_lin = jnp.einsum('bsd,df->bsf', norm_mid, up_w, preferred_element_type=f32) + up_b
    gelu32, gelu_pull = jax.vjp(gelu_exact, up_lin)
    gelu_out = gelu32.astype(bf16)
    layer_out = (resid_mid + jnp.einsum('bsf,fd->bsd', gelu_out, down_w, preferred_element_type=f32) + vecs_all[8]).astype(bf16)

    grad32 = grad_out.astype(f32)
    d_down = jnp.einsum('bsf,bsd->fd', gelu_out, grad_out, preferred_element_type=f32)
    d_gelu = jnp.einsum('bsd,fd->bsf', grad_out, down_w, preferred_element_type=f32)
    d_up_lin = gelu_pull(d_gelu)[0]
    d_up_b = d_up_lin.astype(bf16)
    d_up = jnp.einsum('bsd,bsf->df', norm_mid, d_up_b, preferred_element_type=f32)
    d_norm_mid = jnp.einsum('bsf,df->bsd', d_up_b, up_w, preferred_element_type=f32)
    d_resid_ln, d_gain2, d_bias2 = ln2_pull(d_norm_mid)
    d_resid = grad32 + d_resid_ln
    d_resid_b = d_resid.astype(bf16)
    d_outw = jnp.einsum('bsd,bse->de', attn_out, d_resid_b, preferred_element_type=f32)
    d_attn = jnp.einsum('bse,de->bsd', d_resid_b, out_w, preferred_element_type=f32).reshape(n_seq, seq_len, n_heads, head_dim)
    d_attn_b = d_attn.astype(bf16)
    delta = jnp.swapaxes(jnp.sum(d_attn * attn32, axis=-1), 1, 2)
    d_weights = jnp.einsum('bqhd,bkhd->bhqk', d_attn_b, v_val, preferred_element_type=f32)
    d_scores = (weights * (d_weights - delta[..., None])).astype(bf16)
    d_query = jnp.einsum('bhqk,bkhd->bqhd', d_scores, k_rot, preferred_element_type=f32)
    d_key = jnp.einsum('bhqk,bqhd->bkhd', d_scores, q_rot, preferred_element_type=f32)
    d_value = jnp.einsum('bhqk,bqhd->bkhd', weights_b, d_attn_b, preferred_element_type=f32)
    d_q_lin = rotate(d_query, cos_t, -sin_t) * head_dim ** -0.5
    d_k_lin = rotate(d_key, cos_t, -sin_t)
    d_qkv_lin = jnp.stack([d_q_lin, d_k_lin, d_value], axis=2)
    d_qkv_b = d_qkv_lin.astype(bf16)
    d_qkvw = jnp.einsum('bsd,bsthe->dthe', norm_in, d_qkv_b, preferred_element_type=f32)
    d_norm_in = jnp.einsum('bsthe,dthe->bsd', d_qkv_b, qkv_w, preferred_element_type=f32)
    d_embedded, d_gain1, d_bias1 = ln1_pull(d_norm_in)
    d_embedded = d_embedded + d_resid
    d_table = jnp.einsum('bsv,bsd->vd', one_hot, (d_embedded * keep_scale).astype(bf16), preferred_element_type=f32)
    d_bqkv = jnp.sum(d_qkv_lin, axis=(0, 1)).reshape(3, model_dim)
    d_tail = jnp.stack([jnp.sum(d_resid, axis=(0, 1)), d_gain2, d_bias2, jnp.sum(grad32, axis=(0, 1))])
    d_vecs = jnp.concatenate([jnp.stack([d_gain1, d_bias1]), d_bqkv, d_tail], axis=0)
    g_all = jnp.concatenate([
        d_qkvw.reshape(model_dim, 15, 128).transpose(1, 0, 2),
        d_outw.reshape(model_dim, 5, 128).transpose(1, 0, 2),
        d_up.reshape(model_dim, 20, 128).transpose(1, 0, 2),
        d_down.reshape(4, model_dim, 5, 128).transpose(0, 2, 1, 3).reshape(20, model_dim, 128),
    ], axis=0)
    return layer_out, d_table, d_vecs, g_all, jnp.sum(d_up_lin, axis=(0, 1))


def solution(mesh):
    chips = mesh.shape['fsdp']

    def local_step(tokens, lengths, embed_table, layer_vecs, w_qkv, w_out, w_up, b_up, w_down, grad_out):
        f32 = jnp.float32
        cp = lax.axis_index('cp')
        chip = lax.axis_index('fsdp')
        n_seq, seq_loc = tokens.shape
        half = n_seq // 2
        rows = w_qkv.shape[0]
        vocab, width = embed_table.shape
        w_loc = jnp.concatenate([
            w_qkv.reshape(rows, 15, 128).transpose(1, 0, 2),
            w_out.reshape(rows, 5, 128).transpose(1, 0, 2),
            w_up.reshape(rows, chips, 4, NB).transpose(2, 1, 3, 0).reshape(20, 128, rows).transpose(0, 2, 1),
            w_down.reshape(4, NB, 5, 128).transpose(0, 2, 1, 3).reshape(20, NB, 128),
        ], axis=0)
        s_loc = jnp.pad(jnp.concatenate([layer_vecs.reshape(-1), b_up]), (0, 1024 - 130)).reshape(8, 128)
        w_all, s_all, g_oth, t_oth = gather_all(w_loc, s_loc, grad_out, tokens)
        s_flat = s_all.reshape(chips, 1024)
        vecs_all = s_flat[:, :90].reshape(chips, 9, NB).transpose(1, 0, 2).reshape(9, width)
        up_b = s_flat[:, 90:130].reshape(chips, 4, NB).transpose(1, 0, 2).reshape(-1)
        start = half * cp
        tok_full = jnp.concatenate([lax.dynamic_slice_in_dim(tokens, start, half, 0), t_oth], axis=1)
        grad_full = jnp.concatenate([lax.dynamic_slice_in_dim(grad_out, start, half, 0), g_oth], axis=1)
        len_own = lax.dynamic_slice_in_dim(lengths, start, half, 0)
        positions = jnp.concatenate([cp * seq_loc + jnp.arange(seq_loc), (1 - cp) * seq_loc + jnp.arange(seq_loc)])
        layer_out, d_table, d_vecs, g_all, d_bup = layer_compute(tok_full, len_own, positions, embed_table, vecs_all, w_all, up_b, grad_full)
        small = jnp.concatenate([d_table.reshape(-1), d_vecs.reshape(-1), d_bup])
        small = jnp.pad(small, (0, 2 * SMALL_ROWS * 128 - small.shape[0])).reshape(2, SMALL_ROWS, 128)
        y_own, y_oth = layer_out[:, :seq_loc], layer_out[:, seq_loc:]
        g_red, s_red, y_recv = reduce_all(g_all.reshape(60, SIDE, SIDE, SIDE, NB, 128), small, y_oth)
        out_full = jnp.where(cp == 0, jnp.concatenate([y_own, y_recv], axis=0), jnp.concatenate([y_recv, y_own], axis=0))
        s_flat = s_red.reshape(-1)
        n_tab = vocab * width
        d_embed = s_flat[:n_tab].reshape(vocab, width)
        d_v = lax.dynamic_slice(s_flat[n_tab:n_tab + 9 * width].reshape(9, width), (0, chip * NB), (9, NB))
        d_b = s_flat[n_tab + 9 * width:n_tab + 9 * width + 2560].reshape(4, chips, NB)
        d_b = lax.dynamic_slice(d_b, (0, chip, 0), (4, 1, NB)).reshape(-1)
        d_qkv = g_red[:15].transpose(1, 0, 2).reshape(w_qkv.shape)
        d_wout = g_red[15:20].transpose(1, 0, 2).reshape(w_out.shape)
        d_wup = g_red[20:40].transpose(0, 2, 1).reshape(4, chips, NB, rows).transpose(3, 1, 0, 2).reshape(w_up.shape)
        d_wdown = g_red[40:60].reshape(4, 5, NB, 128).transpose(0, 2, 1, 3).reshape(w_down.shape)
        return out_full, d_embed, d_v, d_qkv, d_wout, d_wup, d_b, d_wdown

    in_specs = (P('fsdp', 'cp'), P('fsdp'), P(), P(None, 'fsdp'), P('fsdp', None, None, None), P('fsdp', None), P('fsdp', None), P('fsdp'), P('fsdp', None), P('fsdp', 'cp', None))
    out_specs = (P('fsdp', 'cp', None), P(), P(None, 'fsdp'), P('fsdp', None, None, None), P('fsdp', None), P('fsdp', None), P('fsdp'), P('fsdp', None))
    return jax.shard_map(local_step, mesh=mesh, in_specs=in_specs, out_specs=out_specs, check_vma=False)
```

time: 2130 us -> 685 us (0.32)
  blocking collectives: 976 us -> 0 us
  waiting for transfers between devices: 546 us -> 0 us
  Pallas kernels: 0 us -> 126 us
  local copies, waits for them, and re-layouts: 54.4 us -> 167 us
  starting transfers between devices: 83.9 us -> 0 us
  matrix products: 323 us -> 247 us
    unnamed x2 -> x0, blocking collectives: 578 us -> none
    all_gather x2 -> x0, blocking collectives: 306 us -> none  [the longest x1 155 us: local_step(): vecs_all = lax.all_gather(layer_vecs, 'fsdp', axis=1, tiled=True)]
    reduce_scatter x1 -> x0, waiting for transfers between devices: 293 us -> none  [reduce_grad(): lax.psum_scatter(full_grad, 'fsdp', scatter_dimension=axis_dim, tiled=True)]
    unnamed x10 -> x0, waiting for transfers between devices: 253 us -> none
    pallas_call x0 -> x2, Pallas kernels: none -> 126 us  [the longest x1 64.4 us: reduce_all(): pl.pallas_call(reduce_kernel, out_shape=(jax.ShapeDtypeStruct((blocks, NB...]
    dot_general x26 -> x19, matrix products: 323 us -> 226 us  [the longest x1 24.4 us: layer_compute(): jnp.einsum('bqhd,bkhd->bhqk', d_attn_b, v_val, preferred_element_type=f32)]
    psum x2 -> x0, blocking collectives: 91.4 us -> none  [the longest x1 61.8 us: reduce_grad(): lax.psum(lax.psum_scatter(full_grad, 'fsdp', scatter_dimension=axis_dim,...]
    ppermute x6 -> x0, starting transfers between devices: 83.6 us -> none  [the longest x1 82.3 us: fwd_body(): lax.ppermute(v_blk, 'cp', send_pairs)]
  transfers between devices with their start and end apart: 14 -> 0, of which waited for: 2 -> 0; matrix products, arithmetic and copies ran while one was open for 20% -> 0% of each run, Pallas kernels for 0% -> 0%
where the time goes in v1:
time: 685 us; the launch traced here: 678 us
  matrix products  247 us (36%)
  local copies, waits for them, and re-layouts  167 us (24%)
  other arithmetic  136 us (20%)
  Pallas kernels  126 us (18%)
    pallas_call x1, Pallas kernels, reduce_all(): pl.pallas_call(reduce_kernel, out_shape=(jax.ShapeDtypeStruct((blocks, NB...  64.4 us
    pallas_call x1, Pallas kernels, gather_all(): pl.pallas_call(gather_kernel, out_shape=(jax.ShapeDtypeStruct((blocks, SI...  61.7 us
    convert_element_type x1, other arithmetic, layer_compute(): gelu_out = gelu32.astype(bf16)  51.1 us
    concatenate x4, local copies, waits for them, and re-layouts, layer_compute(): jnp.concatenate([d_qkvw.reshape(model_dim, 15, 128).transpose(1, 0, 2), d...  26.6 us
    dot_general x1, matrix products, layer_compute(): jnp.einsum('bqhd,bkhd->bhqk', d_attn_b, v_val, preferred_element_type=f32)  24.4 us
    dot_general x1, matrix products, layer_compute(): jnp.einsum('bsd,fd->bsf', grad_out, down_w, preferred_element_type=f32)  24.4 us
    convert_element_type x1, other arithmetic, layer_compute(): weights_b = weights.astype(bf16)  22.7 us
    sub x1, matrix products, layer_compute(): weights = jax.nn.softmax(scores, axis=-1)  21.6 us

profile of v1, /device:TPU:1, one launch (start us, length us, event | category | flops | bytes accessed | tf_op | source)
XLA Modules:
  0.0 678.5 jit_solution(10357153670924584402)
XLA Ops:
  14.1 61.7 %gather_weights.1 = (bf16[60,4,4,4,10,128]{5,4,3,2,1,0:T(8,128)(2,1)}, f32[4,4,4,8,128]{4,3,2,1,0:T(8,128)}, bf16[8,128,640]{2,1,0:T(8,128)(2,1)}, s32[8,128]{1,0:T(8,128)}) custom-call(bf16[60,10,128]{2,1,0:T(8,128)(2,1)} %pad_maximum_fusion.17.w_loc, f32[8,128]{1,0:T(8,128)} %fusion.62.s_loc, bf16[16,128,640]{2,1,0:T(8,128)(2,1)} %g_own.1, s32[16,128]{1,0:T(8,128)} %t_own.1), custom_call_target="tpu_custom_call" | custom-call | tf_op jit(solution)/shard_map/gather_weights/pallas_call | solution.py:161
  86.9 5.7 slice.103
  92.6 13.0 %fusion.76 = (bf16[20,4,4,4,10,128]{5,4,3,2,1,0:T(8,128)(2,1)}, bf16[20,4,4,4,10,128]{5,4,3,2,1,0:T(8,128)(2,1)}) fusion(bf16[60,4,4,4,10,128]{5,4,3,2,1,0:T(8,128)(2,1)} %get-tuple-element.17), kind=kLoop, calls=%fused_computation.166 | loop fusion | bytes 13107200 | tf_op jit(solution)/shard_map/slice | solution.py:404
  105.6 5.9 copy.51
  111.5 3.5 copy.52
  115.0 7.1 %reshape.454 = bf16[4,5,640,128]{3,2,1,0:T(8,128)(2,1)} reshape(bf16[20,4,4,4,10,128]{5,4,3,2,1,0:T(8,128)(2,1)} %get-tuple-element.40) | data formatting | bytes 6553600 | tf_op jit(solution)/shard_map/reshape | solution.py:404
  122.1 7.2 %copy.67 = bf16[4,640,5,128]{1,0,3,2:T(4,128)(2,1)S(1)} copy(bf16[4,640,5,128]{3,1,2,0:T(8,128)(2,1)} %bitcast.229) | data formatting | bytes 6553600 | tf_op jit(solution)/shard_map/transpose | solution.py:404
  131.5 9.4 %copy.62 = bf16[20,4,4,4,10,128]{5,0,4,3,2,1:T(8,128)(2,1)} copy(bf16[20,4,4,4,10,128]{5,4,3,2,1,0:T(8,128)(2,1)} %get-tuple-element.41) | data formatting | bytes 6553600 | tf_op jit(solution)/shard_map/slice | solution.py:403
  140.9 6.1 copy.63
  149.8 7.1 %convolution_add_fusion = f32[8,256,3,20,32]{1,4,3,2,0:T(8,128)S(1)} fusion(bf16[640,3,20,32,1]{0,3,2,1,4:T(8,128)(2,1)S(1)} %bitcast.245, f32[3,20,32]{2,1,0:T(8,128)S(1)} %add.144, f32[8,256,640]{2,1,0:T(8,128)S(1)} %get-tuple-element.72, f32[640]{0:T(1024)S(1)} %add.141, f32[640]{0:T(1024)S(1)} %mul.320, f32[8,256]{1,0:T(8,128)S(1)} %fusion.59, ...), kind=kOutput, calls=%fused_computation.34 | convolution fusion | flops 5044961280 | bytes 23466496 | tf_op jit(solution)/shard_map/bsd,dthe->bsthe/dot_general | solution.py:415
  158.2 4.4 subtract_convert_fusion.1
  163.7 21.6 %fusion.80 = (f32[8,20,256]{2,1,0:T(8,128)S(1)}, f32[8,20,256,256]{2,3,1,0:T(8,128)}) fusion(pred[8,256]{1,0:T(8,128)(4,1)S(1)} %broadcast_compare_fusion, bf16[8,256,20,16]{1,3,2,0:T(8,128)(2,1)S(1)} %get-tuple-element.63, bf16[8,256,20,16]{1,3,2,0:T(8,128)(2,1)} %get-tuple-element.64, bf16[8,256,20,16]{1,3,2,0:T(8,128)(2,1)} %get-tuple-element.48, ...), kind=kOutput, calls=%fused_computation.170 | convolution fusion | flops 713031936 | bytes 47351808 | tf_op jit(solution)/shard_map/sub | solution.py:422
  185.3 22.7 %fusion.12 = bf16[8,20,256,256]{2,3,1,0:T(8,128)(2,1)} fusion(f32[8,20,256,256]{2,3,1,0:T(8,128)} %get-tuple-element.74, f32[8,20,256]{2,1,0:T(8,128)S(1)} %get-tuple-element.73), kind=kLoop, calls=%fused_computation.30 | loop fusion | flops 20971520 | bytes 63078400 | tf_op jit(solution)/shard_map/convert_element_type | solution.py:423
  208.0 15.3 %bitcast_convert_fusion = (bf16[8,256,20,32]{1,3,2,0:T(8,128)(2,1)}, f32[8,20,32,256]{3,2,1,0:T(8,128)}) fusion(bf16[8,20,256,256]{2,3,1,0:T(8,128)(2,1)} %fusion.12, f32[8,256,3,20,32]{1,4,3,2,0:T(8,128)} %copy-done.10), kind=kOutput, calls=%fused_computation.52 | convolution fusion | flops 672399360 | bytes 31457280 | tf_op jit(solution)/shard_map/bhqk,bkhd->bqhd/dot_general | solution.py:424
  223.3 5.4 fusion.81
  232.5 20.4 %fusion.24 = (u8[256,2560]{1,0:T(8,128)(4,1)S(1)}, u8[256,2560]{1,0:T(8,128)(4,1)}, f32[8,256,2560]{2,1,0:T(8,128)}) fusion(f32[2560]{0:T(1024)S(1)} %add.157, bf16[640,2560,1]{0,1,2:T(8,128)(2,1)S(1)} %bitcast.237, f32[8,256,640]{2,1,0:T(8,128)} %copy-done.7, f32[640]{0:T(1024)S(1)} %add.154, f32[640]{0:T(1024)S(1)} %mul.341, f32[8,256]{1,0:T(8,128)S(1)} %fusion.60, ...), kind=kOutput, calls=%fused_computation.69 | convolution fusion | flops 6789529600 | bytes 30833664 | tf_op jit(solution)/shard_map/bsd,df->bsf/dot_general | solution.py:429
  252.9 51.1 %multiply_convert_fusion.1 = (bf16[8,256,2560]{2,1,0:T(8,128)(2,1)S(1)}, f32[8,256,2560]{2,1,0:T(8,128)}) fusion(f32[8,256,2560]{2,1,0:T(8,128)} %get-tuple-element.79, f32[2560]{0:T(1024)S(1)} %add.157, u8[256,2560]{1,0:T(8,128)(4,1)} %get-tuple-element.23, u8[256,2560]{1,0:T(8,128)(4,1)S(1)} %get-tuple-element.22), kind=kLoop, calls=%fused_computation.14 | loop fusion | flops 372244480 | bytes 53749760 | tf_op jit(solution)/shard_map/convert_element_type | solution.py:431
  304.0 24.4 %fusion.82 = (f32[2560]{0:T(1024)}, bf16[8,256,2560]{2,1,0:T(8,128)(2,1)}) fusion(f32[8,256,2560]{2,1,0:T(8,128)} %get-tuple-element.35, bf16[2560,640]{0,1:T(8,128)(2,1)} %bitcast.238, bf16[8,128,640]{2,1,0:T(8,128)(2,1)} %get-tuple-element.18, bf16[8,128,640]{2,1,0:T(8,128)(2,1)S(1)} %copy-done.17, f32[8,256,2560]{2,1,0:T(8,128)} %get-tuple-element.79, ...), kind=kOutput, calls=%fused_computation.172 | convolution fusion | flops 6800012800 | bytes 58347520 | tf_op jit(solution)/shard_map/bsd,fd->bsf/dot_general | solution.py:436
  328.4 12.0 %add_convert_fusion = bf16[8,256,640]{2,1,0:T(8,128)(2,1)} fusion(f32[8,256,640]{2,1,0:T(8,128)S(1)} %bitcast.224, f32[640]{0:T(1024)S(1)} %copy-done.56, bf16[8,256,2560]{2,1,0:T(8,128)(2,1)S(1)} %get-tuple-element.34, bf16[2560,640]{0,1:T(8,128)(2,1)} %bitcast.239), kind=kOutput, calls=%fused_computation.62 | convolution fusion | flops 6714818560 | bytes 21629440 | tf_op jit(solution)/shard_map/bsf,fd->bsd/dot_general | solution.py:432
  340.4 9.2 %convolution_bitcast_fusion = f32[2560,640]{0,1:T(8,128)} fusion(bf16[8,256,2560]{2,1,0:T(8,128)(2,1)S(1)} %get-tuple-element.34, bf16[8,128,640]{2,1,0:T(8,128)(2,1)S(1)} %copy-done.22, bf16[8,128,640]{2,1,0:T(8,128)(2,1)S(1)} %copy-done.17), kind=kOutput, calls=%fused_computation.39 | convolution fusion | flops 6716129280 | bytes 19660800 | tf_op jit(solution)/shard_map/bsf,bsd->fd/dot_general | solution.py:435
  349.6 8.3 %reshape.458 = f32[4,640,5,128]{1,0,3,2:T(4,128)} reshape(f32[2560,640]{0,1:T(8,128)} %convolution_bitcast_fusion) | data formatting | bytes 13107200 | tf_op jit(solution)/shard_map/reshape | solution.py:469
  357.9 9.3 %copy.86 = f32[4,5,640,128]{3,2,1,0:T(8,128)} copy(f32[4,5,640,128]{2,0,3,1:T(4,128)} %bitcast.220) | data formatting | bytes 13107200 | tf_op jit(solution)/shard_map/transpose | solution.py:469
  367.2 3.8 fusion.77
  371.0 13.4 %multiply_reduce_fusion = (f32[640]{0:T(1024)S(1)}, f32[8,256]{1,0:T(8,128)S(1)}, f32[640]{0:T(1024)S(1)}, f32[8,256,640]{2,1,0:T(8,128)S(1)}) fusion(f32[8,256,640]{2,1,0:T(8,128)} %copy-done.7, f32[8,256]{1,0:T(8,128)S(1)} %fusion.60, f32[8,256]{1,0:T(8,128)S(1)} %broadcast_multiply_fusion, f32[640]{0:T(1024)S(1)} %mul.341, ...), kind=kOutput, calls=%fused_computation.54 | convolution fusion | flops 6721369088 | bytes 24280576 | tf_op jit(solution)/shard_map/bsf,df->bsd/dot_general | solution.py:440
  384.4 13.8 %fusion.19 = f32[640,2560,1]{0,1,2:T(8,128)} fusion(bf16[8,256,2560]{2,1,0:T(8,128)(2,1)} %get-tuple-element.84, f32[8,256,640]{2,1,0:T(8,128)S(1)} %bitcast.226, f32[640]{0:T(1024)S(1)} %add.154, f32[640]{0:T(1024)S(1)} %mul.341, f32[8,256]{1,0:T(8,128)S(1)} %fusion.60, f32[8,256]{1,0:T(8,128)S(1)} %broadcast_multiply_fusion), kind=kOutput, calls=%fused_computation.58 | convolution fusion | flops 6717440000 | bytes 22303744 | tf_op jit(solution)/shard_map/bsd,bsf->df/dot_general | solution.py:439
  398.8 3.6 fusion.74
  403.0 8.6 %copy.83 = f32[20,640,128]{2,0,1:T(8,128)} copy(f32[20,640,128]{1,2,0:T(8,128)} %bitcast.233) | data formatting | bytes 13107200 | tf_op jit(solution)/shard_map/transpose | solution.py:468
  411.7 9.0 %copy.88 = f32[20,4,4,4,10,128]{5,4,3,2,1,0:T(8,128)} copy(f32[20,4,4,4,10,128]{5,0,4,3,2,1:T(8,128)} %bitcast.219) | data formatting | bytes 13107200 | tf_op jit(solution)/shard_map/concatenate | solution.py:465
  421.9 3.8 fusion.18
  425.7 12.5 %convolution_bitcast_fusion.1 = f32[8,256,1,20,32]{1,4,3,0,2:T(8,128)} fusion(bf16[8,20,256,256]{2,3,1,0:T(8,128)(2,1)} %fusion.12, bf16[8,256,20,32]{1,3,2,0:T(8,128)(2,1)} %get-tuple-element.82), kind=kOutput, calls=%fused_computation.97 | convolution fusion | flops 671088640 | bytes 28835840 | tf_op jit(solution)/shard_map/bhqk,bqhd->bkhd/dot_general | solution.py:452
  438.2 24.4 %multiply_convert_fusion = bf16[8,20,256,256]{2,3,1,0:T(8,128)(2,1)} fusion(f32[8,20,256]{2,1,0:T(8,128)S(1)} %bitcast.260, f32[8,20,256,256]{2,3,1,0:T(8,128)} %get-tuple-element.74, f32[8,20,256]{2,1,0:T(8,128)S(1)} %copy-done.29, bf16[8,256,20,32]{1,3,2,0:T(8,128)(2,1)} %get-tuple-element.82, f32[8,256,3,20,32]{1,4,3,2,0:T(8,128)} %copy-done.10), kind=kOutput, calls=%fused_computation.1 | convolution fusion | flops 713031680 | bytes 68485120 | tf_op jit(solution)/shard_map/bqhd,bkhd->bhqk/dot_general | solution.py:448
  463.8 3.5 copy.79
  467.3 4.8 fusion.41
  473.6 12.5 %convolution_bitcast_fusion.2 = f32[8,256,20,32]{1,3,2,0:T(8,128)} fusion(bf16[8,20,256,256]{2,3,1,0:T(8,128)(2,1)} %multiply_convert_fusion, bf16[8,256,20,16]{1,3,2,0:T(8,128)(2,1)} %get-tuple-element.48, bf16[8,256,20,16]{1,3,2,0:T(8,128)(2,1)} %get-tuple-element.47), kind=kOutput, calls=%fused_computation.98 | convolution fusion | flops 676331520 | bytes 28835840 | tf_op jit(solution)/shard_map/bhqk,bqhd->bkhd/dot_general | solution.py:451
  486.2 9.0 %convolution_bitcast_fusion.3 = f32[8,256,20,32]{1,3,2,0:T(8,128)S(1)} fusion(bf16[8,20,256,256]{2,3,1,0:T(8,128)(2,1)} %multiply_convert_fusion, bf16[8,256,20,16]{1,3,2,0:T(8,128)(2,1)S(1)} %copy-done.14, bf16[8,256,20,16]{1,3,2,0:T(8,128)(2,1)S(1)} %copy-done.15), kind=kOutput, calls=%fused_computation.99 | convolution fusion | flops 676331520 | bytes 28835840 | tf_op jit(solution)/shard_map/bhqk,bkhd->bqhd/dot_general | solution.py:450
  495.2 4.5 subtract_bitcast_fusion
  499.8 5.8 maximum_multiply_fusion
  505.6 8.6 %concatenate.86 = f32[20,4,4,4,10,128]{5,4,3,2,1,0:T(8,128)} reshape(f32[4,5,640,128]{3,2,1,0:T(8,128)} %copy.86) | data formatting | bytes 13107200 | tf_op jit(solution)/shard_map/concatenate | solution.py:465
  519.0 3.8 fusion.13
  522.9 14.6 %multiply_reduce_fusion.1 = (f32[8,256]{1,0:T(8,128)S(1)}, f32[8,256,640,1,1]{2,1,3,0,4:T(8,128)}) fusion(f32[8,256,640]{2,1,0:T(8,128)} %copy-done.2, f32[640]{0:T(1024)S(1)} %copy-done.48, f32[8,256]{1,0:T(8,128)S(1)} %copy-done.35, f32[8,256]{1,0:T(8,128)S(1)} %copy-done.33, bf16[640,3,20,32,1]{0,3,2,4,1:T(8,128)(2,1)} %bitcast.244, ...), kind=kOutput, calls=%fused_computation.56 | convolution fusion | flops 5047580672 | bytes 28699136 | tf_op jit(solution)/shard_map/bsthe,dthe->bsd/dot_general | solution.py:458
  537.6 14.7 %fusion.31 = f32[640,3,20,32,1]{0,3,2,4,1:T(8,128)} fusion(f32[8,256,640]{2,1,0:T(8,128)S(1)} %bitcast.216, f32[640]{0:T(1024)S(1)} %copy-done.55, f32[640]{0:T(1024)S(1)} %copy-done.48, f32[8,256]{1,0:T(8,128)S(1)} %copy-done.44, f32[8,256]{1,0:T(8,128)S(1)} %copy-done.35, f32[8,256]{1,0:T(8,128)S(1)} %copy-done.33, ...), kind=kOutput, calls=%fused_computation.77 | convolution fusion | flops 5064622080 | bytes 25916416 | tf_op jit(solution)/shard_map/bsd,bsthe->dthe/dot_general | solution.py:457
  552.4 5.9 fusion.53
  558.4 7.2 %fusion.48 = f32[33,640]{1,0:T(8,128)S(1)} fusion(f32[8,256]{1,0:T(8,128)S(1)} %negate_multiply_fusion.1, f32[8,256]{1,0:T(8,128)S(1)} %copy-done.33, f32[8,256,640]{2,1,0:T(8,128)} %get-tuple-element.33, f32[8,256]{1,0:T(8,128)S(1)} %copy-done.46, f32[8,256,640,1,1]{2,1,3,0,4:T(8,128)S(1)} %copy-done.16, f32[8,256,640]{2,1,0:T(8,128)S(1)} %bitcast.216, ...), kind=kOutput, calls=%fused_computation.105 | convolution fusion | flops 108857344 | bytes 18494464 | tf_op jit(solution)/shard_map/bsv,bsd->vd/dot_general | solution.py:461
  566.4 6.3 copy.78
  572.6 7.5 %copy.87 = f32[15,4,4,4,10,128]{5,4,3,2,1,0:T(8,128)} copy(f32[15,4,4,4,10,128]{5,0,4,3,2,1:T(8,128)} %bitcast.222) | data formatting | bytes 9830400 | tf_op jit(solution)/shard_map/concatenate | solution.py:465
  580.1 20.5 %pad_maximum_fusion.g_all = f32[60,4,4,4,10,128]{5,4,3,2,1,0:T(8,128)} fusion(f32[20,4,4,4,10,128]{5,4,3,2,1,0:T(8,128)} %concatenate.86, f32[20,4,4,4,10,128]{5,4,3,2,1,0:T(8,128)} %copy.88, f32[5,4,4,4,10,128]{5,4,3,2,1,0:T(8,128)S(1)} %copy-done.11, f32[15,4,4,4,10,128]{5,4,3,2,1,0:T(8,128)} %copy.87), kind=kLoop, calls=%fused_computation.5 | loop fusion | flops 14745600 | bytes 39321600 | tf_op jit(solution)/shard_map/concatenate | solution.py:465
  600.6 64.4 %reduce_grads.1 = (f32[60,10,128]{2,1,0:T(8,128)}, f32[2,120,128]{2,1,0:T(8,128)}, bf16[8,128,640]{2,1,0:T(8,128)(2,1)}) custom-call(f32[60,4,4,4,10,128]{5,4,3,2,1,0:T(8,128)} %pad_maximum_fusion.g_all, f32[2,120,128]{2,1,0:T(8,128)} %bitcast.249, bf16[8,128,640]{2,1,0:T(8,128)(2,1)} %get-tuple-element.52.y_oth), custom_call_target="tpu_custom_call" | custom-call | tf_op jit(solution)/shard_map/reduce_grads/pallas_call | solution.py:345
  665.0 3.1 maximum_select_fusion
  (244 shorter events, 56.3 us)
Async XLA Ops:
  0.6 146.4 %copy-start = (bf16[33,640]{1,0:T(8,128)(2,1)S(1)}, bf16[33,640]{1,0:T(8,128)(2,1)}, u32[]{:S(2)}) copy-start(bf16[33,640]{1,0:T(8,128)(2,1)} %param.12) | copy-start | bytes 126724
  0.6 76.9 %copy-start.57 = (s32[16]{0:T(128)S(1)}, s32[16]{0:T(128)}, u32[]{:S(2)}) copy-start(s32[16]{0:T(128)} %param.11) | copy-start | bytes 196
  6.1 152.0 %copy-start.30 = (f32[256,16]{0,1:T(8,128)}, f32[256,16]{0,1:T(8,128)S(1)}, u32[]{:S(2)}) copy-start(f32[256,16]{0,1:T(8,128)S(1)} %get-tuple-element.68) | copy-start | bytes 49156
  77.5 69.5 %copy-start.41 = (s32[8,256]{1,0:T(8,128)}, s32[8,256]{1,0:T(8,128)S(1)}, u32[]{:S(2)}) copy-start(s32[8,256]{1,0:T(8,128)S(1)} %get-tuple-element.65) | copy-start | bytes 24580
  77.8 145.5 %copy-start.32 = (f32[8,256]{1,0:T(8,128)}, f32[8,256]{1,0:T(8,128)S(1)}, u32[]{:S(2)}) copy-start(f32[8,256]{1,0:T(8,128)S(1)} %or_select_fusion) | copy-start | bytes 24580
  79.9 69.9 %copy-start.54 = (f32[640]{0:T(1024)}, f32[640]{0:T(1024)S(1)}, u32[]{:S(2)}) copy-start(f32[640]{0:T(1024)S(1)} %add.141) | copy-start | bytes 7684
  80.1 69.7 %copy-start.47 = (f32[640]{0:T(1024)}, f32[640]{0:T(1024)S(1)}, u32[]{:S(2)}) copy-start(f32[640]{0:T(1024)S(1)} %mul.320) | copy-start | bytes 7684
  148.2 8.8 %copy-start.2 = (f32[8,256,640]{2,1,0:T(8,128)}, f32[8,256,640]{2,1,0:T(8,128)S(1)}, u32[]{:S(2)}) copy-start(f32[8,256,640]{2,1,0:T(8,128)S(1)} %get-tuple-element.72) | copy-start | bytes 15728644
  148.2 8.7 %copy-start.34 = (f32[8,256]{1,0:T(8,128)}, f32[8,256]{1,0:T(8,128)S(1)}, u32[]{:S(2)}) copy-start(f32[8,256]{1,0:T(8,128)S(1)} %broadcast_multiply_fusion.1) | copy-start | bytes 24580
  163.7 21.6 %copy-start.13 = (bf16[8,256,20,16]{1,3,2,0:T(8,128)(2,1)}, bf16[8,256,20,16]{1,3,2,0:T(8,128)(2,1)S(1)}, u32[]{:S(2)}) copy-start(bf16[8,256,20,16]{1,3,2,0:T(8,128)(2,1)S(1)} %get-tuple-element.63) | copy-start | bytes 3932164
  163.7 59.5 %slice-start = ((s8[5242880]{0:T(1024)(128)(4,1)}), s8[1048576]{0:T(1024)(128)(4,1)S(1)}, s32[]{:S(2)}) async-start(s8[5242880]{0:T(1024)(128)(4,1)} %bitcast.213), calls=%async_computation | async-start | bytes 2097152
  185.3 22.7 %copy-start.28 = (f32[8,20,256]{2,1,0:T(8,128)}, f32[8,20,256]{2,1,0:T(8,128)S(1)}, u32[]{:S(2)}) copy-start(f32[8,20,256]{2,1,0:T(8,128)S(1)} %get-tuple-element.73) | copy-start | bytes 491524
  185.3 38.0 %slice-start.1 = ((s8[5242880]{0:T(1024)(128)(4,1)}), s8[4194304]{0:T(1024)(128)(4,1)S(1)}, s32[]{:S(2)}) async-start(s8[5242880]{0:T(1024)(128)(4,1)} %bitcast.213), calls=%async_computation.1 | async-start | bytes 8388608
  208.0 15.3 %copy-start.25 = (bf16[640,5,128]{0,2,1:T(8,128)(2,1)S(1)}, bf16[640,5,128]{0,2,1:T(8,128)(2,1)}, u32[]{:S(2)}) copy-start(bf16[640,5,128]{0,2,1:T(8,128)(2,1)} %copy.56) | copy-start | bytes 2457604
  232.1 20.8 %copy-start.38 = (f32[8,256]{1,0:T(8,128)}, f32[8,256]{1,0:T(8,128)S(1)}, u32[]{:S(2)}) copy-start(f32[8,256]{1,0:T(8,128)S(1)} %multiply_reduce_fusion.3) | copy-start | bytes 24580
  252.9 51.1 %copy-start.17 = (bf16[8,128,640]{2,1,0:T(8,128)(2,1)S(1)}, bf16[8,128,640]{2,1,0:T(8,128)(2,1)}, u32[]{:S(2)}) copy-start(bf16[8,128,640]{2,1,0:T(8,128)(2,1)} %constant_dynamic-slice_fusion.1) | copy-start | bytes 3932164
  252.9 75.5 %slice-start.6 = ((s8[5242880]{0:T(1024)(128)(4,1)}), s8[4194304]{0:T(1024)(128)(4,1)S(1)}, s32[]{:S(2)}) async-start(s8[5242880]{0:T(1024)(128)(4,1)} %bitcast.223), calls=%async_computation.6 | async-start | bytes 8388608
  304.0 24.4 %slice-start.7 = ((s8[5242880]{0:T(1024)(128)(4,1)}), s8[1048576]{0:T(1024)(128)(4,1)S(1)}, s32[]{:S(2)}) async-start(s8[5242880]{0:T(1024)(128)(4,1)} %bitcast.223), calls=%async_computation.7 | async-start | bytes 2097152
  304.0 24.4 %copy-start.56 = (f32[640]{0:T(1024)S(1)}, f32[640]{0:T(1024)}, u32[]{:S(2)}) copy-start(f32[640]{0:T(1024)} %add.161) | copy-start | bytes 7684
  328.4 12.0 %copy-start.22 = (bf16[8,128,640]{2,1,0:T(8,128)(2,1)S(1)}, bf16[8,128,640]{2,1,0:T(8,128)(2,1)}, u32[]{:S(2)}) copy-start(bf16[8,128,640]{2,1,0:T(8,128)(2,1)} %get-tuple-element.18) | copy-start | bytes 3932164
  367.2 17.2 %slice-start.8 = ((s8[5242880]{0:T(1024)(128)(4,1)}), s8[4194304]{0:T(1024)(128)(4,1)S(1)}, s32[]{:S(2)}) async-start(s8[5242880]{0:T(1024)(128)(4,1)} %bitcast.225), calls=%async_computation.8 | async-start | bytes 8388608
  371.0 13.4 %slice-start.9 = ((s8[5242880]{0:T(1024)(128)(4,1)}), s8[1048576]{0:T(1024)(128)(4,1)S(1)}, s32[]{:S(2)}) async-start(s8[5242880]{0:T(1024)(128)(4,1)} %bitcast.225), calls=%async_computation.9 | async-start | bytes 2097152
  384.4 14.4 %copy-start.39 = (f32[8,256]{1,0:T(8,128)S(1)}, f32[8,256]{1,0:T(8,128)}, u32[]{:S(2)}) copy-start(f32[8,256]{1,0:T(8,128)} %copy-done.38) | copy-start | bytes 24580
  402.4 18.2 %copy-start.45 = (f32[8,256]{1,0:T(8,128)}, f32[8,256]{1,0:T(8,128)S(1)}, u32[]{:S(2)}) copy-start(f32[8,256]{1,0:T(8,128)S(1)} %negate_multiply_fusion.2) | copy-start | bytes 24580
  403.0 18.8 %slice-start.4 = ((s8[5242880]{0:T(1024)(128)(4,1)}), s8[1048576]{0:T(1024)(128)(4,1)S(1)}, s32[]{:S(2)}) async-start(s8[5242880]{0:T(1024)(128)(4,1)} %bitcast.217), calls=%async_computation.4 | async-start | bytes 2097152
  411.7 9.0 %copy-start.6 = (f32[8,256,640]{2,1,0:T(8,128)S(1)}, f32[8,256,640]{2,1,0:T(8,128)}, u32[]{:S(2)}) copy-start(f32[8,256,640]{2,1,0:T(8,128)} %get-tuple-element.33) | copy-start | bytes 15728644
  411.7 9.0 %copy-start.23 = (bf16[8,128,640]{2,1,0:T(8,128)(2,1)S(1)}, bf16[8,128,640]{2,1,0:T(8,128)(2,1)}, u32[]{:S(2)}) copy-start(bf16[8,128,640]{2,1,0:T(8,128)(2,1)} %get-tuple-element.18) | copy-start | bytes 3932164
  411.7 10.2 %slice-start.5 = ((s8[5242880]{0:T(1024)(128)(4,1)}), s8[4194304]{0:T(1024)(128)(4,1)S(1)}, s32[]{:S(2)}) async-start(s8[5242880]{0:T(1024)(128)(4,1)} %bitcast.217), calls=%async_computation.5 | async-start | bytes 8388608
  425.7 12.5 %copy-start.29 = (f32[8,20,256]{2,1,0:T(8,128)S(1)}, f32[8,20,256]{2,1,0:T(8,128)}, u32[]{:S(2)}) copy-start(f32[8,20,256]{2,1,0:T(8,128)} %copy-done.28) | copy-start | bytes 491524
  438.2 25.6 %copy-start.5 = (bf16[8,256,640]{2,1,0:T(8,128)(2,1)S(1)}, bf16[8,256,640]{2,1,0:T(8,128)(2,1)}, u32[]{:S(2)}) copy-start(bf16[8,256,640]{2,1,0:T(8,128)(2,1)} %copy-done.4) | copy-start | bytes 7864324
  473.6 12.5 %copy-start.14 = (bf16[8,256,20,16]{1,3,2,0:T(8,128)(2,1)S(1)}, bf16[8,256,20,16]{1,3,2,0:T(8,128)(2,1)}, u32[]{:S(2)}) copy-start(bf16[8,256,20,16]{1,3,2,0:T(8,128)(2,1)} %copy-done.13) | copy-start | bytes 3932164
  473.6 12.5 %copy-start.15 = (bf16[8,256,20,16]{1,3,2,0:T(8,128)(2,1)S(1)}, bf16[8,256,20,16]{1,3,2,0:T(8,128)(2,1)}, u32[]{:S(2)}) copy-start(bf16[8,256,20,16]{1,3,2,0:T(8,128)(2,1)} %get-tuple-element.64) | copy-start | bytes 3932164
  486.2 9.1 %copy-start.3 = (f32[8,256,20,32]{1,3,2,0:T(8,128)S(1)}, f32[8,256,20,32]{1,3,2,0:T(8,128)}, u32[]{:S(2)}) copy-start(f32[8,256,20,32]{1,3,2,0:T(8,128)} %convolution_bitcast_fusion.2) | copy-start | bytes 15728644
  486.2 9.1 %copy-start.31 = (f32[256,16]{0,1:T(8,128)S(1)}, f32[256,16]{0,1:T(8,128)}, u32[]{:S(2)}) copy-start(f32[256,16]{0,1:T(8,128)} %copy-done.30) | copy-start | bytes 49156
  486.2 9.1 %copy-start.40 = (f32[256,16]{0,1:T(8,128)S(1)}, f32[256,16]{0,1:T(8,128)}, u32[]{:S(2)}) copy-start(f32[256,16]{0,1:T(8,128)} %get-tuple-element.66) | copy-start | bytes 49156
  519.0 18.5 %slice-start.2 = ((s8[5242880]{0:T(1024)(128)(4,1)}), s8[1048576]{0:T(1024)(128)(4,1)S(1)}, s32[]{:S(2)}) async-start(s8[5242880]{0:T(1024)(128)(4,1)} %bitcast.215), calls=%async_computation.2 | async-start | bytes 2097152
  522.9 14.7 %slice-start.3 = ((s8[5242880]{0:T(1024)(128)(4,1)}), s8[4194304]{0:T(1024)(128)(4,1)S(1)}, s32[]{:S(2)}) async-start(s8[5242880]{0:T(1024)(128)(4,1)} %bitcast.215), calls=%async_computation.3 | async-start | bytes 8388608
  522.9 14.7 %copy-start.44 = (f32[8,256]{1,0:T(8,128)S(1)}, f32[8,256]{1,0:T(8,128)}, u32[]{:S(2)}) copy-start(f32[8,256]{1,0:T(8,128)} %copy-done.43) | copy-start | bytes 24580
  522.9 14.7 %copy-start.55 = (f32[640]{0:T(1024)S(1)}, f32[640]{0:T(1024)}, u32[]{:S(2)}) copy-start(f32[640]{0:T(1024)} %copy-done.54) | copy-start | bytes 7684
  537.6 14.7 %copy-start.37 = (f32[8,256]{1,0:T(8,128)S(1)}, f32[8,256]{1,0:T(8,128)}, u32[]{:S(2)}) copy-start(f32[8,256]{1,0:T(8,128)} %copy-done.36) | copy-start | bytes 24580
  558.3 7.3 %copy-start.50 = (f32[1,640]{1,0:T(1,128)S(1)}, f32[1,640]{1,0:T(1,128)}, u32[]{:S(2)}) copy-start(f32[1,640]{1,0:T(1,128)} %stack.34) | copy-start | bytes 7684
  558.3 7.3 %copy-start.51 = (f32[1,640]{1,0:T(1,128)S(1)}, f32[1,640]{1,0:T(1,128)}, u32[]{:S(2)}) copy-start(f32[1,640]{1,0:T(1,128)} %stack.35) | copy-start | bytes 7684
  558.3 7.3 %copy-start.52 = (f32[1,640]{1,0:T(1,128)S(1)}, f32[1,640]{1,0:T(1,128)}, u32[]{:S(2)}) copy-start(f32[1,640]{1,0:T(1,128)} %stack.36) | copy-start | bytes 7684
  558.3 7.3 %copy-start.53 = (f32[1,640]{1,0:T(1,128)S(1)}, f32[1,640]{1,0:T(1,128)}, u32[]{:S(2)}) copy-start(f32[1,640]{1,0:T(1,128)} %stack.33) | copy-start | bytes 7684
  558.4 7.3 %copy-start.49 = (f32[2560]{0:T(1024)S(1)}, f32[2560]{0:T(1024)}, u32[]{:S(2)}) copy-start(f32[2560]{0:T(1024)} %get-tuple-element.83) | copy-start | bytes 30724
  572.6 7.5 %copy-start.11 = (f32[5,4,4,4,10,128]{5,4,3,2,1,0:T(8,128)S(1)}, f32[5,4,4,4,10,128]{5,4,3,2,1,0:T(8,128)}, u32[]{:S(2)}) copy-start(f32[5,4,4,4,10,128]{5,4,3,2,1,0:T(8,128)} %concatenate.84) | copy-start | bytes 4915204
  600.6 64.4 %copy-start.19 = (bf16[8,128,640]{2,1,0:T(8,128)(2,1)S(1)}, bf16[8,128,640]{2,1,0:T(8,128)(2,1)}, u32[]{:S(2)}) copy-start(bf16[8,128,640]{2,1,0:T(8,128)(2,1)} %get-tuple-element.51) | copy-start | bytes 3932164
  668.8 9.4 %copy-start.1 = (bf16[33,640]{1,0:T(8,128)(2,1)S(1)}, bf16[33,640]{1,0:T(8,128)(2,1)}, u32[]{:S(2)}) copy-start(bf16[33,640]{1,0:T(8,128)(2,1)} %param.12) | copy-start | bytes 126724
  (20 other events, 91.0 us)

commit v2 on v1

--- a/solution.py
+++ b/solution.py
@@ -370,105 +370,367 @@
     )(g_all, small, y_oth)
 
 
-def layer_norm(z_in, ln_gain, ln_bias):
-    row_mean = jnp.mean(z_in, axis=-1, keepdims=True)
-    centered = z_in - row_mean
-    row_var = jnp.mean(centered * centered, axis=-1, keepdims=True)
-    return centered * lax.rsqrt(row_var + LN_EPS) * ln_gain + ln_bias
-
-
-def gelu_exact(z_in):
-    return jax.nn.gelu(z_in, approximate=False)
-
-
-def rope_tables(positions, head_dim):
-    inv_freq = 1.0 / (ROPE_BASE ** (jnp.arange(0, head_dim, 2, dtype=jnp.float32) / head_dim))
-    angles = positions.astype(jnp.float32)[:, None] * inv_freq[None, :]
-    return jnp.cos(angles)[:, None, :], jnp.sin(angles)[:, None, :]
-
-
-def rotate(z_in, cos_t, sin_t):
-    lower_half, upper_half = jnp.split(z_in, 2, axis=-1)
-    return jnp.concatenate([lower_half * cos_t - upper_half * sin_t, upper_half * cos_t + lower_half * sin_t], axis=-1)
-
-
-def layer_compute(tokens, lengths, positions, embed_table, vecs_all, w_all, up_b, grad_out):
-    f32, bf16 = jnp.float32, jnp.bfloat16
+SEQS = 8
+STEP_SEQS = 2
+STEPS = SEQS // STEP_SEQS
+SEQ = 256
+TOK = STEP_SEQS * SEQ
+TILES = 5
+HEADS_PER = 4
+HEAD = 32
+LANES = 128
+F32 = jnp.float32
+BF16 = jnp.bfloat16
+
+
+def mm(lhs, rhs):
+    return lax.dot_general(lhs, rhs, (((1,), (0,)), ((), ())), preferred_element_type=F32)
+
+
+def mm_t(lhs, rhs):
+    return lax.dot_general(lhs, rhs, (((1,), (1,)), ((), ())), preferred_element_type=F32)
+
+
+def fold8(value):
+    return jnp.sum(value.reshape(value.shape[0] // 8, 8, value.shape[1]), axis=0)
+
+
+def wide(ref, first, count):
+    return jnp.concatenate([ref[first + j] for j in range(count)], axis=1)
+
+
+def add_blocks(ref, first, value):
+    for j in range(value.shape[1] // LANES):
+        ref[first + j] += value[:, j * LANES:(j + 1) * LANES]
+
+
+def norm_stats(value):
+    mean = jnp.mean(value, axis=-1, keepdims=True)
+    cent = value - mean
+    var = jnp.mean(cent * cent, axis=-1, keepdims=True)
+    rstd = lax.rsqrt(var + LN_EPS)
+    return cent * rstd, rstd
+
+
+def norm_back(d_out, gain, xhat, rstd):
+    d_hat = d_out * gain
+    m1 = jnp.mean(d_hat, axis=-1, keepdims=True)
+    m2 = jnp.mean(d_hat * xhat, axis=-1, keepdims=True)
+    return rstd * (d_hat - m1 - xhat * m2)
+
+
+def gelu_pair(u):
+    z = u * (0.5 ** 0.5)
+    t = 1.0 / (1.0 + 0.3275911 * jnp.abs(z))
+    poly = t * (0.127414796 + t * (-0.142248368 + t * (0.710706871 + t * (-0.7265760135 + t * 0.5307027145))))
+    ex = jnp.exp(-z * z)
+    tail = poly * ex
+    cdf = jnp.where(u >= 0, 1.0 - tail, tail)
+    return u * cdf, cdf + u * (ex * 0.3989422804014327)
+
+
+def unturn(z, cos, sin, groups):
+    parts = z.reshape(groups, 2, HEAD // 2, z.shape[1])
+    lo, up = parts[:, 0], parts[:, 1]
+    out = jnp.stack([lo * cos + up * sin, up * cos - lo * sin], axis=1)
+    return out.reshape(z.shape)
+
+
+def turn(z, cos, sin, groups):
+    return unturn(z, cos, -sin, groups)
+
+
+def layer_kernel(tok_ref, keep_ref, mask_ref, emb_ref, vec_ref, bqkv_ref, bup_ref, cos_ref, sin_ref, cosn_ref, sinn_ref,
+                 w_hbm, g_own, g_oth,
+                 y_own, y_oth, grads, dtab, dsum, dbq, dbkv, dbup,
+                 w, wt, acc, gbuf, e_s, ht, qt, kt, vt, qn, kn, vn, pt, ot32, otb, x1, nm, nmt, y_s, dnm, dot_s, dqkv,
+                 wsem, gsem, osem):
+    step = pl.program_id(0)
+    cp = lax.axis_index('cp')
+    chips = SIDE ** 3
+
+    @pl.when(step == 0)
+    def _():
+        own = pltpu.make_async_copy(g_own.at[pl.ds(cp * SEQS, SEQS)], gbuf.at[:, 0], gsem.at[0])
+        oth = pltpu.make_async_copy(g_oth, gbuf.at[:, 1], gsem.at[1])
+
+        @pl.loop(0, chips)
+        def _(i):
+            pltpu.make_async_copy(w_hbm.at[:, i], w.at[:, pl.ds(i * NB, NB), :], wsem).start()
+
+        own.start()
+        oth.start()
+
+        @pl.loop(0, 60)
+        def _(i):
+            acc[i] = jnp.zeros((640, LANES), F32)
+
+        dtab[...] = jnp.zeros_like(dtab)
+        dsum[...] = jnp.zeros_like(dsum)
+        dbq[...] = jnp.zeros_like(dbq)
+        dbkv[...] = jnp.zeros_like(dbkv)
+        dbup[...] = jnp.zeros_like(dbup)
+
+        @pl.loop(0, chips)
+        def _(i):
+            pltpu.make_async_copy(w_hbm.at[:, i], w.at[:, pl.ds(i * NB, NB), :], wsem).wait()
+
+        own.wait()
+        oth.wait()
+
+        @pl.loop(0, 15)
+        def _(n):
+            wt[n] = w[n].T
+
+    def grad_rows():
+        return gbuf[pl.ds(step * STEP_SEQS, STEP_SEQS)].reshape(TOK, 640)
+
+    vocab = lax.broadcasted_iota(jnp.int32, (64, TOK), 0)
+    one_hot = jnp.where(vocab == tok_ref[0], 1.0, 0.0).astype(BF16)
+    e_s[...] = lax.dot_general(one_hot, emb_ref[...], (((0,), (0,)), ((), ())), preferred_element_type=F32)
+
+    @pl.loop(0, TOK // 128)
+    def _(r):
+        rows = pl.ds(pl.multiple_of(r * 128, 128), 128)
+        keep = jnp.concatenate([keep_ref[rows]] * TILES, axis=1)
+        emb = e_s[rows] * keep
+        e_s[rows] = emb
+        xhat, _ = norm_stats(emb)
+        nm[rows] = (xhat * vec_ref[0:1] + vec_ref[1:2]).astype(BF16)
+
+    ht[...] = nm[...].T
+
+    cos, sin = cos_ref[...], sin_ref[...]
+    for kind, (t_ref, n_ref) in enumerate(((qt, qn), (kt, kn), (vt, vn))):
+        z = mm(wt[kind * TILES:(kind + 1) * TILES].reshape(640, 640), ht[...])
+        bias = bqkv_ref[kind * 640:(kind + 1) * 640]
+        z = z + jnp.concatenate([bias] * (TOK // LANES), axis=1)
+        if kind == 0:
+            z = z * HEAD ** -0.5
+        if kind < 2:
+            z = turn(z, cos, sin, 20)
+        zb = z.astype(BF16)
+        for s in range(STEP_SEQS):
+            for t in range(TILES):
+                piece = zb[t * LANES:(t + 1) * LANES, s * SEQ:(s + 1) * SEQ]
+                t_ref[s, t] = piece
+                n_ref[s, t] = piece.T
+
+    lane_head = lax.broadcasted_iota(jnp.int32, (1, LANES), 1) // HEAD
+    pick = [jnp.where(lane_head == h, 1.0, 0.0).astype(BF16) for h in range(HEADS_PER)]
+
+    @pl.loop(0, STEP_SEQS)
+    def _(s):
+        rows = pl.ds(pl.multiple_of(s * SEQ, SEQ), SEQ)
+
+        @pl.loop(0, TILES)
+        def _(t):
+            bias = mask_ref[rows]
+            bias = jnp.concatenate([bias, bias], axis=1)
+            q_t, k_n, v_t = qt[s, t], kn[s, t], vt[s, t]
+            outs = []
+            for h in range(HEADS_PER):
+                score = mm(k_n * pick[h], q_t) + bias
+                top = jnp.max(score, axis=0, keepdims=True)
+                p = jnp.exp(score - top)
+                p = p * (1.0 / jnp.sum(p, axis=0, keepdims=True))
+                pb = p.astype(BF16)
+                pt[s, t * HEADS_PER + h] = pb
+                outs.append(mm(v_t[h * HEAD:(h + 1) * HEAD], pb))
+            out = jnp.concatenate(outs, axis=0)
+            ot32[s, t] = out
+            outb = out.astype(BF16)
+            otb[t, :, rows] = outb
+            dqkv[t, rows] = outb.T
+
+    w_out = wide(w, 15, TILES)
+    x1[...] = e_s[...] + mm(wide(dqkv, 0, TILES), w_out) + vec_ref[5:6]
+
+    @pl.loop(0, TOK // 128)
+    def _(r):
+        rows = pl.ds(pl.multiple_of(r * 128, 128), 128)
+        xhat, _ = norm_stats(x1[rows])
+        nm[rows] = (xhat * vec_ref[6:7] + vec_ref[7:8]).astype(BF16)
+
+    nmt[...] = nm[...].T
+    y_s[...] = jnp.zeros_like(y_s)
+    dnm[...] = jnp.zeros_like(dnm)
+
+    @pl.loop(0, 4)
+    def _(c):
+        g = grad_rows()
+        w_up = wide(w, 20 + TILES * c, TILES)
+        u = mm(nm[...], w_up) + bup_ref[c]
+        a, slope = gelu_pair(u)
+        ab = a.astype(BF16)
+        w_down = wide(w, 40 + TILES * c, TILES)
+        du = mm_t(g, w_down) * slope
+        dbup[c] += fold8(du)
+        dub = du.astype(BF16)
+        y_s[...] += mm(ab, w_down)
+        dnm[...] += mm_t(dub, w_up)
+        add_blocks(acc, 40 + TILES * c, mm(ab.T, g))
+        add_blocks(acc, 20 + TILES * c, mm(nmt[...], dub))
+
+    @pl.loop(0, TOK // 128)
+    def _(r):
+        rows = pl.ds(pl.multiple_of(r * 128, 128), 128)
+        x = x1[rows]
+        out = (x + y_s[rows] + vec_ref[8:9]).astype(BF16)
+        seq = r // 2
+
+        @pl.when(lax.rem(r, 2) == 0)
+        def _():
+            y_own[seq] = out
+
+        @pl.when(lax.rem(r, 2) == 1)
+        def _():
+            y_oth[seq] = out
+
+        xhat, rstd = norm_stats(x)
+        d_n = dnm[rows]
+        g32 = gbuf[step * STEP_SEQS + seq, lax.rem(r, 2)].astype(F32)
+        dsum[3] += fold8(d_n * xhat)
+        dsum[4] += fold8(d_n)
+        d_r = g32 + norm_back(d_n, vec_ref[6:7], xhat, rstd)
+        dsum[2] += fold8(d_r)
+        dsum[5] += fold8(g32)
+        y_s[rows] = d_r
+        nm[rows] = d_r.astype(BF16)
+
+    d_rb = nm[...]
+    add_blocks(acc, 15, mm(otb[...].reshape(640, TOK), d_rb))
+    d_o = mm(wide(w, 15, TILES), d_rb.T)
+    for t in range(TILES):
+        dot_s[t] = d_o[t * LANES:(t + 1) * LANES]
+
+    @pl.loop(0, STEP_SEQS)
+    def _(s):
+        rows = pl.ds(pl.multiple_of(s * SEQ, SEQ), SEQ)
+
+        @pl.loop(0, TILES)
+        def _(t):
+            d_ot = dot_s[t, :, rows]
+            d_otb = d_ot.astype(BF16)
+            d_on = d_otb.T
+            prod = d_ot * ot32[s, t]
+            k_t, v_n, q_n = kt[s, t], vn[s, t], qn[s, t]
+            dqs = []
+            dk, dv = None, None
+            for h in range(HEADS_PER):
+                lanes = slice(h * HEAD, (h + 1) * HEAD)
+                pb = pt[s, t * HEADS_PER + h]
+                delta = jnp.sum(prod[lanes], axis=0, keepdims=True)
+                d_p = mm(v_n * pick[h], d_otb)
+                d_sb = (pb.astype(F32) * (d_p - delta)).astype(BF16)
+                dqs.append(mm(k_t[lanes], d_sb))
+                dk_h = mm(d_sb, q_n * pick[h])
+                dv_h = mm(pb, d_on * pick[h])
+                dk = dk_h if dk is None else dk + dk_h
+                dv = dv_h if dv is None else dv + dv_h
+            dq = unturn(jnp.concatenate(dqs, axis=0), cos[:, :SEQ], sin[:, :SEQ], HEADS_PER) * HEAD ** -0.5
+            dbq[t] += dq[:, :LANES] + dq[:, LANES:]
+            dqkv[t, rows] = dq.astype(BF16).T
+            low = lax.rem(lax.broadcasted_iota(jnp.int32, (SEQ, LANES), 1), HEAD) < HEAD // 2
+            other = jnp.where(low, pltpu.roll(dk, LANES - HEAD // 2, 1), pltpu.roll(dk, HEAD // 2, 1))
+            dk = dk * cosn_ref[...] + other * sinn_ref[...]
+            dbkv[0, t] += fold8(dk)
+            dbkv[1, t] += fold8(dv)
+            dqkv[TILES + t, rows] = dk.astype(BF16)
+            dqkv[2 * TILES + t, rows] = dv.astype(BF16)
+
+    for kind in range(3):
+        add_blocks(acc, kind * TILES, mm(ht[...], wide(dqkv, kind * TILES, TILES)))
+    dnm[...] = mm(wide(dqkv, 0, 15), wt[...].reshape(1920, 640))
+
+    @pl.loop(0, TOK // 128)
+    def _(r):
+        rows = pl.ds(pl.multiple_of(r * 128, 128), 128)
+        xhat, rstd = norm_stats(e_s[rows])
+        d_n = dnm[rows]
+        dsum[0] += fold8(d_n * xhat)
+        dsum[1] += fold8(d_n)
+        keep = jnp.concatenate([keep_ref[rows]] * TILES, axis=1)
+        nm[rows] = ((norm_back(d_n, vec_ref[0:1], xhat, rstd) + y_s[rows]) * keep).astype(BF16)
+
+    dtab[...] += mm(one_hot, nm[...])
+
+    @pl.when(step == STEPS - 1)
+    def _():
+        @pl.loop(0, chips)
+        def _(i):
+            pltpu.make_async_copy(acc.at[:, pl.ds(i * NB, NB), :], grads.at[:, i], osem).start()
+
+        @pl.loop(0, chips)
+        def _(i):
+            pltpu.make_async_copy(acc.at[:, pl.ds(i * NB, NB), :], grads.at[:, i], osem).wait()
+
+
+def layer_call(tok, keep, mask, emb, vecs, bqkv, bup, cos, sin, cosn, sinn, w_hbm, g_own, g_oth):
+    vm = pltpu.VMEM
+    dma = pltpu.SemaphoreType.DMA
+
+    def whole(shape):
+        return pl.BlockSpec(shape, lambda i: (0,) * len(shape))
+
+    pair = pl.BlockSpec((STEP_SEQS, 128, 640), lambda i: (i, 0, 0))
+    out_shape = (
+        jax.ShapeDtypeStruct((SEQS, 128, 640), BF16),
+        jax.ShapeDtypeStruct((SEQS, 128, 640), BF16),
+        jax.ShapeDtypeStruct((60, 64, NB, LANES), F32),
+        jax.ShapeDtypeStruct((64, 640), F32),
+        jax.ShapeDtypeStruct((6, 8, 640), F32),
+        jax.ShapeDtypeStruct((TILES, LANES, LANES), F32),
+        jax.ShapeDtypeStruct((2, TILES, 8, LANES), F32),
+        jax.ShapeDtypeStruct((4, 8, 640), F32),
+    )
+    out_specs = (pair, pair, ANY) + tuple(whole(o.shape) for o in out_shape[3:])
+    in_specs = [
+        pl.BlockSpec((1, 1, TOK), lambda i: (i, 0, 0)),
+        pl.BlockSpec((TOK, LANES), lambda i: (i, 0)),
+        pl.BlockSpec((TOK, LANES), lambda i: (i, 0)),
+    ] + [whole(a.shape) for a in (emb, vecs, bqkv, bup, cos, sin, cosn, sinn)] + [ANY] * 3
+    halves = (STEP_SEQS, TILES, LANES, SEQ)
+    flipped = (STEP_SEQS, TILES, SEQ, LANES)
+    scratch = [
+        vm((60, 640, LANES), BF16), vm((15, LANES, 640), BF16), vm((60, 640, LANES), F32), vm((SEQS, 2, 128, 640), BF16),
+        vm((TOK, 640), F32), vm((640, TOK), BF16),
+        vm(halves, BF16), vm(halves, BF16), vm(halves, BF16), vm(flipped, BF16), vm(flipped, BF16), vm(flipped, BF16),
+        vm((STEP_SEQS, 20, SEQ, SEQ), BF16), vm(halves, F32), vm((TILES, LANES, TOK), BF16),
+        vm((TOK, 640), F32), vm((TOK, 640), BF16), vm((640, TOK), BF16), vm((TOK, 640), F32), vm((TOK, 640), F32),
+        vm((TILES, LANES, TOK), F32), vm((15, TOK, LANES), BF16),
+        dma, dma((2,)), dma,
+    ]
+    return pl.pallas_call(
+        layer_kernel,
+        grid=(STEPS,),
+        out_shape=out_shape,
+        in_specs=in_specs,
+        out_specs=out_specs,
+        scratch_shapes=scratch,
+        compiler_params=pltpu.CompilerParams(dimension_semantics=('arbitrary',), vmem_limit_bytes=67043328),
+        name='layer',
+    )(tok, keep, mask, emb, vecs, bqkv, bup, cos, sin, cosn, sinn, w_hbm, g_own, g_oth)
+
+
+def prepare(tokens, lengths, positions, embed_table, vecs_all):
     n_seq, seq_len = tokens.shape
-    vocab_size, model_dim = embed_table.shape
-    n_heads, head_dim = 20, 32
-    mats = w_all.reshape(60, model_dim, 128)
-    qkv_w = mats[:15].transpose(1, 0, 2).reshape(model_dim, 3, n_heads, head_dim)
-    out_w = mats[15:20].transpose(1, 0, 2).reshape(model_dim, model_dim)
-    up_w = mats[20:40].transpose(1, 0, 2).reshape(model_dim, 2560)
-    down_w = mats[40:60].reshape(4, 5, model_dim, 128).transpose(0, 2, 1, 3).reshape(2560, model_dim)
-    len_col = lengths[:, None]
     is_mask = tokens == MASK_ID
-    tok_valid = positions[None, :] < len_col
+    tok_valid = positions[None, :] < lengths[:, None]
     mask_count = jnp.sum(is_mask.astype(jnp.int32), axis=1)
-    drop_scale = (1.0 - TRAIN_RATIO) / (1.0 - mask_count.astype(f32) / lengths.astype(f32))
-    keep_scale = jnp.where(is_mask | jnp.logical_not(tok_valid), 0.0, drop_scale[:, None])[:, :, None]
-    one_hot = (tokens[:, :, None] == jnp.arange(vocab_size)).astype(bf16)
-    embedded = jnp.einsum('bsv,vd->bsd', one_hot, embed_table, preferred_element_type=f32) * keep_scale
-    norm_in32, ln1_pull = jax.vjp(layer_norm, embedded, vecs_all[0], vecs_all[1])
-    norm_in = norm_in32.astype(bf16)
-    qkv_lin = jnp.einsum('bsd,dthe->bsthe', norm_in, qkv_w, preferred_element_type=f32) + vecs_all[2:5].reshape(3, n_heads, head_dim)
-    cos_t, sin_t = rope_tables(positions, head_dim)
-    q_rot = rotate(qkv_lin[:, :, 0] * head_dim ** -0.5, cos_t, sin_t).astype(bf16)
-    k_rot = rotate(qkv_lin[:, :, 1], cos_t, sin_t).astype(bf16)
-    v_val = qkv_lin[:, :, 2].astype(bf16)
-    scores = jnp.einsum('bqhd,bkhd->bhqk', q_rot, k_rot, preferred_element_type=f32)
-    scores = jnp.where(tok_valid[:, None, None, :], scores, NEG_BIG)
-    weights = jax.nn.softmax(scores, axis=-1)
-    weights_b = weights.astype(bf16)
-    attn32 = jnp.einsum('bhqk,bkhd->bqhd', weights_b, v_val, preferred_element_type=f32)
-    attn_out = attn32.astype(bf16).reshape(n_seq, seq_len, model_dim)
-    resid_mid = embedded + jnp.einsum('bsd,de->bse', attn_out, out_w, preferred_element_type=f32) + vecs_all[5]
-    norm_mid32, ln2_pull = jax.vjp(layer_norm, resid_mid, vecs_all[6], vecs_all[7])
-    norm_mid = norm_mid32.astype(bf16)
-    up_lin = jnp.einsum('bsd,df->bsf', norm_mid, up_w, preferred_element_type=f32) + up_b
-    gelu32, gelu_pull = jax.vjp(gelu_exact, up_lin)
-    gelu_out = gelu32.astype(bf16)
-    layer_out = (resid_mid + jnp.einsum('bsf,fd->bsd', gelu_out, down_w, preferred_element_type=f32) + vecs_all[8]).astype(bf16)
-
-    grad32 = grad_out.astype(f32)
-    d_down = jnp.einsum('bsf,bsd->fd', gelu_out, grad_out, preferred_element_type=f32)
-    d_gelu = jnp.einsum('bsd,fd->bsf', grad_out, down_w, preferred_element_type=f32)
-    d_up_lin = gelu_pull(d_gelu)[0]
-    d_up_b = d_up_lin.astype(bf16)
-    d_up = jnp.einsum('bsd,bsf->df', norm_mid, d_up_b, preferred_element_type=f32)
-    d_norm_mid = jnp.einsum('bsf,df->bsd', d_up_b, up_w, preferred_element_type=f32)
-    d_resid_ln, d_gain2, d_bias2 = ln2_pull(d_norm_mid)
-    d_resid = grad32 + d_resid_ln
-    d_resid_b = d_resid.astype(bf16)
-    d_outw = jnp.einsum('bsd,bse->de', attn_out, d_resid_b, preferred_element_type=f32)
-    d_attn = jnp.einsum('bse,de->bsd', d_resid_b, out_w, preferred_element_type=f32).reshape(n_seq, seq_len, n_heads, head_dim)
-    d_attn_b = d_attn.astype(bf16)
-    delta = jnp.swapaxes(jnp.sum(d_attn * attn32, axis=-1), 1, 2)
-    d_weights = jnp.einsum('bqhd,bkhd->bhqk', d_attn_b, v_val, preferred_element_type=f32)
-    d_scores = (weights * (d_weights - delta[..., None])).astype(bf16)
-    d_query = jnp.einsum('bhqk,bkhd->bqhd', d_scores, k_rot, preferred_element_type=f32)
-    d_key = jnp.einsum('bhqk,bqhd->bkhd', d_scores, q_rot, preferred_element_type=f32)
-    d_value = jnp.einsum('bhqk,bqhd->bkhd', weights_b, d_attn_b, preferred_element_type=f32)
-    d_q_lin = rotate(d_query, cos_t, -sin_t) * head_dim ** -0.5
-    d_k_lin = rotate(d_key, cos_t, -sin_t)
-    d_qkv_lin = jnp.stack([d_q_lin, d_k_lin, d_value], axis=2)
-    d_qkv_b = d_qkv_lin.astype(bf16)
-    d_qkvw = jnp.einsum('bsd,bsthe->dthe', norm_in, d_qkv_b, preferred_element_type=f32)
-    d_norm_in = jnp.einsum('bsthe,dthe->bsd', d_qkv_b, qkv_w, preferred_element_type=f32)
-    d_embedded, d_gain1, d_bias1 = ln1_pull(d_norm_in)
-    d_embedded = d_embedded + d_resid
-    d_table = jnp.einsum('bsv,bsd->vd', one_hot, (d_embedded * keep_scale).astype(bf16), preferred_element_type=f32)
-    d_bqkv = jnp.sum(d_qkv_lin, axis=(0, 1)).reshape(3, model_dim)
-    d_tail = jnp.stack([jnp.sum(d_resid, axis=(0, 1)), d_gain2, d_bias2, jnp.sum(grad32, axis=(0, 1))])
-    d_vecs = jnp.concatenate([jnp.stack([d_gain1, d_bias1]), d_bqkv, d_tail], axis=0)
-    g_all = jnp.concatenate([
-        d_qkvw.reshape(model_dim, 15, 128).transpose(1, 0, 2),
-        d_outw.reshape(model_dim, 5, 128).transpose(1, 0, 2),
-        d_up.reshape(model_dim, 20, 128).transpose(1, 0, 2),
-        d_down.reshape(4, model_dim, 5, 128).transpose(0, 2, 1, 3).reshape(20, model_dim, 128),
-    ], axis=0)
-    return layer_out, d_table, d_vecs, g_all, jnp.sum(d_up_lin, axis=(0, 1))
+    drop_scale = (1.0 - TRAIN_RATIO) / (1.0 - mask_count.astype(F32) / lengths.astype(F32))
+    keep = jnp.where(is_mask | jnp.logical_not(tok_valid), 0.0, drop_scale[:, None])
+    keep = jnp.broadcast_to(keep.reshape(-1, 1), (n_seq * seq_len, LANES))
+    mask = jnp.broadcast_to(jnp.where(tok_valid, 0.0, NEG_BIG).reshape(-1, 1), (n_seq * seq_len, LANES)).astype(F32)
+    emb = jnp.pad(embed_table, ((0, 64 - embed_table.shape[0]), (0, 0)))
+    bqkv = jnp.broadcast_to(vecs_all[2:5].reshape(-1, 1), (1920, LANES))
+    inv_freq = 1.0 / (ROPE_BASE ** (jnp.arange(0, HEAD, 2, dtype=F32) / HEAD))
+    angles = positions.astype(F32)[:, None] * inv_freq[None, :]
+    cos, sin = jnp.cos(angles), jnp.sin(angles)
+    cos_t, sin_t = jnp.tile(cos.T, (1, STEP_SEQS)), jnp.tile(sin.T, (1, STEP_SEQS))
+    cos_n = jnp.tile(cos, (1, 8))
+    sin_n = jnp.tile(jnp.concatenate([sin, -sin], axis=1), (1, 4))
+    return tokens.reshape(STEPS, 1, TOK), keep, mask, emb, bqkv, cos_t, sin_t, cos_n, sin_n
 
 
 def solution(mesh):
@@ -495,13 +757,16 @@
         up_b = s_flat[:, 90:130].reshape(chips, 4, NB).transpose(1, 0, 2).reshape(-1)
         start = half * cp
         tok_full = jnp.concatenate([lax.dynamic_slice_in_dim(tokens, start, half, 0), t_oth], axis=1)
-        grad_full = jnp.concatenate([lax.dynamic_slice_in_dim(grad_out, start, half, 0), g_oth], axis=1)
         len_own = lax.dynamic_slice_in_dim(lengths, start, half, 0)
         positions = jnp.concatenate([cp * seq_loc + jnp.arange(seq_loc), (1 - cp) * seq_loc + jnp.arange(seq_loc)])
-        layer_out, d_table, d_vecs, g_all, d_bup = layer_compute(tok_full, len_own, positions, embed_table, vecs_all, w_all, up_b, grad_full)
-        small = jnp.concatenate([d_table.reshape(-1), d_vecs.reshape(-1), d_bup])
+        tok, keep, mask, emb, bqkv, cos, sin, cosn, sinn = prepare(tok_full, len_own, positions, embed_table, vecs_all)
+        y_own, y_oth, g_all, dtab, dsum, dbq, dbkv, dbup = layer_call(
+            tok, keep, mask, emb, vecs_all, bqkv, up_b.reshape(4, 1, 640), cos, sin, cosn, sinn, w_all.reshape(60, chips, NB, 128), grad_out, g_oth)
+        rowsum = jnp.sum(dsum, axis=1)
+        d_bq = jnp.sum(dbq, axis=2).reshape(1, width)
+        d_bkv = jnp.sum(dbkv, axis=2).reshape(2, width)
+        small = jnp.concatenate([dtab[:vocab].reshape(-1), rowsum[:2].reshape(-1), d_bq.reshape(-1), d_bkv.reshape(-1), rowsum[2:].reshape(-1), jnp.sum(dbup, axis=1).reshape(-1)])
         small = jnp.pad(small, (0, 2 * SMALL_ROWS * 128 - small.shape[0])).reshape(2, SMALL_ROWS, 128)
-        y_own, y_oth = layer_out[:, :seq_loc], layer_out[:, seq_loc:]
         g_red, s_red, y_recv = reduce_all(g_all.reshape(60, SIDE, SIDE, SIDE, NB, 128), small, y_oth)
         out_full = jnp.where(cp == 0, jnp.concatenate([y_own, y_recv], axis=0), jnp.concatenate([y_recv, y_own], axis=0))
         s_flat = s_red.reshape(-1)

time: 685 us -> 412 us (0.60)
  matrix products: 247 us -> 0 us
  Pallas kernels: 126 us -> 370 us
  local copies, waits for them, and re-layouts: 167 us -> 29.5 us
  other arithmetic: 136 us -> 10.5 us
    pallas_call x0 -> x1, Pallas kernels: none -> 244 us  [layer_call(): pl.pallas_call(layer_kernel, grid=(STEPS,), out_shape=out_shape, in_specs...]
    dot_general x19 -> x0, matrix products: 226 us -> none  [the longest x1 24.4 us: layer_compute(): jnp.einsum('bqhd,bkhd->bhqk', d_attn_b, v_val, preferred_element_type=f32)]
    convert_element_type x3 -> x1, other arithmetic: 73.8 us -> 0.01 us  [prepare(): angles = positions.astype(F32)[:, None] * inv_freq[None, :]]
    slice x16 -> x5, local copies, waits for them, and re-layouts: 40.6 us -> 1.02 us  [the longest x1 0.9 us: local_step(): dtab[:vocab].reshape(-1)]
    transpose x7 -> x1, local copies, waits for them, and re-layouts: 37.1 us -> 0.16 us  [local_step(): s_flat[:, :90].reshape(chips, 9, NB).transpose(1, 0, 2).reshape(9, width)]
    concatenate x5 -> x1, local copies, waits for them, and re-layouts: 26.7 us -> 0.01 us  [local_step(): jnp.concatenate([dtab[:vocab].reshape(-1), rowsum[:2].reshape(-1), d_bq.r...]
    concatenate x3 -> x1, other arithmetic: 25.7 us -> 0.01 us  [prepare(): sin_n = jnp.tile(jnp.concatenate([sin, -sin], axis=1), (1, 4))]
    sub x1 -> x0, matrix products: 21.6 us -> none  [layer_compute(): weights = jax.nn.softmax(scores, axis=-1)]
where the time goes in v2:
time: 412 us; the launch traced here: 411 us
  Pallas kernels  370 us (90%)
  local copies, waits for them, and re-layouts  29.5 us (7%)
  other arithmetic  10.5 us (3%)
    pallas_call x1, Pallas kernels, layer_call(): pl.pallas_call(layer_kernel, grid=(STEPS,), out_shape=out_shape, in_specs...  244 us
    pallas_call x1, Pallas kernels, reduce_all(): pl.pallas_call(reduce_kernel, out_shape=(jax.ShapeDtypeStruct((blocks, NB...  64.3 us
    pallas_call x1, Pallas kernels, gather_all(): pl.pallas_call(gather_kernel, out_shape=(jax.ShapeDtypeStruct((blocks, SI...  61.7 us

profile of v2, /device:TPU:1, one launch (start us, length us, event | category | flops | bytes accessed | tf_op | source)
XLA Modules:
  0.0 411.2 jit_solution(16681772955815896823)
XLA Ops:
  0.7 0.8 constant_dynamic-slice_fusion.1
  1.5 2.3 reshape.280
  3.8 0.2 copy.23
  3.9 1.2 reshape.281
  5.3 0.1 reshape.278
  5.5 0.7 pad_maximum_fusion.w_loc
  6.4 0.7 fusion.3.s_loc
  7.0 61.7 %gather_weights.1 = (bf16[60,4,4,4,10,128]{5,4,3,2,1,0:T(8,128)(2,1)}, f32[4,4,4,8,128]{4,3,2,1,0:T(8,128)}, bf16[8,128,640]{2,1,0:T(8,128)(2,1)}, s32[8,128]{1,0:T(8,128)}) custom-call(bf16[60,10,128]{2,1,0:T(8,128)(2,1)} %pad_maximum_fusion.w_loc, f32[8,128]{1,0:T(8,128)} %fusion.3.s_loc, bf16[16,128,640]{2,1,0:T(8,128)(2,1)} %g_own.3, s32[16,128]{1,0:T(8,128)} %t_own.1), custom_call_target="tpu_custom_call" | custom-call | tf_op jit(solution)/shard_map/gather_weights/pallas_call | solution.py:161
  68.7 0.8 convert_reduce_fusion
  69.8 1.3 broadcast_in_dim.42.keep_ref
  71.1 1.3 broadcast_in_dim.44.mask_ref
  72.4 0.1 multiply_sine_fusion
  72.6 0.8 copy.33.sinn_ref
  73.4 0.6 reshape.286.tok_ref
  74.0 0.7 copy.32.cosn_ref
  74.8 0.1 multiply_sine_fusion.1
  74.9 0.6 copy.44
  75.5 0.6 copy.45
  76.3 0.1 copy.28
  76.4 0.1 broadcast_in_dim.45
  76.6 1.3 broadcast_in_dim.46.bqkv_ref
  77.9 0.2 copy.27
  78.0 0.8 reshape.289.vec_ref
  79.0 0.1 copy.30
  79.1 0.7 reshape_reshape.12.bup_ref
  79.9 0.6 pad.13.emb_ref
  80.5 244.1 %layer.1 = (bf16[8,128,640]{2,1,0:T(8,128)(2,1)}, bf16[8,128,640]{2,1,0:T(8,128)(2,1)}, f32[60,64,10,128]{3,2,1,0:T(8,128)}, f32[64,640]{1,0:T(8,128)}, f32[6,8,...) custom-call(s32[4,1,512]{2,1,0:T(1,128)} %reshape.286.tok_ref, ...), custom_call_target="tpu_custom_call" | custom-call | tf_op jit(solution)/shard_map/layer/pallas_call | solution.py:704
  324.6 0.9 slice.50
  325.6 0.9 reduce_sum.46
  326.5 1.1 reduce_sum.47
  327.7 0.8 reduce_sum.48
  328.6 0.9 reduce_sum.49
  329.5 0.7 pad.14
  330.2 64.3 %reduce_grads.1 = (f32[60,10,128]{2,1,0:T(8,128)}, f32[2,120,128]{2,1,0:T(8,128)}, bf16[8,128,640]{2,1,0:T(8,128)(2,1)}) custom-call(f32[60,4,4,4,10,128]{5,4,3,2,1,0:T(8,128)} %bitcast.65, f32[2,120,128]{2,1,0:T(8,128)} %bitcast.73, bf16[8,128,640]{2,1,0:T(8,128)(2,1)} %get-tuple-element.34.y_oth), custom_call_target="tpu_custom_call" | custom-call | tf_op jit(solution)/shard_map/reduce_grads/pallas_call | solution.py:345
  394.5 1.0 fusion.5
  395.6 1.4 reshape.300
  397.0 0.9 copy.37
  397.8 1.8 reshape.301
  399.6 4.0 maximum_select_fusion
  403.6 1.6 slice.59
  405.3 0.6 reshape.302
  405.9 0.7 copy.54
  406.6 0.9 slice_bitcast_fusion.1
  407.5 0.9 reshape.298
  408.4 0.7 slice.67
  409.1 0.8 slice_bitcast_fusion.2
  409.9 0.6 copy.46
  410.5 0.7 constant_dynamic-slice_fusion
  (68 shorter events, 1.1 us)
Async XLA Ops:
  0.6 4.5 %copy-start.3 = (bf16[40,640]{1,0:T(8,128)(2,1)S(1)}, bf16[40,640]{1,0:T(8,128)(2,1)}, u32[]{:S(2)}) copy-start(bf16[40,640]{1,0:T(8,128)(2,1)} %param.18) | copy-start | bytes 153604
  0.6 4.7 %copy-start.2 = (bf16[10,3,20,32]{3,2,1,0:T(8,128)(2,1)S(1)}, bf16[10,3,20,32]{3,2,1,0:T(8,128)(2,1)}, u32[]{:S(2)}) copy-start(bf16[10,3,20,32]{3,2,1,0:T(8,128)(2,1)} %param.14) | copy-start | bytes 115204
  0.7 4.8 %copy-start.5 = (bf16[10,640]{1,0:T(8,128)(2,1)S(1)}, bf16[10,640]{1,0:T(8,128)(2,1)}, u32[]{:S(2)}) copy-start(bf16[10,640]{1,0:T(8,128)(2,1)} %param.15) | copy-start | bytes 38404
  0.7 5.6 %copy-start.6 = (f32[9,10]{1,0:T(8,128)S(1)}, f32[9,10]{1,0:T(8,128)}, u32[]{:S(2)}) copy-start(f32[9,10]{1,0:T(8,128)} %param.13) | copy-start | bytes 1084
  0.7 5.7 %copy-start.7 = (f32[40]{0:T(128)S(1)}, f32[40]{0:T(128)}, u32[]{:S(2)}) copy-start(f32[40]{0:T(128)} %param.17) | copy-start | bytes 484
  3.9 65.7 %copy-start.8 = (s32[16]{0:T(128)S(1)}, s32[16]{0:T(128)}, u32[]{:S(2)}) copy-start(s32[16]{0:T(128)} %param.11) | copy-start | bytes 196
  68.7 7.4 %copy-start.1 = (f32[4,4,4,8,128]{4,3,2,1,0:T(8,128)S(1)}, f32[4,4,4,8,128]{4,3,2,1,0:T(8,128)}, u32[]{:S(2)}) copy-start(f32[4,4,4,8,128]{4,3,2,1,0:T(8,128)} %get-tuple-element.24) | copy-start | bytes 786436
  71.1 8.8 %copy-start.4 = (bf16[33,640]{1,0:T(8,128)(2,1)S(1)}, bf16[33,640]{1,0:T(8,128)(2,1)}, u32[]{:S(2)}) copy-start(bf16[33,640]{1,0:T(8,128)(2,1)} %param.12) | copy-start | bytes 126724
  399.6 4.0 copy-start

commit v3 on v2

--- a/solution.py
+++ b/solution.py
@@ -519,25 +519,39 @@
     lane_head = lax.broadcasted_iota(jnp.int32, (1, LANES), 1) // HEAD
     pick = [jnp.where(lane_head == h, 1.0, 0.0).astype(BF16) for h in range(HEADS_PER)]
 
+    def stack(tile):
+        return jnp.concatenate([tile * pick[h] for h in range(HEADS_PER)], axis=0)
+
+    def spot(h):
+        return slice((h % 2) * SEQ, (h % 2 + 1) * SEQ), (h // 2) * SEQ
+
+    def stage(buf, value):
+        for h in range(HEADS_PER):
+            down, along = spot(h)
+            buf[down, along:along + SEQ] = value[h * SEQ:(h + 1) * SEQ]
+
     @pl.loop(0, STEP_SEQS)
     def _(s):
         rows = pl.ds(pl.multiple_of(s * SEQ, SEQ), SEQ)
-
-        @pl.loop(0, TILES)
-        def _(t):
+        bufs = (y_s, dnm)
+
+        def scores(t):
+            stage(bufs[t % 2], mm(stack(kn[s, t]), qt[s, t]))
+
+        scores(0)
+        for t in range(TILES):
+            if t + 1 < TILES:
+                scores(t + 1)
             bias = mask_ref[rows]
-            bias = jnp.concatenate([bias, bias], axis=1)
-            q_t, k_n, v_t = qt[s, t], kn[s, t], vt[s, t]
-            outs = []
             for h in range(HEADS_PER):
-                score = mm(k_n * pick[h], q_t) + bias
-                top = jnp.max(score, axis=0, keepdims=True)
-                p = jnp.exp(score - top)
-                p = p * (1.0 / jnp.sum(p, axis=0, keepdims=True))
-                pb = p.astype(BF16)
-                pt[s, t * HEADS_PER + h] = pb
-                outs.append(mm(v_t[h * HEAD:(h + 1) * HEAD], pb))
-            out = jnp.concatenate(outs, axis=0)
+                down, along = spot(h)
+                for c in range(0, SEQ, LANES):
+                    score = bufs[t % 2][down, along + c:along + c + LANES] + bias
+                    p = jnp.exp(score - jnp.max(score, axis=0, keepdims=True))
+                    p = p * (1.0 / jnp.sum(p, axis=0, keepdims=True))
+                    pt[s, t * HEADS_PER + h, :, c:c + LANES] = p.astype(BF16)
+            v_t = vt[s, t]
+            out = jnp.concatenate([mm(v_t[h * HEAD:(h + 1) * HEAD], pt[s, t * HEADS_PER + h]) for h in range(HEADS_PER)], axis=0)
             ot32[s, t] = out
             outb = out.astype(BF16)
             otb[t, :, rows] = outb
@@ -607,30 +621,38 @@
     @pl.loop(0, STEP_SEQS)
     def _(s):
         rows = pl.ds(pl.multiple_of(s * SEQ, SEQ), SEQ)
-
-        @pl.loop(0, TILES)
-        def _(t):
+        bufs = (x1, dnm)
+        outs = (nm, nmt)
+
+        def slopes(t):
+            stage(bufs[t % 2], mm(stack(vn[s, t]), dot_s[t, :, rows].astype(BF16)))
+
+        slopes(0)
+        for t in range(TILES):
+            if t + 1 < TILES:
+                slopes(t + 1)
             d_ot = dot_s[t, :, rows]
-            d_otb = d_ot.astype(BF16)
-            d_on = d_otb.T
             prod = d_ot * ot32[s, t]
-            k_t, v_n, q_n = kt[s, t], vn[s, t], qn[s, t]
+            ds_ref = outs[t % 2]
+            for h in range(HEADS_PER):
+                down, along = spot(h)
+                delta = jnp.sum(prod[h * HEAD:(h + 1) * HEAD], axis=0, keepdims=True)
+                for c in range(0, SEQ, LANES):
+                    d_p = bufs[t % 2][down, along + c:along + c + LANES]
+                    p = pt[s, t * HEADS_PER + h, :, c:c + LANES].astype(F32)
+                    ds_ref[down, along + c:along + c + LANES] = (p * (d_p - delta[:, c:c + LANES])).astype(BF16)
+            k_t, q_n = kt[s, t], qn[s, t]
             dqs = []
-            dk, dv = None, None
             for h in range(HEADS_PER):
-                lanes = slice(h * HEAD, (h + 1) * HEAD)
-                pb = pt[s, t * HEADS_PER + h]
-                delta = jnp.sum(prod[lanes], axis=0, keepdims=True)
-                d_p = mm(v_n * pick[h], d_otb)
-                d_sb = (pb.astype(F32) * (d_p - delta)).astype(BF16)
-                dqs.append(mm(k_t[lanes], d_sb))
-                dk_h = mm(d_sb, q_n * pick[h])
-                dv_h = mm(pb, d_on * pick[h])
-                dk = dk_h if dk is None else dk + dk_h
-                dv = dv_h if dv is None else dv + dv_h
+                down, along = spot(h)
+                dqs.append(mm(k_t[h * HEAD:(h + 1) * HEAD], ds_ref[down, along:along + SEQ]))
             dq = unturn(jnp.concatenate(dqs, axis=0), cos[:, :SEQ], sin[:, :SEQ], HEADS_PER) * HEAD ** -0.5
             dbq[t] += dq[:, :LANES] + dq[:, LANES:]
             dqkv[t, rows] = dq.astype(BF16).T
+            dk = mm(ds_ref[:SEQ, :2 * SEQ], jnp.concatenate([q_n * pick[0], q_n * pick[2]], axis=0))
+            dk = dk + mm(ds_ref[SEQ:2 * SEQ, :2 * SEQ], jnp.concatenate([q_n * pick[1], q_n * pick[3]], axis=0))
+            p_wide = jnp.concatenate([pt[s, t * HEADS_PER + h] for h in range(HEADS_PER)], axis=1)
+            dv = mm(p_wide, stack(d_ot.astype(BF16).T))
             low = lax.rem(lax.broadcasted_iota(jnp.int32, (SEQ, LANES), 1), HEAD) < HEAD // 2
             other = jnp.where(low, pltpu.roll(dk, LANES - HEAD // 2, 1), pltpu.roll(dk, HEAD // 2, 1))
             dk = dk * cosn_ref[...] + other * sinn_ref[...]

time: 412 us -> 346 us (0.84)
  Pallas kernels: 370 us -> 304 us
    pallas_call x1, Pallas kernels: 244 us -> 178 us  [layer_call(): pl.pallas_call(layer_kernel, grid=(STEPS,), out_shape=out_shape, in_specs...]
where the time goes in v3:
time: 346 us; the launch traced here: 345 us
  Pallas kernels  304 us (88%)
  local copies, waits for them, and re-layouts  29.5 us (9%)
  other arithmetic  10.5 us (3%)
    pallas_call x1, Pallas kernels, layer_call(): pl.pallas_call(layer_kernel, grid=(STEPS,), out_shape=out_shape, in_specs...  178 us
    pallas_call x1, Pallas kernels, reduce_all(): pl.pallas_call(reduce_kernel, out_shape=(jax.ShapeDtypeStruct((blocks, NB...  64.3 us
    pallas_call x1, Pallas kernels, gather_all(): pl.pallas_call(gather_kernel, out_shape=(jax.ShapeDtypeStruct((blocks, SI...  61.7 us

profile of v3, /device:TPU:1, one launch (start us, length us, event | category | flops | bytes accessed | tf_op | source)
XLA Modules:
  0.0 345.3 jit_solution(12932466507489606483)
XLA Ops:
  0.7 0.8 constant_dynamic-slice_fusion.1
  1.5 2.3 reshape.280
  3.8 0.2 copy.23
  3.9 1.2 reshape.281
  5.3 0.1 reshape.278
  5.5 0.7 pad_maximum_fusion.w_loc
  6.4 0.7 fusion.3.s_loc
  7.0 61.7 %gather_weights.1 = (bf16[60,4,4,4,10,128]{5,4,3,2,1,0:T(8,128)(2,1)}, f32[4,4,4,8,128]{4,3,2,1,0:T(8,128)}, bf16[8,128,640]{2,1,0:T(8,128)(2,1)}, s32[8,128]{1,0:T(8,128)}) custom-call(bf16[60,10,128]{2,1,0:T(8,128)(2,1)} %pad_maximum_fusion.w_loc, f32[8,128]{1,0:T(8,128)} %fusion.3.s_loc, bf16[16,128,640]{2,1,0:T(8,128)(2,1)} %g_own.3, s32[16,128]{1,0:T(8,128)} %t_own.1), custom_call_target="tpu_custom_call" | custom-call | tf_op jit(solution)/shard_map/gather_weights/pallas_call | solution.py:161
  68.7 0.8 convert_reduce_fusion
  69.8 1.3 broadcast_in_dim.42.keep_ref
  71.1 1.3 broadcast_in_dim.44.mask_ref
  72.4 0.1 multiply_sine_fusion
  72.6 0.8 copy.33.sinn_ref
  73.4 0.6 reshape.286.tok_ref
  74.0 0.7 copy.32.cosn_ref
  74.8 0.1 multiply_sine_fusion.1
  74.9 0.6 copy.44
  75.5 0.6 copy.45
  76.3 0.1 copy.28
  76.4 0.1 broadcast_in_dim.45
  76.6 1.3 broadcast_in_dim.46.bqkv_ref
  77.9 0.2 copy.27
  78.0 0.8 reshape.289.vec_ref
  79.0 0.1 copy.30
  79.1 0.7 reshape_reshape.12.bup_ref
  79.9 0.6 pad.13.emb_ref
  80.5 178.2 %layer.1 = (bf16[8,128,640]{2,1,0:T(8,128)(2,1)}, bf16[8,128,640]{2,1,0:T(8,128)(2,1)}, f32[60,64,10,128]{3,2,1,0:T(8,128)}, f32[64,640]{1,0:T(8,128)}, f32[6,8,...) custom-call(s32[4,1,512]{2,1,0:T(1,128)} %reshape.286.tok_ref, ...), custom_call_target="tpu_custom_call" | custom-call | tf_op jit(solution)/shard_map/layer/pallas_call | solution.py:726
  258.7 0.9 slice.50
  259.7 0.9 reduce_sum.46
  260.7 1.1 reduce_sum.47
  261.8 0.8 reduce_sum.48
  262.7 0.9 reduce_sum.49
  263.6 0.7 pad.14
  264.3 64.3 %reduce_grads.1 = (f32[60,10,128]{2,1,0:T(8,128)}, f32[2,120,128]{2,1,0:T(8,128)}, bf16[8,128,640]{2,1,0:T(8,128)(2,1)}) custom-call(f32[60,4,4,4,10,128]{5,4,3,2,1,0:T(8,128)} %bitcast.65, f32[2,120,128]{2,1,0:T(8,128)} %bitcast.73, bf16[8,128,640]{2,1,0:T(8,128)(2,1)} %get-tuple-element.34.y_oth), custom_call_target="tpu_custom_call" | custom-call | tf_op jit(solution)/shard_map/reduce_grads/pallas_call | solution.py:345
  328.6 1.0 fusion.5
  329.7 1.4 reshape.300
  331.1 0.9 copy.37
  332.0 1.8 reshape.301
  333.8 4.0 %maximum_select_fusion = bf16[16,128,640]{2,1,0:T(8,128)(2,1)} fusion(bf16[8,128,640]{2,1,0:T(8,128)(2,1)} %get-tuple-element.35, bf16[8,128,640]{2,1,0:T(8,128)(2,1)} %get-tuple-element.27, pred[]{:T(512)S(6)} %eq.14), kind=kLoop, calls=%fused_computation | loop fusion | flops 3932160 | bytes 5242881 | tf_op jit(solution)/shard_map/jit(_where)/select_n | solution.py:793
  337.7 1.6 slice.59
  339.4 0.6 reshape.302
  340.0 0.7 copy.54
  340.7 0.9 slice_bitcast_fusion.1
  341.7 0.9 reshape.298
  342.6 0.7 slice.67
  343.2 0.8 slice_bitcast_fusion.2
  344.0 0.6 copy.46
  344.6 0.7 constant_dynamic-slice_fusion
  (68 shorter events, 1.1 us)
Async XLA Ops:
  0.6 4.5 %copy-start.3 = (bf16[40,640]{1,0:T(8,128)(2,1)S(1)}, bf16[40,640]{1,0:T(8,128)(2,1)}, u32[]{:S(2)}) copy-start(bf16[40,640]{1,0:T(8,128)(2,1)} %param.18) | copy-start | bytes 153604
  0.6 4.7 %copy-start.2 = (bf16[10,3,20,32]{3,2,1,0:T(8,128)(2,1)S(1)}, bf16[10,3,20,32]{3,2,1,0:T(8,128)(2,1)}, u32[]{:S(2)}) copy-start(bf16[10,3,20,32]{3,2,1,0:T(8,128)(2,1)} %param.14) | copy-start | bytes 115204
  0.7 4.8 %copy-start.5 = (bf16[10,640]{1,0:T(8,128)(2,1)S(1)}, bf16[10,640]{1,0:T(8,128)(2,1)}, u32[]{:S(2)}) copy-start(bf16[10,640]{1,0:T(8,128)(2,1)} %param.15) | copy-start | bytes 38404
  0.7 5.6 %copy-start.6 = (f32[9,10]{1,0:T(8,128)S(1)}, f32[9,10]{1,0:T(8,128)}, u32[]{:S(2)}) copy-start(f32[9,10]{1,0:T(8,128)} %param.13) | copy-start | bytes 1084
  0.7 5.7 %copy-start.7 = (f32[40]{0:T(128)S(1)}, f32[40]{0:T(128)}, u32[]{:S(2)}) copy-start(f32[40]{0:T(128)} %param.17) | copy-start | bytes 484
  3.9 65.7 %copy-start.8 = (s32[16]{0:T(128)S(1)}, s32[16]{0:T(128)}, u32[]{:S(2)}) copy-start(s32[16]{0:T(128)} %param.11) | copy-start | bytes 196
  68.7 7.4 %copy-start.1 = (f32[4,4,4,8,128]{4,3,2,1,0:T(8,128)S(1)}, f32[4,4,4,8,128]{4,3,2,1,0:T(8,128)}, u32[]{:S(2)}) copy-start(f32[4,4,4,8,128]{4,3,2,1,0:T(8,128)} %get-tuple-element.24) | copy-start | bytes 786436
  71.1 8.8 %copy-start.4 = (bf16[33,640]{1,0:T(8,128)(2,1)S(1)}, bf16[33,640]{1,0:T(8,128)(2,1)}, u32[]{:S(2)}) copy-start(bf16[33,640]{1,0:T(8,128)(2,1)} %param.12) | copy-start | bytes 126724
  333.8 4.0 %copy-start = (f32[2,120,128]{2,1,0:T(8,128)S(1)}, f32[2,120,128]{2,1,0:T(8,128)}, u32[]{:S(2)}) copy-start(f32[2,120,128]{2,1,0:T(8,128)} %get-tuple-element.36) | copy-start | bytes 368644

commit v4 on v3

--- a/solution.py
+++ b/solution.py
@@ -15,8 +15,10 @@
 SIDE = 4
 COLORS = 3
 NB = 10
-HALF = 5
+GROUP = 5
+PER = 6
 SMALL_ROWS = 120
+QUARTERS = (2, 1, 3, 0)
 MESH_ID = pl.DeviceIdType.MESH
 ANY = pl.BlockSpec(memory_space=pl.ANY)
 
@@ -52,11 +54,11 @@
     return pltpu.make_async_remote_copy(src_ref=src, dst_ref=dst, send_sem=send_sem, recv_sem=recv_sem, device_id=target, device_id_type=MESH_ID)
 
 
-def gather_kernel(w_loc, s_loc, g_own, t_own, w_all, s_all, g_oth, t_oth, ssem, rsem, fsend, frecv, s_ssem, s_rsem, psend, precv, lsem):
+def gather_kernel(w_loc, s_loc, g_own, t_own, w_out, s_out, g_oth, t_oth, w_all, s_all, ssem, rsem, fsend, frecv, s_ssem, s_rsem, psend, precv, lsem, osem, xsem):
     cp = lax.axis_index('cp')
     me = my_coords()
     mate = {'cp': 1 - cp}
-    own_w = pltpu.make_async_copy(w_loc, w_all.at[:, me[0], me[1], me[2]], lsem.at[0])
+    own_w = pltpu.make_async_copy(w_loc, w_all.at[me[0], me[1], me[2]], lsem.at[0])
     own_s = pltpu.make_async_copy(s_loc, s_all.at[me[0], me[1], me[2]], lsem.at[1])
     own_w.start()
     own_s.start()
@@ -67,7 +69,7 @@
 
     def region(ref, first, count, dims, at):
         index = [slice(None) if d in dims else at[d] for d in range(3)]
-        return ref.at[(pl.ds(first, count), *index)]
+        return ref.at[(*index, pl.ds(first, count))]
 
     def small_region(dims, at):
         index = [slice(None) if d in dims else at[d] for d in range(3)]
@@ -75,15 +77,26 @@
 
     forwards = []
     pending = []
+    stores = []
+    arrivals = {}
+
+    def store(first, count, dims, at, sem):
+        index = [slice(None) if d in dims else at[d] for d in range(3)]
+        index = (*index, pl.ds(first, count))
+        copy = pltpu.make_async_copy(w_all.at[index], w_out.at[index], sem)
+        copy.start()
+        stores.append(copy)
+
     own_s.wait()
     own_w.wait()
+    store(0, 2 * PER, (), me, lsem.at[2])
     for phase in range(3):
         firsts = {}
         for color in range(COLORS):
             dim = GATHER_ORDER[color][phase]
             done = GATHER_ORDER[color][:phase]
-            base = cp * (COLORS * NB) + color * NB
-            mine = region(w_all, base, NB, done, me)
+            base = cp * PER + color * 2
+            mine = region(w_all, base, 2, done, me)
             right, left = chip_id(moved(me, dim, 1)), chip_id(moved(me, dim, 3))
             to_right = push(mine, mine, ssem.at[color, phase, 0], rsem.at[color, phase, 0], right)
             to_left = push(mine, mine, ssem.at[color, phase, 1], rsem.at[color, phase, 1], left)
@@ -102,27 +115,30 @@
         for color in range(COLORS):
             dim = GATHER_ORDER[color][phase]
             done = GATHER_ORDER[color][:phase]
-            base = cp * (COLORS * NB) + color * NB
+            base = cp * PER + color * 2
             right, left = chip_id(moved(me, dim, 1)), chip_id(moved(me, dim, 3))
             from_left, from_right = moved(me, dim, 3), moved(me, dim, 1)
             to_right, to_left = firsts[color]
             to_right.wait_recv()
-            part = region(w_all, base, HALF, done, from_left)
+            part = region(w_all, base, 1, done, from_left)
             on_right = push(part, part, ssem.at[color, phase, 2], rsem.at[color, phase, 2], right)
             on_right.start()
-            whole_l = region(w_all, base, NB, done, from_left)
+            whole_l = region(w_all, base, 2, done, from_left)
             fwd_l = push(whole_l, whole_l, fsend.at[color, phase, 0], frecv.at[color, phase, 0], mate)
             fwd_l.start()
+            store(base, 2, done, from_left, osem.at[color, phase, 0])
             to_left.wait_recv()
-            part = region(w_all, base + HALF, HALF, done, from_right)
+            part = region(w_all, base + 1, 1, done, from_right)
             on_left = push(part, part, ssem.at[color, phase, 3], rsem.at[color, phase, 3], left)
             on_left.start()
-            whole_r = region(w_all, base, NB, done, from_right)
+            whole_r = region(w_all, base, 2, done, from_right)
             fwd_r = push(whole_r, whole_r, fsend.at[color, phase, 1], frecv.at[color, phase, 1], mate)
             fwd_r.start()
+            store(base, 2, done, from_right, osem.at[color, phase, 1])
             seconds[color] = (on_right, on_left)
             pending += [on_right, on_left]
             forwards += [fwd_l, fwd_r]
+            arrivals[color, phase] = [(fwd_l, done, from_left, 0), (fwd_r, done, from_right, 1)]
             if color == 0:
                 s_right.wait_recv()
                 s_left.wait_recv()
@@ -133,20 +149,30 @@
         for color in range(COLORS):
             dim = GATHER_ORDER[color][phase]
             done = GATHER_ORDER[color][:phase]
-            base = cp * (COLORS * NB) + color * NB
+            base = cp * PER + color * 2
             on_right, on_left = seconds[color]
             on_right.wait_recv()
             on_left.wait_recv()
-            far = region(w_all, base, NB, done, moved(me, dim, 2))
+            far = region(w_all, base, 2, done, moved(me, dim, 2))
             fwd_f = push(far, far, fsend.at[color, phase, 2], frecv.at[color, phase, 2], mate)
             fwd_f.start()
+            store(base, 2, done, moved(me, dim, 2), osem.at[color, phase, 2])
             forwards.append(fwd_f)
+            arrivals[color, phase].append((fwd_f, done, moved(me, dim, 2), 2))
             if color == 0:
                 s_on.wait_recv()
         if phase == 0:
             swap_g.start()
-    for copy in forwards:
-        copy.wait_recv()
+    s_store = pltpu.make_async_copy(s_all, s_out, lsem.at[3])
+    s_store.start()
+    for phase in range(3):
+        for color in range(COLORS):
+            for copy, done, at, slot in arrivals[color, phase]:
+                copy.wait_recv()
+                store((1 - cp) * PER + color * 2, 2, done, at, xsem.at[color, phase, slot])
+    s_store.wait()
+    for copy in stores:
+        copy.wait()
     swap_g.wait()
     swap_t.wait()
     for copy in pending + forwards:
@@ -155,21 +181,23 @@
 
 def gather_all(w_loc, s_loc, grad_out, tokens):
     bf16, f32 = jnp.bfloat16, jnp.float32
-    blocks = w_loc.shape[0]
     seqs, pos, width = grad_out.shape
     dma = pltpu.SemaphoreType.DMA
     return pl.pallas_call(
         gather_kernel,
         out_shape=(
-            jax.ShapeDtypeStruct((blocks, SIDE, SIDE, SIDE, NB, 128), bf16),
+            jax.ShapeDtypeStruct((SIDE, SIDE, SIDE, *w_loc.shape), bf16),
             jax.ShapeDtypeStruct((SIDE, SIDE, SIDE, 8, 128), f32),
             jax.ShapeDtypeStruct((seqs // 2, pos, width), bf16),
             jax.ShapeDtypeStruct((seqs // 2, pos), jnp.int32),
         ),
         in_specs=[ANY] * 4,
         out_specs=(ANY,) * 4,
-        scratch_shapes=[dma((3, 3, 4)), dma((3, 3, 4)), dma((3, 3, 3)), dma((3, 3, 3)), dma((3, 3)), dma((3, 3)), dma((2,)), dma((2,)), dma((2,))],
-        compiler_params=pltpu.CompilerParams(collective_id=0, has_side_effects=True),
+        scratch_shapes=[
+            pltpu.VMEM((SIDE, SIDE, SIDE, *w_loc.shape), bf16), pltpu.VMEM((SIDE, SIDE, SIDE, 8, 128), f32),
+            dma((3, 3, 4)), dma((3, 3, 4)), dma((3, 3, 3)), dma((3, 3, 3)), dma((3, 3)), dma((3, 3)), dma((2,)), dma((2,)), dma((4,)), dma((3, 3, 3)), dma((3, 3, 3)),
+        ],
+        compiler_params=pltpu.CompilerParams(collective_id=0, has_side_effects=True, vmem_limit_bytes=40 * 1024 * 1024),
         name='gather_weights',
     )(w_loc, s_loc, grad_out, tokens)
 
@@ -179,24 +207,33 @@
     cp = lax.axis_index('cp')
     me = my_coords()
     mate = {'cp': 1 - cp}
-    per = COLORS * NB
-    loads = []
-    for color in range(COLORS):
-        load = pltpu.make_async_copy(g_all.at[pl.ds(cp * per + color * NB, NB)], held.at[pl.ds(color * NB, NB)], lsem.at[color])
-        load.start()
-        loads.append(load)
-    s_load = pltpu.make_async_copy(small, s_acc, lsem.at[3])
+    per = PER
+    loads = {}
+
+    def quarter(ref, first, color, by):
+        dim = REDUCE_ORDER[color][0]
+        index = [slice(None)] * 3
+        index[dim] = moved(me, dim, by)[dim]
+        return ref.at[(*index, pl.ds(first + color * 2, 2))]
+
+    for by in QUARTERS:
+        for color in range(COLORS):
+            load = pltpu.make_async_copy(quarter(g_all, cp * per, color, by), quarter(held, 0, color, by), lsem.at[color, by])
+            load.start()
+            loads[color, by] = load
+    s_load = pltpu.make_async_copy(small, s_acc, msem.at[2])
     s_load.start()
     entry_barrier(me, cp)
     sends = []
-    s_swap = push(small, s_pair, psend.at[3], precv.at[3], mate)
+    s_swap = push(small, s_pair, osend.at[2], orecv.at[2], mate)
     s_swap.start()
-    swaps = []
-    for color in range(COLORS):
-        swap = push(g_all.at[pl.ds((1 - cp) * per + color * NB, NB)], pair.at[pl.ds(color * NB, NB)], psend.at[color], precv.at[color], mate)
-        swap.start()
-        swaps.append(swap)
-    y_swap = push(y_oth, y_recv, psend.at[4], precv.at[4], mate)
+    swaps = {}
+    for by in QUARTERS:
+        for color in range(COLORS):
+            swap = push(quarter(g_all, (1 - cp) * per, color, by), quarter(pair, 0, color, by), psend.at[color, by], precv.at[color, by], mate)
+            swap.start()
+            swaps[color, by] = swap
+    y_swap = push(y_oth, y_recv, osend.at[3], orecv.at[3], mate)
     y_swap.start()
 
     bufs = ((ra0, rb0), (ra1, rb1), (ra2, rb2))
@@ -205,21 +242,46 @@
         return [slice(None) if d in dims else at[d] for d in range(3)]
 
     def region(first, count, dims, at):
-        return held.at[(pl.ds(first, count), *index_of(dims, at))]
-
-    def start_phase(color, phase):
+        return held.at[(*index_of(dims, at), pl.ds(first, count))]
+
+    def side(rb, color, way, rest, half):
+        return rb.at[(color, way, *[slice(None)] * len(rest), pl.ds(half, 1))]
+
+    def accumulate(rest, at, first, count, *sources):
+        where = index_of(rest, at)
+        units = slice(first, first + count)
+
+        def add(lead):
+            total = held[(*where, units)]
+            for ref, color, way in sources:
+                total = total + ref[(color, way, *lead)]
+            held[(*where, units)] = total
+
+        if rest:
+            dim = min(rest)
+
+            @pl.loop(0, SIDE)
+            def _(v):
+                where[dim] = v
+                add((v,))
+        else:
+            add(())
+
+    def start_phase(color, phase, part=None):
         dim = REDUCE_ORDER[color][phase]
         rest = REDUCE_ORDER[color][phase + 1:]
-        base = color * NB
+        base = color * 2
         ra, rb = bufs[phase]
         right, left = moved(me, dim, 1), moved(me, dim, 3)
         far = moved(me, dim, 2)
         out = [
-            push(region(base, HALF, rest, far), ra.at[color, 0], ssem.at[color, phase, 0], rsem.at[color, phase, 0], chip_id(right)),
-            push(region(base + HALF, HALF, rest, far), ra.at[color, 1], ssem.at[color, phase, 1], rsem.at[color, phase, 1], chip_id(left)),
-            push(region(base + HALF, HALF, rest, right), rb.at[color, 0, pl.ds(HALF, HALF)], ssem.at[color, phase, 2], rsem.at[color, phase, 2], chip_id(right)),
-            push(region(base, HALF, rest, left), rb.at[color, 1, pl.ds(0, HALF)], ssem.at[color, phase, 3], rsem.at[color, phase, 3], chip_id(left)),
+            push(region(base, 1, rest, far), ra.at[color, 0], ssem.at[color, phase, 0], rsem.at[color, phase, 0], chip_id(right)),
+            push(region(base + 1, 1, rest, far), ra.at[color, 1], ssem.at[color, phase, 1], rsem.at[color, phase, 1], chip_id(left)),
+            push(region(base + 1, 1, rest, right), side(rb, color, 0, rest, 1), ssem.at[color, phase, 2], rsem.at[color, phase, 2], chip_id(right)),
+            push(region(base, 1, rest, left), side(rb, color, 1, rest, 0), ssem.at[color, phase, 3], rsem.at[color, phase, 3], chip_id(left)),
         ]
+        if part is not None:
+            out = {2: out[:2], 1: out[2:3], 3: out[3:]}[part]
         for copy in out:
             copy.start()
         sends.extend(out)
@@ -228,43 +290,31 @@
     def middle(color, phase, copies):
         dim = REDUCE_ORDER[color][phase]
         rest = REDUCE_ORDER[color][phase + 1:]
-        base = color * NB
+        base = color * 2
         ra, rb = bufs[phase]
         right, left = moved(me, dim, 1), moved(me, dim, 3)
         copies[0].wait_recv()
-        to_r = index_of(rest, right)
-
-        @pl.loop(0, HALF)
-        def _(b):
-            held[(base + b, *to_r)] += ra[color, 0, b]
-
-        fwd_r = push(region(base, HALF, rest, right), rb.at[color, 0, pl.ds(0, HALF)], ssem.at[color, phase, 4], rsem.at[color, phase, 4], chip_id(right))
+        accumulate(rest, right, base, 1, (ra, color, 0))
+
+        fwd_r = push(region(base, 1, rest, right), side(rb, color, 0, rest, 0), ssem.at[color, phase, 4], rsem.at[color, phase, 4], chip_id(right))
         fwd_r.start()
         copies[1].wait_recv()
-        to_l = index_of(rest, left)
-
-        @pl.loop(0, HALF)
-        def _(b):
-            held[(base + HALF + b, *to_l)] += ra[color, 1, b]
-
-        fwd_l = push(region(base + HALF, HALF, rest, left), rb.at[color, 1, pl.ds(HALF, HALF)], ssem.at[color, phase, 5], rsem.at[color, phase, 5], chip_id(left))
+        accumulate(rest, left, base + 1, 1, (ra, color, 1))
+
+        fwd_l = push(region(base + 1, 1, rest, left), side(rb, color, 1, rest, 1), ssem.at[color, phase, 5], rsem.at[color, phase, 5], chip_id(left))
         fwd_l.start()
         sends.extend([fwd_r, fwd_l])
         return [fwd_r, fwd_l]
 
     def finish(color, phase, copies, late):
         rest = REDUCE_ORDER[color][phase + 1:]
-        base = color * NB
+        base = color * 2
         ra, rb = bufs[phase]
         copies[2].wait_recv()
         copies[3].wait_recv()
         late[0].wait_recv()
         late[1].wait_recv()
-        here = index_of(rest, me)
-
-        @pl.loop(0, NB)
-        def _(b):
-            held[(base + b, *here)] += rb[color, 0, b] + rb[color, 1, b]
+        accumulate(rest, me, base, 2, (rb, color, 0), (rb, color, 1))
 
     s_copies = []
 
@@ -295,17 +345,24 @@
     s_swap.wait()
     s_acc[...] = s_acc[...] + s_pair[...]
     s_out_copies = small_start(0)
-    started = []
-    for color in range(COLORS):
-        loads[color].wait()
-        swaps[color].wait_recv()
-
-        @pl.loop(0, NB)
-        def _(b):
-            for z in range(SIDE):
-                held[color * NB + b, z] += pair[color * NB + b, z]
-
-        started.append(start_phase(color, 0))
+    started = [[] for _ in range(COLORS)]
+    for by in QUARTERS:
+        for color in range(COLORS):
+            loads[color, by].wait()
+            swaps[color, by].wait_recv()
+            dim = REDUCE_ORDER[color][0]
+            part = [slice(None)] * 3
+            part[dim] = moved(me, dim, by)[dim]
+            other = (dim + 1) % 3
+
+            @pl.loop(0, SIDE)
+            def _(v):
+                part[other] = v
+                at = (*part, slice(color * 2, color * 2 + 2))
+                held[at] += pair[at]
+
+            if by:
+                started[color] += start_phase(color, 0, by)
     for phase in range(3):
         late = [middle(color, phase, started[color]) for color in range(COLORS)]
         nxt = []
@@ -317,7 +374,7 @@
         if phase < 2:
             s_out_copies = small_start(phase + 1)
         started = nxt
-    mine = held.at[:, me[0], me[1], me[2]]
+    mine = held.at[me[0], me[1], me[2]]
     out_far = push(mine, g_out.at[pl.ds(cp * per, per)], osend.at[0], orecv.at[0], mate)
     out_far.start()
     s_far = push(s_acc.at[cp], s_out.at[cp], osend.at[1], orecv.at[1], mate)
@@ -328,7 +385,7 @@
     s_own.start()
     for copy in sends:
         copy.wait_send()
-    for copy in swaps:
+    for copy in swaps.values():
         copy.wait_send()
     y_swap.wait()
     out_own.wait()
@@ -339,31 +396,31 @@
 
 def reduce_all(g_all, small, y_oth):
     f32 = jnp.float32
-    blocks = g_all.shape[0]
+    units, rows = g_all.shape[3:5]
     dma = pltpu.SemaphoreType.DMA
     vm = pltpu.VMEM
     return pl.pallas_call(
         reduce_kernel,
         out_shape=(
-            jax.ShapeDtypeStruct((blocks, NB, 128), f32),
+            jax.ShapeDtypeStruct((units, rows, 128), f32),
             jax.ShapeDtypeStruct(small.shape, f32),
             jax.ShapeDtypeStruct(y_oth.shape, y_oth.dtype),
         ),
         in_specs=[ANY] * 3,
         out_specs=(ANY,) * 3,
         scratch_shapes=[
-            vm((blocks // 2, SIDE, SIDE, SIDE, NB, 128), f32),
-            vm((blocks // 2, SIDE, SIDE, SIDE, NB, 128), f32),
-            vm((COLORS, 2, HALF, SIDE, SIDE, NB, 128), f32),
-            vm((COLORS, 2, NB, SIDE, SIDE, NB, 128), f32),
-            vm((COLORS, 2, HALF, SIDE, NB, 128), f32),
-            vm((COLORS, 2, NB, SIDE, NB, 128), f32),
-            vm((COLORS, 2, HALF, NB, 128), f32),
-            vm((COLORS, 2, NB, NB, 128), f32),
+            vm((SIDE, SIDE, SIDE, PER, rows, 128), f32),
+            vm((SIDE, SIDE, SIDE, PER, rows, 128), f32),
+            vm((COLORS, 2, SIDE, SIDE, 1, rows, 128), f32),
+            vm((COLORS, 2, SIDE, SIDE, 2, rows, 128), f32),
+            vm((COLORS, 2, SIDE, 1, rows, 128), f32),
+            vm((COLORS, 2, SIDE, 2, rows, 128), f32),
+            vm((COLORS, 2, 1, rows, 128), f32),
+            vm((COLORS, 2, 2, rows, 128), f32),
             vm(small.shape, f32),
             vm((3, 3) + small.shape[1:], f32),
             vm(small.shape, f32),
-            dma((4,)), dma((5,)), dma((5,)), dma((3, 3, 6)), dma((3, 3, 6)), dma((3, 3)), dma((3, 3)), dma((2,)), dma((2,)), dma((2,)),
+            dma((3, 4)), dma((3, 4)), dma((3, 4)), dma((3, 3, 6)), dma((3, 3, 6)), dma((3, 3)), dma((3, 3)), dma((4,)), dma((4,)), dma((3,)),
         ],
         compiler_params=pltpu.CompilerParams(collective_id=1, has_side_effects=True, vmem_limit_bytes=62 * 1024 * 1024),
         name='reduce_grads',
@@ -395,13 +452,17 @@
     return jnp.sum(value.reshape(value.shape[0] // 8, 8, value.shape[1]), axis=0)
 
 
-def wide(ref, first, count):
+def wide(ref, group):
+    return jnp.concatenate([ref[group, j] for j in range(GROUP)], axis=1)
+
+
+def flat(ref, first, count):
     return jnp.concatenate([ref[first + j] for j in range(count)], axis=1)
 
 
-def add_blocks(ref, first, value):
-    for j in range(value.shape[1] // LANES):
-        ref[first + j] += value[:, j * LANES:(j + 1) * LANES]
+def add_blocks(ref, group, value):
+    for j in range(GROUP):
+        ref[group, j] += value[:, j * LANES:(j + 1) * LANES]
 
 
 def norm_stats(value):
@@ -456,14 +517,16 @@
 
         @pl.loop(0, chips)
         def _(i):
-            pltpu.make_async_copy(w_hbm.at[:, i], w.at[:, pl.ds(i * NB, NB), :], wsem).start()
+            for r in range(GROUP):
+                pltpu.make_async_copy(w_hbm.at[i, :, pl.ds(r * NB, NB)], w.at[:, r, pl.ds(i * NB, NB)], wsem).start()
 
         own.start()
         oth.start()
 
-        @pl.loop(0, 60)
+        @pl.loop(0, 2 * PER)
         def _(i):
-            acc[i] = jnp.zeros((640, LANES), F32)
+            for r in range(GROUP):
+                acc[i, r] = jnp.zeros((640, LANES), F32)
 
         dtab[...] = jnp.zeros_like(dtab)
         dsum[...] = jnp.zeros_like(dsum)
@@ -473,14 +536,16 @@
 
         @pl.loop(0, chips)
         def _(i):
-            pltpu.make_async_copy(w_hbm.at[:, i], w.at[:, pl.ds(i * NB, NB), :], wsem).wait()
+            for r in range(GROUP):
+                pltpu.make_async_copy(w_hbm.at[i, :, pl.ds(r * NB, NB)], w.at[:, r, pl.ds(i * NB, NB)], wsem).wait()
 
         own.wait()
         oth.wait()
 
-        @pl.loop(0, 15)
+        @pl.loop(0, 3)
         def _(n):
-            wt[n] = w[n].T
+            for r in range(GROUP):
+                wt[n * GROUP + r] = w[n, r].T
 
     def grad_rows():
         return gbuf[pl.ds(step * STEP_SEQS, STEP_SEQS)].reshape(TOK, 640)
@@ -557,8 +622,8 @@
             otb[t, :, rows] = outb
             dqkv[t, rows] = outb.T
 
-    w_out = wide(w, 15, TILES)
-    x1[...] = e_s[...] + mm(wide(dqkv, 0, TILES), w_out) + vec_ref[5:6]
+    w_out = wide(w, 3)
+    x1[...] = e_s[...] + mm(flat(dqkv, 0, TILES), w_out) + vec_ref[5:6]
 
     @pl.loop(0, TOK // 128)
     def _(r):
@@ -573,18 +638,18 @@
     @pl.loop(0, 4)
     def _(c):
         g = grad_rows()
-        w_up = wide(w, 20 + TILES * c, TILES)
+        w_up = wide(w, 4 + c)
         u = mm(nm[...], w_up) + bup_ref[c]
         a, slope = gelu_pair(u)
         ab = a.astype(BF16)
-        w_down = wide(w, 40 + TILES * c, TILES)
+        w_down = wide(w, 8 + c)
         du = mm_t(g, w_down) * slope
         dbup[c] += fold8(du)
         dub = du.astype(BF16)
         y_s[...] += mm(ab, w_down)
         dnm[...] += mm_t(dub, w_up)
-        add_blocks(acc, 40 + TILES * c, mm(ab.T, g))
-        add_blocks(acc, 20 + TILES * c, mm(nmt[...], dub))
+        add_blocks(acc, 8 + c, mm(ab.T, g))
+        add_blocks(acc, 4 + c, mm(nmt[...], dub))
 
     @pl.loop(0, TOK // 128)
     def _(r):
@@ -613,8 +678,8 @@
         nm[rows] = d_r.astype(BF16)
 
     d_rb = nm[...]
-    add_blocks(acc, 15, mm(otb[...].reshape(640, TOK), d_rb))
-    d_o = mm(wide(w, 15, TILES), d_rb.T)
+    add_blocks(acc, 3, mm(otb[...].reshape(640, TOK), d_rb))
+    d_o = mm(wide(w, 3), d_rb.T)
     for t in range(TILES):
         dot_s[t] = d_o[t * LANES:(t + 1) * LANES]
 
@@ -662,8 +727,8 @@
             dqkv[2 * TILES + t, rows] = dv.astype(BF16)
 
     for kind in range(3):
-        add_blocks(acc, kind * TILES, mm(ht[...], wide(dqkv, kind * TILES, TILES)))
-    dnm[...] = mm(wide(dqkv, 0, 15), wt[...].reshape(1920, 640))
+        add_blocks(acc, kind, mm(ht[...], flat(dqkv, kind * TILES, TILES)))
+    dnm[...] = mm(flat(dqkv, 0, 15), wt[...].reshape(1920, 640))
 
     @pl.loop(0, TOK // 128)
     def _(r):
@@ -681,11 +746,13 @@
     def _():
         @pl.loop(0, chips)
         def _(i):
-            pltpu.make_async_copy(acc.at[:, pl.ds(i * NB, NB), :], grads.at[:, i], osem).start()
+            for r in range(GROUP):
+                pltpu.make_async_copy(acc.at[:, r, pl.ds(i * NB, NB)], grads.at[i, :, pl.ds(r * NB, NB)], osem).start()
 
         @pl.loop(0, chips)
         def _(i):
-            pltpu.make_async_copy(acc.at[:, pl.ds(i * NB, NB), :], grads.at[:, i], osem).wait()
+            for r in range(GROUP):
+                pltpu.make_async_copy(acc.at[:, r, pl.ds(i * NB, NB)], grads.at[i, :, pl.ds(r * NB, NB)], osem).wait()
 
 
 def layer_call(tok, keep, mask, emb, vecs, bqkv, bup, cos, sin, cosn, sinn, w_hbm, g_own, g_oth):
@@ -699,7 +766,7 @@
     out_shape = (
         jax.ShapeDtypeStruct((SEQS, 128, 640), BF16),
         jax.ShapeDtypeStruct((SEQS, 128, 640), BF16),
-        jax.ShapeDtypeStruct((60, 64, NB, LANES), F32),
+        jax.ShapeDtypeStruct((64, 2 * PER, GROUP * NB, LANES), F32),
         jax.ShapeDtypeStruct((64, 640), F32),
         jax.ShapeDtypeStruct((6, 8, 640), F32),
         jax.ShapeDtypeStruct((TILES, LANES, LANES), F32),
@@ -715,7 +782,7 @@
     halves = (STEP_SEQS, TILES, LANES, SEQ)
     flipped = (STEP_SEQS, TILES, SEQ, LANES)
     scratch = [
-        vm((60, 640, LANES), BF16), vm((15, LANES, 640), BF16), vm((60, 640, LANES), F32), vm((SEQS, 2, 128, 640), BF16),
+        vm((2 * PER, GROUP, 640, LANES), BF16), vm((15, LANES, 640), BF16), vm((2 * PER, GROUP, 640, LANES), F32), vm((SEQS, 2, 128, 640), BF16),
         vm((TOK, 640), F32), vm((640, TOK), BF16),
         vm(halves, BF16), vm(halves, BF16), vm(halves, BF16), vm(flipped, BF16), vm(flipped, BF16), vm(flipped, BF16),
         vm((STEP_SEQS, 20, SEQ, SEQ), BF16), vm(halves, F32), vm((TILES, LANES, TOK), BF16),
@@ -773,7 +840,7 @@
             w_down.reshape(4, NB, 5, 128).transpose(0, 2, 1, 3).reshape(20, NB, 128),
         ], axis=0)
         s_loc = jnp.pad(jnp.concatenate([layer_vecs.reshape(-1), b_up]), (0, 1024 - 130)).reshape(8, 128)
-        w_all, s_all, g_oth, t_oth = gather_all(w_loc, s_loc, grad_out, tokens)
+        w_all, s_all, g_oth, t_oth = gather_all(w_loc.reshape(2 * PER, GROUP * NB, 128), s_loc, grad_out, tokens)
         s_flat = s_all.reshape(chips, 1024)
         vecs_all = s_flat[:, :90].reshape(chips, 9, NB).transpose(1, 0, 2).reshape(9, width)
         up_b = s_flat[:, 90:130].reshape(chips, 4, NB).transpose(1, 0, 2).reshape(-1)
@@ -783,13 +850,14 @@
         positions = jnp.concatenate([cp * seq_loc + jnp.arange(seq_loc), (1 - cp) * seq_loc + jnp.arange(seq_loc)])
         tok, keep, mask, emb, bqkv, cos, sin, cosn, sinn = prepare(tok_full, len_own, positions, embed_table, vecs_all)
         y_own, y_oth, g_all, dtab, dsum, dbq, dbkv, dbup = layer_call(
-            tok, keep, mask, emb, vecs_all, bqkv, up_b.reshape(4, 1, 640), cos, sin, cosn, sinn, w_all.reshape(60, chips, NB, 128), grad_out, g_oth)
+            tok, keep, mask, emb, vecs_all, bqkv, up_b.reshape(4, 1, 640), cos, sin, cosn, sinn, w_all.reshape(chips, 2 * PER, GROUP * NB, 128), grad_out, g_oth)
         rowsum = jnp.sum(dsum, axis=1)
         d_bq = jnp.sum(dbq, axis=2).reshape(1, width)
         d_bkv = jnp.sum(dbkv, axis=2).reshape(2, width)
         small = jnp.concatenate([dtab[:vocab].reshape(-1), rowsum[:2].reshape(-1), d_bq.reshape(-1), d_bkv.reshape(-1), rowsum[2:].reshape(-1), jnp.sum(dbup, axis=1).reshape(-1)])
         small = jnp.pad(small, (0, 2 * SMALL_ROWS * 128 - small.shape[0])).reshape(2, SMALL_ROWS, 128)
-        g_red, s_red, y_recv = reduce_all(g_all.reshape(60, SIDE, SIDE, SIDE, NB, 128), small, y_oth)
+        g_red, s_red, y_recv = reduce_all(g_all.reshape(SIDE, SIDE, SIDE, 2 * PER, GROUP * NB, 128), small, y_oth)
+        g_red = g_red.reshape(60, NB, 128)
         out_full = jnp.where(cp == 0, jnp.concatenate([y_own, y_recv], axis=0), jnp.concatenate([y_recv, y_own], axis=0))
         s_flat = s_red.reshape(-1)
         n_tab = vocab * width

time: 346 us -> 327 us (0.945)
  Pallas kernels: 304 us -> 283 us
  local copies, waits for them, and re-layouts: 29.5 us -> 33.7 us
    pallas_call x2, Pallas kernels: 126 us -> 106 us  [the longest x1 57.5 us: reduce_all(): pl.pallas_call(reduce_kernel, out_shape=(jax.ShapeDtypeStruct((units, row...]
where the time goes in v4:
time: 327 us; the launch traced here: 326 us
  Pallas kernels  283 us (87%)
  local copies, waits for them, and re-layouts  33.7 us (10%)
  other arithmetic  8.5 us (3%)
    pallas_call x1, Pallas kernels, layer_call(): pl.pallas_call(layer_kernel, grid=(STEPS,), out_shape=out_shape, in_specs...  177 us
    pallas_call x1, Pallas kernels, reduce_all(): pl.pallas_call(reduce_kernel, out_shape=(jax.ShapeDtypeStruct((units, row...  57.5 us
    pallas_call x1, Pallas kernels, gather_all(): pl.pallas_call(gather_kernel, out_shape=(jax.ShapeDtypeStruct((SIDE, SIDE...  48 us

profile of v4, /device:TPU:1, one launch (start us, length us, event | category | flops | bytes accessed | tf_op | source)
XLA Modules:
  0.0 326.2 jit_solution(10178164782168419329)
XLA Ops:
  0.7 0.8 constant_dynamic-slice_fusion.1
  1.5 3.1 reshape.289
  4.7 1.2 copy.40
  5.9 1.2 reshape.290
  7.3 1.1 reshape.287
  8.5 0.1 copy.42
  8.8 48.0 %gather_weights.1 = (bf16[4,4,4,12,50,128]{5,4,3,2,1,0:T(8,128)(2,1)}, f32[4,4,4,8,128]{4,3,2,1,0:T(8,128)S(1)}, bf16[8,128,640]{2,1,0:T(8,128)(2,1)S(1)}, s32[8,128]{1,0:T(8,128)S(1)}) custom-call(bf16[12,50,128]{2,1,0:T(8,128)(2,1)S(1)} %reshape.293.w_loc, f32[8,128]{1,0:T(8,128)S(1)} %fusion.3.s_loc, bf16[16,128,640]{2,1,0:T(8,128)(2,1)S(1)} %copy-done, ...), custom_call_target="tpu_custom_call" | custom-call | tf_op jit(solution)/shard_map/gather_weights/pallas_call | solution.py:186
  56.9 1.0 copy-done.1
  58.0 0.1 convert_reduce_fusion
  58.3 1.3 broadcast_in_dim.42.keep_ref
  59.6 1.4 broadcast_in_dim.44.mask_ref
  61.0 0.1 multiply_sine_fusion
  61.1 0.8 copy.50.sinn_ref
  61.9 0.6 reshape.296.tok_ref
  62.5 0.7 copy.49.cosn_ref
  63.3 0.1 multiply_sine_fusion.1
  63.4 0.6 copy.62
  64.1 0.6 copy.63
  64.9 0.1 copy.45
  65.0 0.1 broadcast_in_dim.45
  65.1 1.3 broadcast_in_dim.46.bqkv_ref
  66.4 0.2 copy.44
  66.6 0.8 reshape.299.vec_ref
  67.5 0.1 copy.47
  67.7 0.8 reshape_reshape.12.bup_ref
  68.4 0.6 pad.13.emb_ref
  69.1 177.4 %layer.1 = (bf16[8,128,640]{2,1,0:T(8,128)(2,1)}, bf16[8,128,640]{2,1,0:T(8,128)(2,1)}, f32[64,12,50,128]{3,2,1,0:T(8,128)}, f32[64,640]{1,0:T(8,128)}, f32[6,8,...) custom-call(s32[4,1,512]{2,1,0:T(1,128)} %reshape.296.tok_ref, ...), custom_call_target="tpu_custom_call" | custom-call | tf_op jit(solution)/shard_map/layer/pallas_call | solution.py:793
  246.5 0.9 slice.60
  247.4 0.9 reduce_sum.46
  248.4 1.1 reduce_sum.47
  249.6 0.8 reduce_sum.48
  250.4 0.9 reduce_sum.49
  251.4 0.7 pad.14
  252.0 57.5 %reduce_grads.1 = (f32[12,50,128]{2,1,0:T(8,128)}, f32[2,120,128]{2,1,0:T(8,128)}, bf16[8,128,640]{2,1,0:T(8,128)(2,1)}) custom-call(f32[4,4,4,12,50,128]{5,4,3,2,1,0:T(8,128)} %bitcast.59, f32[2,120,128]{2,1,0:T(8,128)} %bitcast.67, bf16[8,128,640]{2,1,0:T(8,128)(2,1)} %get-tuple-element.34.y_oth), custom_call_target="tpu_custom_call" | custom-call | tf_op jit(solution)/shard_map/reduce_grads/pallas_call | solution.py:402
  309.5 1.0 fusion.5
  310.6 1.4 reshape.310
  311.9 0.9 copy.54
  312.8 1.8 reshape.311
  314.6 4.0 %maximum_select_fusion = bf16[16,128,640]{2,1,0:T(8,128)(2,1)} fusion(bf16[8,128,640]{2,1,0:T(8,128)(2,1)} %get-tuple-element.35, bf16[8,128,640]{2,1,0:T(8,128)(2,1)} %get-tuple-element.27, pred[]{:T(512)S(6)} %eq.14), kind=kLoop, calls=%fused_computation | loop fusion | flops 3932160 | bytes 5242881 | tf_op jit(solution)/shard_map/jit(_where)/select_n | solution.py:861
  318.6 1.6 slice.72
  320.3 0.6 reshape.312
  320.9 0.9 slice.66
  321.8 0.9 reshape.308
  322.7 0.7 copy.69
  323.4 0.7 slice.80
  324.1 0.8 slice.68
  324.9 0.6 copy.64
  325.5 0.7 constant_dynamic-slice_fusion
  (74 shorter events, 1.4 us)
Async XLA Ops:
  0.6 8.2 %copy-start.2 = (s32[16,128]{1,0:T(8,128)S(1)}, s32[16,128]{1,0:T(8,128)}, u32[]{:S(2)}) copy-start(s32[16,128]{1,0:T(8,128)} %t_own.1) | copy-start | bytes 24580
  0.6 6.5 %copy-start.4 = (bf16[40,640]{1,0:T(8,128)(2,1)S(1)}, bf16[40,640]{1,0:T(8,128)(2,1)}, u32[]{:S(2)}) copy-start(bf16[40,640]{1,0:T(8,128)(2,1)} %param.18) | copy-start | bytes 153604
  0.7 7.7 %copy-start.6 = (bf16[10,640]{1,0:T(8,128)(2,1)S(1)}, bf16[10,640]{1,0:T(8,128)(2,1)}, u32[]{:S(2)}) copy-start(bf16[10,640]{1,0:T(8,128)(2,1)} %param.15) | copy-start | bytes 38404
  0.7 8.0 %copy-start.7 = (f32[9,10]{1,0:T(8,128)S(1)}, f32[9,10]{1,0:T(8,128)}, u32[]{:S(2)}) copy-start(f32[9,10]{1,0:T(8,128)} %param.13) | copy-start | bytes 1084
  0.7 8.1 %copy-start.8 = (f32[40]{0:T(128)S(1)}, f32[40]{0:T(128)}, u32[]{:S(2)}) copy-start(f32[40]{0:T(128)} %param.17) | copy-start | bytes 484
  0.7 8.2 %copy-start = (bf16[16,128,640]{2,1,0:T(8,128)(2,1)S(1)}, bf16[16,128,640]{2,1,0:T(8,128)(2,1)}, u32[]{:S(2)}) copy-start(bf16[16,128,640]{2,1,0:T(8,128)(2,1)} %g_own.3) | copy-start | bytes 7864324
  5.9 52.2 %copy-start.9 = (s32[16]{0:T(128)S(1)}, s32[16]{0:T(128)}, u32[]{:S(2)}) copy-start(s32[16]{0:T(128)} %param.11) | copy-start | bytes 196
  56.9 1.1 copy-start.1
  59.6 8.8 %copy-start.5 = (bf16[33,640]{1,0:T(8,128)(2,1)S(1)}, bf16[33,640]{1,0:T(8,128)(2,1)}, u32[]{:S(2)}) copy-start(bf16[33,640]{1,0:T(8,128)(2,1)} %param.12) | copy-start | bytes 126724
  314.6 4.0 %copy-start.3 = (f32[2,120,128]{2,1,0:T(8,128)S(1)}, f32[2,120,128]{2,1,0:T(8,128)}, u32[]{:S(2)}) copy-start(f32[2,120,128]{2,1,0:T(8,128)} %get-tuple-element.36) | copy-start | bytes 368644

commit v5 on v4

--- a/solution.py
+++ b/solution.py
@@ -2,6 +2,7 @@
 
 import jax
 import jax.numpy as jnp
+import numpy as np
 from jax import lax
 from jax.experimental import pallas as pl
 from jax.experimental.pallas import tpu as pltpu
@@ -202,7 +203,7 @@
     )(w_loc, s_loc, grad_out, tokens)
 
 
-def reduce_kernel(g_all, small, y_oth, g_out, s_out, y_recv, held, pair, ra0, rb0, ra1, rb1, ra2, rb2, s_pair, s_slots, s_acc,
+def reduce_kernel(g_all, small, y_own, y_oth, g_out, s_out, y_full, y_hold, held, pair, ra0, rb0, ra1, rb1, ra2, rb2, s_pair, s_slots, s_acc,
                   lsem, psend, precv, ssem, rsem, s_ssem, s_rsem, osend, orecv, msem):
     cp = lax.axis_index('cp')
     me = my_coords()
@@ -233,8 +234,11 @@
             swap = push(quarter(g_all, (1 - cp) * per, color, by), quarter(pair, 0, color, by), psend.at[color, by], precv.at[color, by], mate)
             swap.start()
             swaps[color, by] = swap
-    y_swap = push(y_oth, y_recv, osend.at[3], orecv.at[3], mate)
+    y_rows = y_full.at[pl.ds(y_own.shape[0] * cp, y_own.shape[0])]
+    y_swap = push(y_oth, y_rows, osend.at[3], orecv.at[3], mate)
     y_swap.start()
+    y_in = pltpu.make_async_copy(y_own, y_hold, msem.at[3])
+    y_in.start()
 
     bufs = ((ra0, rb0), (ra1, rb1), (ra2, rb2))
 
@@ -341,6 +345,9 @@
             total = value if total is None else total + value
         s_acc[cp] = total
 
+    y_in.wait()
+    y_put = pltpu.make_async_copy(y_hold, y_rows, msem.at[4])
+    y_put.start()
     s_load.wait()
     s_swap.wait()
     s_acc[...] = s_acc[...] + s_pair[...]
@@ -388,13 +395,14 @@
     for copy in swaps.values():
         copy.wait_send()
     y_swap.wait()
+    y_put.wait()
     out_own.wait()
     s_own.wait()
     out_far.wait()
     s_far.wait()
 
 
-def reduce_all(g_all, small, y_oth):
+def reduce_all(g_all, small, y_own, y_oth):
     f32 = jnp.float32
     units, rows = g_all.shape[3:5]
     dma = pltpu.SemaphoreType.DMA
@@ -404,11 +412,12 @@
         out_shape=(
             jax.ShapeDtypeStruct((units, rows, 128), f32),
             jax.ShapeDtypeStruct(small.shape, f32),
-            jax.ShapeDtypeStruct(y_oth.shape, y_oth.dtype),
+            jax.ShapeDtypeStruct((2 * y_oth.shape[0], *y_oth.shape[1:]), y_oth.dtype),
         ),
-        in_specs=[ANY] * 3,
+        in_specs=[ANY] * 4,
         out_specs=(ANY,) * 3,
         scratch_shapes=[
+            vm(y_own.shape, y_own.dtype),
             vm((SIDE, SIDE, SIDE, PER, rows, 128), f32),
             vm((SIDE, SIDE, SIDE, PER, rows, 128), f32),
             vm((COLORS, 2, SIDE, SIDE, 1, rows, 128), f32),
@@ -420,11 +429,11 @@
             vm(small.shape, f32),
             vm((3, 3) + small.shape[1:], f32),
             vm(small.shape, f32),
-            dma((3, 4)), dma((3, 4)), dma((3, 4)), dma((3, 3, 6)), dma((3, 3, 6)), dma((3, 3)), dma((3, 3)), dma((4,)), dma((4,)), dma((3,)),
+            dma((3, 4)), dma((3, 4)), dma((3, 4)), dma((3, 3, 6)), dma((3, 3, 6)), dma((3, 3)), dma((3, 3)), dma((4,)), dma((4,)), dma((5,)),
         ],
         compiler_params=pltpu.CompilerParams(collective_id=1, has_side_effects=True, vmem_limit_bytes=62 * 1024 * 1024),
         name='reduce_grads',
-    )(g_all, small, y_oth)
+    )(g_all, small, y_own, y_oth)
 
 
 SEQS = 8
@@ -501,24 +510,44 @@
     return unturn(z, cos, -sin, groups)
 
 
-def layer_kernel(tok_ref, keep_ref, mask_ref, emb_ref, vec_ref, bqkv_ref, bup_ref, cos_ref, sin_ref, cosn_ref, sinn_ref,
+def layer_kernel(tok_ref, keep_in, mask_in, emb_ref, vec_ref, bup_ref, cos_ref, sin_ref, cosn_ref, sinn_ref,
                  w_hbm, g_own, g_oth,
                  y_own, y_oth, grads, dtab, dsum, dbq, dbkv, dbup,
-                 w, wt, acc, gbuf, e_s, ht, qt, kt, vt, qn, kn, vn, pt, ot32, otb, x1, nm, nmt, y_s, dnm, dot_s, dqkv,
+                 w, wt, acc, gbuf, e_s, ht, qt, kt, vt, qn, kn, vn, pt, ot32, otb, x1, nm, nmt, y_s, dnm, dot_s, dqkv, keep_ref, mask_ref, bqkv_ref,
                  wsem, gsem, osem):
     step = pl.program_id(0)
     cp = lax.axis_index('cp')
     chips = SIDE ** 3
 
-    @pl.when(step == 0)
-    def _():
-        own = pltpu.make_async_copy(g_own.at[pl.ds(cp * SEQS, SEQS)], gbuf.at[:, 0], gsem.at[0])
-        oth = pltpu.make_async_copy(g_oth, gbuf.at[:, 1], gsem.at[1])
-
+    def weights(act, first, count):
         @pl.loop(0, chips)
         def _(i):
             for r in range(GROUP):
-                pltpu.make_async_copy(w_hbm.at[i, :, pl.ds(r * NB, NB)], w.at[:, r, pl.ds(i * NB, NB)], wsem).start()
+                src = w_hbm.at[i, pl.ds(first, count), pl.ds(r * NB, NB)]
+                dst = w.at[pl.ds(first, count), r, pl.ds(i * NB, NB)]
+                getattr(pltpu.make_async_copy(src, dst, wsem.at[first // 4]), act)()
+
+    def ship(act, first, count):
+        @pl.loop(0, chips)
+        def _(i):
+            for r in range(GROUP):
+                src = acc.at[pl.ds(first, count), r, pl.ds(i * NB, NB)]
+                dst = grads.at[i, pl.ds(first, count), pl.ds(r * NB, NB)]
+                getattr(pltpu.make_async_copy(src, dst, osem.at[first // 4]), act)()
+
+    def grad_loads():
+        own = pltpu.make_async_copy(g_own.at[pl.ds(cp * SEQS, SEQS)], gbuf.at[:, 0], gsem.at[0])
+        oth = pltpu.make_async_copy(g_oth, gbuf.at[:, 1], gsem.at[1])
+        return own, oth
+
+    keep_ref[...] = jnp.broadcast_to(keep_in[0], (LANES, TOK)).T
+    mask_ref[...] = jnp.broadcast_to(mask_in[0], (LANES, TOK)).T
+
+    @pl.when(step == 0)
+    def _():
+        own, oth = grad_loads()
+        weights('start', 0, 4)
+        weights('start', 4, 8)
 
         own.start()
         oth.start()
@@ -534,13 +563,13 @@
         dbkv[...] = jnp.zeros_like(dbkv)
         dbup[...] = jnp.zeros_like(dbup)
 
-        @pl.loop(0, chips)
-        def _(i):
-            for r in range(GROUP):
-                pltpu.make_async_copy(w_hbm.at[i, :, pl.ds(r * NB, NB)], w.at[:, r, pl.ds(i * NB, NB)], wsem).wait()
-
-        own.wait()
-        oth.wait()
+        for kind in range(3):
+            for t in range(TILES):
+                first = (kind * TILES + t) * LANES
+                row = vec_ref[2 + kind:3 + kind, t * LANES:(t + 1) * LANES]
+                bqkv_ref[first:first + LANES] = jnp.broadcast_to(row, (LANES, LANES)).T
+
+        weights('wait', 0, 4)
 
         @pl.loop(0, 3)
         def _(n):
@@ -554,7 +583,7 @@
     one_hot = jnp.where(vocab == tok_ref[0], 1.0, 0.0).astype(BF16)
     e_s[...] = lax.dot_general(one_hot, emb_ref[...], (((0,), (0,)), ((), ())), preferred_element_type=F32)
 
-    @pl.loop(0, TOK // 128)
+    @pl.loop(0, TOK // 128, unroll=2)
     def _(r):
         rows = pl.ds(pl.multiple_of(r * 128, 128), 128)
         keep = jnp.concatenate([keep_ref[rows]] * TILES, axis=1)
@@ -565,7 +594,7 @@
 
     ht[...] = nm[...].T
 
-    cos, sin = cos_ref[...], sin_ref[...]
+    cos, sin = cos_ref[cp], sin_ref[cp]
     for kind, (t_ref, n_ref) in enumerate(((qt, qn), (kt, kn), (vt, vn))):
         z = mm(wt[kind * TILES:(kind + 1) * TILES].reshape(640, 640), ht[...])
         bias = bqkv_ref[kind * 640:(kind + 1) * 640]
@@ -625,7 +654,7 @@
     w_out = wide(w, 3)
     x1[...] = e_s[...] + mm(flat(dqkv, 0, TILES), w_out) + vec_ref[5:6]
 
-    @pl.loop(0, TOK // 128)
+    @pl.loop(0, TOK // 128, unroll=2)
     def _(r):
         rows = pl.ds(pl.multiple_of(r * 128, 128), 128)
         xhat, _ = norm_stats(x1[rows])
@@ -634,6 +663,12 @@
     nmt[...] = nm[...].T
     y_s[...] = jnp.zeros_like(y_s)
     dnm[...] = jnp.zeros_like(dnm)
+
+    @pl.when(step == 0)
+    def _():
+        weights('wait', 4, 8)
+        for copy in grad_loads():
+            copy.wait()
 
     @pl.loop(0, 4)
     def _(c):
@@ -651,31 +686,27 @@
         add_blocks(acc, 8 + c, mm(ab.T, g))
         add_blocks(acc, 4 + c, mm(nmt[...], dub))
 
-    @pl.loop(0, TOK // 128)
-    def _(r):
-        rows = pl.ds(pl.multiple_of(r * 128, 128), 128)
-        x = x1[rows]
-        out = (x + y_s[rows] + vec_ref[8:9]).astype(BF16)
-        seq = r // 2
-
-        @pl.when(lax.rem(r, 2) == 0)
-        def _():
-            y_own[seq] = out
-
-        @pl.when(lax.rem(r, 2) == 1)
-        def _():
-            y_oth[seq] = out
-
-        xhat, rstd = norm_stats(x)
-        d_n = dnm[rows]
-        g32 = gbuf[step * STEP_SEQS + seq, lax.rem(r, 2)].astype(F32)
-        dsum[3] += fold8(d_n * xhat)
-        dsum[4] += fold8(d_n)
-        d_r = g32 + norm_back(d_n, vec_ref[6:7], xhat, rstd)
-        dsum[2] += fold8(d_r)
-        dsum[5] += fold8(g32)
-        y_s[rows] = d_r
-        nm[rows] = d_r.astype(BF16)
+    @pl.when(step == STEPS - 1)
+    def _():
+        ship('start', 4, 8)
+
+    @pl.loop(0, STEP_SEQS)
+    def _(seq):
+        for part in range(2):
+            rows = pl.ds(pl.multiple_of(seq * SEQ, SEQ) + part * 128, 128)
+            x = x1[rows]
+            out = (x + y_s[rows] + vec_ref[8:9]).astype(BF16)
+            (y_own, y_oth)[part][seq] = out
+            xhat, rstd = norm_stats(x)
+            d_n = dnm[rows]
+            g32 = gbuf[step * STEP_SEQS + seq, part].astype(F32)
+            dsum[3] += fold8(d_n * xhat)
+            dsum[4] += fold8(d_n)
+            d_r = g32 + norm_back(d_n, vec_ref[6:7], xhat, rstd)
+            dsum[2] += fold8(d_r)
+            dsum[5] += fold8(g32)
+            y_s[rows] = d_r
+            nm[rows] = d_r.astype(BF16)
 
     d_rb = nm[...]
     add_blocks(acc, 3, mm(otb[...].reshape(640, TOK), d_rb))
@@ -720,7 +751,7 @@
             dv = mm(p_wide, stack(d_ot.astype(BF16).T))
             low = lax.rem(lax.broadcasted_iota(jnp.int32, (SEQ, LANES), 1), HEAD) < HEAD // 2
             other = jnp.where(low, pltpu.roll(dk, LANES - HEAD // 2, 1), pltpu.roll(dk, HEAD // 2, 1))
-            dk = dk * cosn_ref[...] + other * sinn_ref[...]
+            dk = dk * cosn_ref[cp] + other * sinn_ref[cp]
             dbkv[0, t] += fold8(dk)
             dbkv[1, t] += fold8(dv)
             dqkv[TILES + t, rows] = dk.astype(BF16)
@@ -730,7 +761,7 @@
         add_blocks(acc, kind, mm(ht[...], flat(dqkv, kind * TILES, TILES)))
     dnm[...] = mm(flat(dqkv, 0, 15), wt[...].reshape(1920, 640))
 
-    @pl.loop(0, TOK // 128)
+    @pl.loop(0, TOK // 128, unroll=2)
     def _(r):
         rows = pl.ds(pl.multiple_of(r * 128, 128), 128)
         xhat, rstd = norm_stats(e_s[rows])
@@ -744,18 +775,12 @@
 
     @pl.when(step == STEPS - 1)
     def _():
-        @pl.loop(0, chips)
-        def _(i):
-            for r in range(GROUP):
-                pltpu.make_async_copy(acc.at[:, r, pl.ds(i * NB, NB)], grads.at[i, :, pl.ds(r * NB, NB)], osem).start()
-
-        @pl.loop(0, chips)
-        def _(i):
-            for r in range(GROUP):
-                pltpu.make_async_copy(acc.at[:, r, pl.ds(i * NB, NB)], grads.at[i, :, pl.ds(r * NB, NB)], osem).wait()
-
-
-def layer_call(tok, keep, mask, emb, vecs, bqkv, bup, cos, sin, cosn, sinn, w_hbm, g_own, g_oth):
+        ship('start', 0, 4)
+        ship('wait', 4, 8)
+        ship('wait', 0, 4)
+
+
+def layer_call(tok, keep, mask, emb, vecs, bup, cos, sin, cosn, sinn, w_hbm, g_own, g_oth):
     vm = pltpu.VMEM
     dma = pltpu.SemaphoreType.DMA
 
@@ -776,9 +801,9 @@
     out_specs = (pair, pair, ANY) + tuple(whole(o.shape) for o in out_shape[3:])
     in_specs = [
         pl.BlockSpec((1, 1, TOK), lambda i: (i, 0, 0)),
-        pl.BlockSpec((TOK, LANES), lambda i: (i, 0)),
-        pl.BlockSpec((TOK, LANES), lambda i: (i, 0)),
-    ] + [whole(a.shape) for a in (emb, vecs, bqkv, bup, cos, sin, cosn, sinn)] + [ANY] * 3
+        pl.BlockSpec((1, 1, TOK), lambda i: (i, 0, 0)),
+        pl.BlockSpec((1, 1, TOK), lambda i: (i, 0, 0)),
+    ] + [whole(a.shape) for a in (emb, vecs, bup, cos, sin, cosn, sinn)] + [ANY] * 3
     halves = (STEP_SEQS, TILES, LANES, SEQ)
     flipped = (STEP_SEQS, TILES, SEQ, LANES)
     scratch = [
@@ -787,8 +812,8 @@
         vm(halves, BF16), vm(halves, BF16), vm(halves, BF16), vm(flipped, BF16), vm(flipped, BF16), vm(flipped, BF16),
         vm((STEP_SEQS, 20, SEQ, SEQ), BF16), vm(halves, F32), vm((TILES, LANES, TOK), BF16),
         vm((TOK, 640), F32), vm((TOK, 640), BF16), vm((640, TOK), BF16), vm((TOK, 640), F32), vm((TOK, 640), F32),
-        vm((TILES, LANES, TOK), F32), vm((15, TOK, LANES), BF16),
-        dma, dma((2,)), dma,
+        vm((TILES, LANES, TOK), F32), vm((15, TOK, LANES), BF16), vm((TOK, LANES), F32), vm((TOK, LANES), F32), vm((1920, LANES), F32),
+        dma((2,)), dma((2,)), dma((2,)),
     ]
     return pl.pallas_call(
         layer_kernel,
@@ -799,7 +824,7 @@
         scratch_shapes=scratch,
         compiler_params=pltpu.CompilerParams(dimension_semantics=('arbitrary',), vmem_limit_bytes=67043328),
         name='layer',
-    )(tok, keep, mask, emb, vecs, bqkv, bup, cos, sin, cosn, sinn, w_hbm, g_own, g_oth)
+    )(tok, keep, mask, emb, vecs, bup, cos, sin, cosn, sinn, w_hbm, g_own, g_oth)
 
 
 def prepare(tokens, lengths, positions, embed_table, vecs_all):
@@ -809,17 +834,24 @@
     mask_count = jnp.sum(is_mask.astype(jnp.int32), axis=1)
     drop_scale = (1.0 - TRAIN_RATIO) / (1.0 - mask_count.astype(F32) / lengths.astype(F32))
     keep = jnp.where(is_mask | jnp.logical_not(tok_valid), 0.0, drop_scale[:, None])
-    keep = jnp.broadcast_to(keep.reshape(-1, 1), (n_seq * seq_len, LANES))
-    mask = jnp.broadcast_to(jnp.where(tok_valid, 0.0, NEG_BIG).reshape(-1, 1), (n_seq * seq_len, LANES)).astype(F32)
+    mask = jnp.where(tok_valid, 0.0, NEG_BIG).astype(F32)
     emb = jnp.pad(embed_table, ((0, 64 - embed_table.shape[0]), (0, 0)))
-    bqkv = jnp.broadcast_to(vecs_all[2:5].reshape(-1, 1), (1920, LANES))
-    inv_freq = 1.0 / (ROPE_BASE ** (jnp.arange(0, HEAD, 2, dtype=F32) / HEAD))
-    angles = positions.astype(F32)[:, None] * inv_freq[None, :]
-    cos, sin = jnp.cos(angles), jnp.sin(angles)
-    cos_t, sin_t = jnp.tile(cos.T, (1, STEP_SEQS)), jnp.tile(sin.T, (1, STEP_SEQS))
-    cos_n = jnp.tile(cos, (1, 8))
-    sin_n = jnp.tile(jnp.concatenate([sin, -sin], axis=1), (1, 4))
-    return tokens.reshape(STEPS, 1, TOK), keep, mask, emb, bqkv, cos_t, sin_t, cos_n, sin_n
+    rows = [x.reshape(STEPS, 1, TOK) for x in (tokens, keep, mask)]
+    return (*rows, emb, *rope_tables(seq_len // 2))
+
+
+def rope_tables(half):
+    inv_freq = (1.0 / (np.float32(ROPE_BASE) ** (np.arange(0, HEAD, 2, dtype=np.float32) / np.float32(HEAD)))).astype(np.float32)
+    tables = []
+    for cp in range(2):
+        positions = np.concatenate([np.arange(half) + cp * half, np.arange(half) + (1 - cp) * half]).astype(np.float32)
+        angles = (positions[:, None] * inv_freq[None, :]).astype(np.float64)
+        cos, sin = np.cos(angles), np.sin(angles)
+        tables.append((
+            np.tile(cos.T, (1, STEP_SEQS)), np.tile(sin.T, (1, STEP_SEQS)),
+            np.tile(cos, (1, 8)), np.tile(np.concatenate([sin, -sin], axis=1), (1, 4)),
+        ))
+    return tuple(jnp.asarray(np.stack(pair), F32) for pair in zip(*tables))
 
 
 def solution(mesh):
@@ -848,17 +880,16 @@
         tok_full = jnp.concatenate([lax.dynamic_slice_in_dim(tokens, start, half, 0), t_oth], axis=1)
         len_own = lax.dynamic_slice_in_dim(lengths, start, half, 0)
         positions = jnp.concatenate([cp * seq_loc + jnp.arange(seq_loc), (1 - cp) * seq_loc + jnp.arange(seq_loc)])
-        tok, keep, mask, emb, bqkv, cos, sin, cosn, sinn = prepare(tok_full, len_own, positions, embed_table, vecs_all)
+        tok, keep, mask, emb, cos, sin, cosn, sinn = prepare(tok_full, len_own, positions, embed_table, vecs_all)
         y_own, y_oth, g_all, dtab, dsum, dbq, dbkv, dbup = layer_call(
-            tok, keep, mask, emb, vecs_all, bqkv, up_b.reshape(4, 1, 640), cos, sin, cosn, sinn, w_all.reshape(chips, 2 * PER, GROUP * NB, 128), grad_out, g_oth)
+            tok, keep, mask, emb, vecs_all, up_b.reshape(4, 1, 640), cos, sin, cosn, sinn, w_all.reshape(chips, 2 * PER, GROUP * NB, 128), grad_out, g_oth)
         rowsum = jnp.sum(dsum, axis=1)
         d_bq = jnp.sum(dbq, axis=2).reshape(1, width)
         d_bkv = jnp.sum(dbkv, axis=2).reshape(2, width)
         small = jnp.concatenate([dtab[:vocab].reshape(-1), rowsum[:2].reshape(-1), d_bq.reshape(-1), d_bkv.reshape(-1), rowsum[2:].reshape(-1), jnp.sum(dbup, axis=1).reshape(-1)])
         small = jnp.pad(small, (0, 2 * SMALL_ROWS * 128 - small.shape[0])).reshape(2, SMALL_ROWS, 128)
-        g_red, s_red, y_recv = reduce_all(g_all.reshape(SIDE, SIDE, SIDE, 2 * PER, GROUP * NB, 128), small, y_oth)
+        g_red, s_red, out_full = reduce_all(g_all.reshape(SIDE, SIDE, SIDE, 2 * PER, GROUP * NB, 128), small, y_own, y_oth)
         g_red = g_red.reshape(60, NB, 128)
-        out_full = jnp.where(cp == 0, jnp.concatenate([y_own, y_recv], axis=0), jnp.concatenate([y_recv, y_own], axis=0))
         s_flat = s_red.reshape(-1)
         n_tab = vocab * width
         d_embed = s_flat[:n_tab].reshape(vocab, width)

time: 327 us -> 312 us (0.954)
  Pallas kernels: 283 us -> 274 us
  other arithmetic: 8.5 us -> 4.77 us
    pallas_call x1, Pallas kernels: 177 us -> 168 us  [layer_call(): pl.pallas_call(layer_kernel, grid=(STEPS,), out_shape=out_shape, in_specs...]
    broadcast_in_dim x4 -> x3, local copies, waits for them, and re-layouts: 4.07 us -> 0.19 us  [prepare(): jnp.where(is_mask | jnp.logical_not(tok_valid), 0.0, drop_scale[:, None])]
    select_n x1, other arithmetic: 3.97 us -> 0.62 us  [prepare(): mask = jnp.where(tok_valid, 0.0, NEG_BIG).astype(F32)]
where the time goes in v5:
time: 312 us; the launch traced here: 311 us
  Pallas kernels  274 us (88%)
  local copies, waits for them, and re-layouts  30.9 us (10%)
  other arithmetic  4.77 us (2%)
    pallas_call x1, Pallas kernels, layer_call(): pl.pallas_call(layer_kernel, grid=(STEPS,), out_shape=out_shape, in_specs...  168 us
    pallas_call x1, Pallas kernels, reduce_all(): pl.pallas_call(reduce_kernel, out_shape=(jax.ShapeDtypeStruct((units, row...  57.8 us
    pallas_call x1, Pallas kernels, gather_all(): pl.pallas_call(gather_kernel, out_shape=(jax.ShapeDtypeStruct((SIDE, SIDE...  48.1 us

profile of v5, /device:TPU:1, one launch (start us, length us, event | category | flops | bytes accessed | tf_op | source)
XLA Modules:
  0.0 310.9 jit_solution(4325821013139413990)
XLA Ops:
  0.6 0.7 constant_dynamic-slice_fusion.1
  1.3 3.1 %reshape.230 = bf16[10,64,4,10]{3,2,1,0:T(4,128)(2,1)} reshape(bf16[10,2560]{1,0:T(8,128)(2,1)} %param.20) | data formatting | bytes 102400 | tf_op jit(solution)/shard_map/reshape | solution.py:871
  4.5 1.4 copy.41
  5.9 1.2 reshape.231
  7.1 0.1 reshape.232
  7.3 1.1 reshape.228
  8.4 0.8 reshape.229
  9.2 0.1 copy.43
  9.4 0.1 reshape.235
  9.5 0.1 fusion.s_loc
  9.6 48.1 %gather_weights.1 = (bf16[4,4,4,12,50,128]{5,4,3,2,1,0:T(8,128)(2,1)}, f32[4,4,4,8,128]{4,3,2,1,0:T(8,128)S(1)}, bf16[8,128,640]{2,1,0:T(8,128)(2,1)S(1)}, s32[8,128]{1,0:T(8,128)S(1)}) custom-call(bf16[12,50,128]{2,1,0:T(8,128)(2,1)S(1)} %reshape.234.w_loc, f32[8,128]{1,0:T(8,128)S(1)} %fusion.s_loc, bf16[16,128,640]{2,1,0:T(8,128)(2,1)S(1)} %copy-done, ...), custom_call_target="tpu_custom_call" | custom-call | tf_op jit(solution)/shard_map/gather_weights/pallas_call | solution.py:187
  57.6 1.0 copy-done.1
  58.7 0.1 convert_reduce_fusion
  58.8 0.1 subtract_divide_fusion
  58.9 0.1 broadcast_in_dim.26
  59.0 0.1 broadcast_in_dim.27
  59.1 0.1 lt.46
  59.3 0.6 compare_select_fusion
  60.0 0.1 copy.55
  60.1 0.2 copy.45
  60.3 0.8 reshape.240.vec_ref
  61.1 0.1 slice.71
  61.3 0.1 copy.47
  61.4 0.7 reshape_reshape.12.bup_ref
  62.2 0.6 pad.13.emb_ref
  62.8 168.3 %layer.1 = (bf16[8,128,640]{2,1,0:T(8,128)(2,1)}, bf16[8,128,640]{2,1,0:T(8,128)(2,1)}, f32[64,12,50,128]{3,2,1,0:T(8,128)}, f32[64,640]{1,0:T(8,128)}, f32[6,8,...) custom-call(s32[4,1,512]{2,1,0:T(1,128)} %copy-done.5, ...), custom_call_target="tpu_custom_call" | custom-call | tf_op jit(solution)/shard_map/layer/pallas_call | solution.py:818
  231.1 0.9 slice.55
  232.0 0.9 reduce_sum.46
  233.0 1.1 reduce_sum.47
  234.2 0.8 reduce_sum.48
  235.1 0.9 reduce_sum.49
  236.0 0.7 pad.14
  236.7 57.8 %reduce_grads.1 = (f32[12,50,128]{2,1,0:T(8,128)}, f32[2,120,128]{2,1,0:T(8,128)}, bf16[16,128,640]{2,1,0:T(8,128)(2,1)}) custom-call(f32[4,4,4,12,50,128]{5,4,3,2,1,0:T(8,128)} %bitcast.50, f32[2,120,128]{2,1,0:T(8,128)} %bitcast.56, bf16[8,128,640]{2,1,0:T(8,128)(2,1)} %get-tuple-element.33.y_own, bf16[8,128,640]{2,1,0:T(8,128)(2,1)} %get-tuple-element.34.y_oth), custom_call_target="tpu_custom_call" | custom-call | tf_op jit(solution)/shard_map/reduce_grads/pallas_call | solution.py:410
  294.5 1.0 fusion.1
  295.5 1.4 reshape.251
  296.9 0.9 copy.52
  297.8 1.8 reshape.252
  299.6 2.8 slice.67
  302.4 1.1 slice.76
  303.5 0.6 reshape.253
  304.1 0.9 slice.61
  305.0 0.9 reshape.249
  306.0 0.7 copy.64
  306.7 0.7 slice.74
  307.3 0.8 slice.63
  308.1 0.6 copy.59
  308.7 0.7 constant_dynamic-slice_fusion
  309.4 1.5 copy.72
  (64 shorter events, 0.8 us)
Async XLA Ops:
  0.6 6.5 %copy-start.6 = (bf16[40,640]{1,0:T(8,128)(2,1)S(1)}, bf16[40,640]{1,0:T(8,128)(2,1)}, u32[]{:S(2)}) copy-start(bf16[40,640]{1,0:T(8,128)(2,1)} %param.22) | copy-start | bytes 153604
  4.5 5.1 %copy-start = (bf16[16,128,640]{2,1,0:T(8,128)(2,1)S(1)}, bf16[16,128,640]{2,1,0:T(8,128)(2,1)}, u32[]{:S(2)}) copy-start(bf16[16,128,640]{2,1,0:T(8,128)(2,1)} %g_own.3) | copy-start | bytes 7864324
  5.9 3.5 %copy-start.8 = (f32[9,10]{1,0:T(8,128)S(1)}, f32[9,10]{1,0:T(8,128)}, u32[]{:S(2)}) copy-start(f32[9,10]{1,0:T(8,128)} %param.17) | copy-start | bytes 1084
  5.9 3.6 %copy-start.9 = (f32[40]{0:T(128)S(1)}, f32[40]{0:T(128)}, u32[]{:S(2)}) copy-start(f32[40]{0:T(128)} %param.21) | copy-start | bytes 484
  5.9 3.7 %copy-start.2 = (s32[16,128]{1,0:T(8,128)S(1)}, s32[16,128]{1,0:T(8,128)}, u32[]{:S(2)}) copy-start(s32[16,128]{1,0:T(8,128)} %t_own.1) | copy-start | bytes 24580
  9.3 49.5 %copy-start.10 = (s32[16]{0:T(128)S(1)}, s32[16]{0:T(128)}, u32[]{:S(2)}) copy-start(s32[16]{0:T(128)} %param.15) | copy-start | bytes 196
  57.6 1.1 copy-start.1
  58.7 3.5 %copy-start.7 = (bf16[33,640]{1,0:T(8,128)(2,1)S(1)}, bf16[33,640]{1,0:T(8,128)(2,1)}, u32[]{:S(2)}) copy-start(bf16[33,640]{1,0:T(8,128)(2,1)} %param.16) | copy-start | bytes 126724
  59.3 0.7 copy-start.5
  296.9 2.7 copy-start.4
  302.4 7.0 %copy-start.3 = (bf16[16,128,640]{2,1,0:T(8,128)(2,1)S(1)}, bf16[16,128,640]{2,1,0:T(8,128)(2,1)}, u32[]{:S(2)}) copy-start(bf16[16,128,640]{2,1,0:T(8,128)(2,1)} %get-tuple-element.56) | copy-start | bytes 7864324

commit v6 on v5

--- a/solution.py
+++ b/solution.py
@@ -19,6 +19,8 @@
 GROUP = 5
 PER = 6
 SMALL_ROWS = 120
+SMALL_BLOCK = 48
+VOCAB = 33
 QUARTERS = (2, 1, 3, 0)
 MESH_ID = pl.DeviceIdType.MESH
 ANY = pl.BlockSpec(memory_space=pl.ANY)
@@ -512,8 +514,8 @@
 
 def layer_kernel(tok_ref, keep_in, mask_in, emb_ref, vec_ref, bup_ref, cos_ref, sin_ref, cosn_ref, sinn_ref,
                  w_hbm, g_own, g_oth,
-                 y_own, y_oth, grads, dtab, dsum, dbq, dbkv, dbup,
-                 w, wt, acc, gbuf, e_s, ht, qt, kt, vt, qn, kn, vn, pt, ot32, otb, x1, nm, nmt, y_s, dnm, dot_s, dqkv, keep_ref, mask_ref, bqkv_ref,
+                 y_own, y_oth, grads, small,
+                 w, wt, acc, gbuf, e_s, ht, qt, kt, vt, qn, kn, vn, pt, ot32, otb, x1, nm, nmt, y_s, dnm, dot_s, dqkv, keep_ref, mask_ref, bqkv_ref, dtab, dsum, dbq, dbkv, dbup,
                  wsem, gsem, osem):
     step = pl.program_id(0)
     cp = lax.axis_index('cp')
@@ -776,6 +778,14 @@
     @pl.when(step == STEPS - 1)
     def _():
         ship('start', 0, 4)
+        for t in range(TILES):
+            lanes = slice(t * LANES, (t + 1) * LANES)
+            sums = [dsum[0, :, lanes], dsum[1, :, lanes], dbq[t].T, dbkv[0, t], dbkv[1, t]]
+            sums += [dsum[k, :, lanes] for k in range(2, 6)] + [dbup[k, :, lanes] for k in range(4)]
+            small[t, :VOCAB] = dtab[:VOCAB, lanes]
+            for k, value in enumerate(sums):
+                small[t, VOCAB + k:VOCAB + k + 1] = jnp.sum(value, axis=0, keepdims=True)
+            small[t, VOCAB + 13:] = jnp.zeros((SMALL_BLOCK - VOCAB - 13, LANES), F32)
         ship('wait', 4, 8)
         ship('wait', 0, 4)
 
@@ -792,11 +802,7 @@
         jax.ShapeDtypeStruct((SEQS, 128, 640), BF16),
         jax.ShapeDtypeStruct((SEQS, 128, 640), BF16),
         jax.ShapeDtypeStruct((64, 2 * PER, GROUP * NB, LANES), F32),
-        jax.ShapeDtypeStruct((64, 640), F32),
-        jax.ShapeDtypeStruct((6, 8, 640), F32),
-        jax.ShapeDtypeStruct((TILES, LANES, LANES), F32),
-        jax.ShapeDtypeStruct((2, TILES, 8, LANES), F32),
-        jax.ShapeDtypeStruct((4, 8, 640), F32),
+        jax.ShapeDtypeStruct((TILES, SMALL_BLOCK, LANES), F32),
     )
     out_specs = (pair, pair, ANY) + tuple(whole(o.shape) for o in out_shape[3:])
     in_specs = [
@@ -813,6 +819,7 @@
         vm((STEP_SEQS, 20, SEQ, SEQ), BF16), vm(halves, F32), vm((TILES, LANES, TOK), BF16),
         vm((TOK, 640), F32), vm((TOK, 640), BF16), vm((640, TOK), BF16), vm((TOK, 640), F32), vm((TOK, 640), F32),
         vm((TILES, LANES, TOK), F32), vm((15, TOK, LANES), BF16), vm((TOK, LANES), F32), vm((TOK, LANES), F32), vm((1920, LANES), F32),
+        vm((64, 640), F32), vm((6, 8, 640), F32), vm((TILES, LANES, LANES), F32), vm((2, TILES, 8, LANES), F32), vm((4, 8, 640), F32),
         dma((2,)), dma((2,)), dma((2,)),
     ]
     return pl.pallas_call(
@@ -881,21 +888,16 @@
         len_own = lax.dynamic_slice_in_dim(lengths, start, half, 0)
         positions = jnp.concatenate([cp * seq_loc + jnp.arange(seq_loc), (1 - cp) * seq_loc + jnp.arange(seq_loc)])
         tok, keep, mask, emb, cos, sin, cosn, sinn = prepare(tok_full, len_own, positions, embed_table, vecs_all)
-        y_own, y_oth, g_all, dtab, dsum, dbq, dbkv, dbup = layer_call(
+        y_own, y_oth, g_all, small = layer_call(
             tok, keep, mask, emb, vecs_all, up_b.reshape(4, 1, 640), cos, sin, cosn, sinn, w_all.reshape(chips, 2 * PER, GROUP * NB, 128), grad_out, g_oth)
-        rowsum = jnp.sum(dsum, axis=1)
-        d_bq = jnp.sum(dbq, axis=2).reshape(1, width)
-        d_bkv = jnp.sum(dbkv, axis=2).reshape(2, width)
-        small = jnp.concatenate([dtab[:vocab].reshape(-1), rowsum[:2].reshape(-1), d_bq.reshape(-1), d_bkv.reshape(-1), rowsum[2:].reshape(-1), jnp.sum(dbup, axis=1).reshape(-1)])
-        small = jnp.pad(small, (0, 2 * SMALL_ROWS * 128 - small.shape[0])).reshape(2, SMALL_ROWS, 128)
+        small = small.reshape(2, SMALL_ROWS, 128)
         g_red, s_red, out_full = reduce_all(g_all.reshape(SIDE, SIDE, SIDE, 2 * PER, GROUP * NB, 128), small, y_own, y_oth)
         g_red = g_red.reshape(60, NB, 128)
-        s_flat = s_red.reshape(-1)
-        n_tab = vocab * width
-        d_embed = s_flat[:n_tab].reshape(vocab, width)
-        d_v = lax.dynamic_slice(s_flat[n_tab:n_tab + 9 * width].reshape(9, width), (0, chip * NB), (9, NB))
-        d_b = s_flat[n_tab + 9 * width:n_tab + 9 * width + 2560].reshape(4, chips, NB)
-        d_b = lax.dynamic_slice(d_b, (0, chip, 0), (4, 1, NB)).reshape(-1)
+        s_rows = s_red.reshape(TILES, SMALL_BLOCK, 128)[:, :VOCAB + 13].transpose(1, 0, 2).reshape(VOCAB + 13, width)
+        d_embed = s_rows[:vocab]
+        s_mine = lax.dynamic_slice(s_rows, (vocab, chip * NB), (13, NB))
+        d_v = s_mine[:9]
+        d_b = s_mine[9:].reshape(-1)
         d_qkv = g_red[:15].transpose(1, 0, 2).reshape(w_qkv.shape)
         d_wout = g_red[15:20].transpose(1, 0, 2).reshape(w_out.shape)
         d_wup = g_red[20:40].transpose(0, 2, 1).reshape(4, chips, NB, rows).transpose(3, 1, 0, 2).reshape(w_up.shape)

time: 312 us -> 302 us (0.968)
  local copies, waits for them, and re-layouts: 30.9 us -> 25 us
  other arithmetic: 4.77 us -> 0.97 us
    slice x8 -> x3, local copies, waits for them, and re-layouts: 5.43 us -> 0.76 us  [the longest x1 0.68 us: local_step(): d_v = s_mine[:9]]
    reduce_sum x4 -> x0, other arithmetic: 3.8 us -> none  [the longest x1 1.15 us: local_step(): d_bq = jnp.sum(dbq, axis=2).reshape(1, width)]
where the time goes in v6:
time: 302 us; the launch traced here: 301 us
  Pallas kernels  274 us (91%)
  local copies, waits for them, and re-layouts  25 us (8%)
    pallas_call x1, Pallas kernels, layer_call(): pl.pallas_call(layer_kernel, grid=(STEPS,), out_shape=out_shape, in_specs...  168 us
    pallas_call x1, Pallas kernels, reduce_all(): pl.pallas_call(reduce_kernel, out_shape=(jax.ShapeDtypeStruct((units, row...  58.1 us
    pallas_call x1, Pallas kernels, gather_all(): pl.pallas_call(gather_kernel, out_shape=(jax.ShapeDtypeStruct((SIDE, SIDE...  48.1 us

profile of v6, /device:TPU:1, one launch (start us, length us, event | category | flops | bytes accessed | tf_op | source)
XLA Modules:
  0.0 301.4 jit_solution(2460173720785001006)
XLA Ops:
  0.7 0.0 copy-start
  0.7 0.8 constant_dynamic-slice_fusion.1
  1.5 3.1 %reshape.215 = bf16[10,64,4,10]{3,2,1,0:T(4,128)(2,1)} reshape(bf16[10,2560]{1,0:T(8,128)(2,1)} %param.20) | data formatting | bytes 102400 | tf_op jit(solution)/shard_map/reshape | solution.py:878
  4.7 1.2 copy.43
  5.9 0.0 copy-start.11
  5.9 1.2 reshape.216
  7.1 0.1 reshape.217
  7.3 1.1 reshape.213
  8.4 0.1 pad_maximum_fusion
  8.5 0.1 copy.45
  8.6 0.0 copy-start.7
  8.6 0.1 reshape.219.w_loc
  8.7 0.1 reshape.220
  8.8 0.1 fusion.s_loc
  8.9 48.1 %gather_weights.1 = (bf16[4,4,4,12,50,128]{5,4,3,2,1,0:T(8,128)(2,1)}, f32[4,4,4,8,128]{4,3,2,1,0:T(8,128)S(1)}, bf16[8,128,640]{2,1,0:T(8,128)(2,1)S(1)}, s32[8,128]{1,0:T(8,128)S(1)}) custom-call(bf16[12,50,128]{2,1,0:T(8,128)(2,1)S(1)} %reshape.219.w_loc, f32[8,128]{1,0:T(8,128)S(1)} %fusion.s_loc, bf16[16,128,640]{2,1,0:T(8,128)(2,1)S(1)} %copy-done, ...), custom_call_target="tpu_custom_call" | custom-call | tf_op jit(solution)/shard_map/gather_weights/pallas_call | solution.py:189
  56.9 0.0 copy-start.1
  56.9 1.0 copy-done.1
  58.0 0.1 convert_reduce_fusion
  58.1 0.1 subtract_divide_fusion
  58.2 0.1 broadcast_in_dim.26
  58.3 0.1 broadcast_in_dim.27
  58.4 0.1 lt.43
  58.5 0.1 lt.44
  58.6 0.6 compare_select_fusion
  59.3 0.1 copy.58
  59.5 0.2 copy.47
  59.6 0.8 reshape.225.vec_ref
  60.5 0.1 slice.58
  60.5 0.1 copy.59
  60.6 0.1 copy.49
  60.7 0.8 reshape_reshape.4.bup_ref
  61.5 0.6 pad.9.emb_ref
  62.1 168.2 %layer.1 = (bf16[8,128,640]{2,1,0:T(8,128)(2,1)}, bf16[8,128,640]{2,1,0:T(8,128)(2,1)}, f32[64,12,50,128]{3,2,1,0:T(8,128)}, f32[5,48,128]{2,1,0:T(8,128)}) custom-call(s32[4,1,512]{2,1,0:T(1,128)} %copy-done.5, f32[4,1,512]{2,1,0:T(1,128)} %get-tuple-element.35.keep_in, f32[4,1,512]{2,1,0:T(1,128)} %get-tuple-element.34.mask_in, ...), custom_call_target="tpu_custom_call" | custom-call | tf_op jit(solution)/shard_map/layer/pallas_call | solution.py:825
  230.3 58.1 %reduce_grads.1 = (f32[12,50,128]{2,1,0:T(8,128)}, f32[2,120,128]{2,1,0:T(8,128)}, bf16[16,128,640]{2,1,0:T(8,128)(2,1)}) custom-call(f32[4,4,4,12,50,128]{5,4,3,2,1,0:T(8,128)} %bitcast.59, f32[2,120,128]{2,1,0:T(8,128)} %bitcast.82, bf16[8,128,640]{2,1,0:T(8,128)(2,1)} %get-tuple-element.25.y_own, bf16[8,128,640]{2,1,0:T(8,128)(2,1)} %get-tuple-element.26.y_oth), custom_call_target="tpu_custom_call" | custom-call | tf_op jit(solution)/shard_map/reduce_grads/pallas_call | solution.py:412
  288.5 1.0 fusion.1
  289.5 1.4 reshape.234
  290.9 0.9 copy.55
  291.8 1.8 reshape.235
  293.6 1.0 slice.49
  294.7 0.9 reshape.232
  295.6 0.7 copy.72
  296.4 0.7 copy.63
  297.1 0.7 constant_dynamic-slice_fusion
  297.8 0.1 dynamic-slice.1
  297.8 0.6 reshape.236
  298.4 0.8 slice.51
  299.2 0.6 copy.65
  299.9 1.5 copy.74
  (47 shorter events, 0.6 us)
Async XLA Ops:
  0.6 8.2 %copy-start.2 = (s32[16,128]{1,0:T(8,128)S(1)}, s32[16,128]{1,0:T(8,128)}, u32[]{:S(2)}) copy-start(s32[16,128]{1,0:T(8,128)} %t_own.1) | copy-start | bytes 24580
  0.6 6.5 %copy-start.6 = (bf16[40,640]{1,0:T(8,128)(2,1)S(1)}, bf16[40,640]{1,0:T(8,128)(2,1)}, u32[]{:S(2)}) copy-start(bf16[40,640]{1,0:T(8,128)(2,1)} %param.22) | copy-start | bytes 153604
  0.7 7.7 %copy-start.8 = (bf16[10,640]{1,0:T(8,128)(2,1)S(1)}, bf16[10,640]{1,0:T(8,128)(2,1)}, u32[]{:S(2)}) copy-start(bf16[10,640]{1,0:T(8,128)(2,1)} %param.19) | copy-start | bytes 38404
  0.7 8.0 %copy-start.9 = (f32[9,10]{1,0:T(8,128)S(1)}, f32[9,10]{1,0:T(8,128)}, u32[]{:S(2)}) copy-start(f32[9,10]{1,0:T(8,128)} %param.17) | copy-start | bytes 1084
  0.7 8.1 %copy-start.10 = (f32[40]{0:T(128)S(1)}, f32[40]{0:T(128)}, u32[]{:S(2)}) copy-start(f32[40]{0:T(128)} %param.21) | copy-start | bytes 484
  0.7 8.2 %copy-start = (bf16[16,128,640]{2,1,0:T(8,128)(2,1)S(1)}, bf16[16,128,640]{2,1,0:T(8,128)(2,1)}, u32[]{:S(2)}) copy-start(bf16[16,128,640]{2,1,0:T(8,128)(2,1)} %g_own.3) | copy-start | bytes 7864324
  5.9 52.2 %copy-start.11 = (s32[16]{0:T(128)S(1)}, s32[16]{0:T(128)}, u32[]{:S(2)}) copy-start(s32[16]{0:T(128)} %param.15) | copy-start | bytes 196
  8.6 52.9 %copy-start.7 = (bf16[33,640]{1,0:T(8,128)(2,1)S(1)}, bf16[33,640]{1,0:T(8,128)(2,1)}, u32[]{:S(2)}) copy-start(bf16[33,640]{1,0:T(8,128)(2,1)} %param.16) | copy-start | bytes 126724
  56.9 1.1 copy-start.1
  58.6 0.7 copy-start.5
  290.9 5.4 %copy-start.4 = (f32[2,120,128]{2,1,0:T(8,128)S(1)}, f32[2,120,128]{2,1,0:T(8,128)}, u32[]{:S(2)}) copy-start(f32[2,120,128]{2,1,0:T(8,128)} %get-tuple-element.28) | copy-start | bytes 368644
  293.6 6.3 %copy-start.3 = (bf16[16,128,640]{2,1,0:T(8,128)(2,1)S(1)}, bf16[16,128,640]{2,1,0:T(8,128)(2,1)}, u32[]{:S(2)}) copy-start(bf16[16,128,640]{2,1,0:T(8,128)(2,1)} %get-tuple-element.48) | copy-start | bytes 7864324
